TPU v7x, 8 devices: a whole 2x2x1 slice. The times are simulated.
8 devices in a mesh: dp: 2 (over z, y), tp: 4 (over x, core).
Axes of the slice: x: 2, y: 2, z: 1, core: 2. Of those that a mesh axis runs over, the one named last changes fastest.
Arguments:
- resid_in: bfloat16 [256, 1, 3072], P(('dp', 'tp')), parts along dimension 0
- grad_out: bfloat16 [256, 1, 3072], P(('dp', 'tp')), parts along dimension 0
- positions: int32 [256], P('dp'), parts along dimension 0
- ln1_gain: float32 [3072], replicated
- ln1_bias: float32 [3072], replicated
- ln2_gain: float32 [3072], replicated
- ln2_bias: float32 [3072], replicated
- w_query: bfloat16 [3072, 3072], P(None, 'tp')
- w_key: bfloat16 [3072, 1024], P(None, 'tp')
- w_value: bfloat16 [3072, 1024], P(None, 'tp')
- w_out: bfloat16 [3072, 3072], P('tp')
- w_up: bfloat16 [3072, 8192], P(None, 'tp')
- w_down: bfloat16 [8192, 3072], P('tp')
Outputs:
- output 1: bfloat16 [256, 1, 3072], P(('dp', 'tp')), parts along dimension 0
- output 2: bfloat16 [256, 1, 3072], P(('dp', 'tp')), parts along dimension 0
- output 3: float32 [6144], P('dp'), parts along dimension 0
- output 4: float32 [6144], P('dp'), parts along dimension 0
- output 5: float32 [6144], P('dp'), parts along dimension 0
- output 6: float32 [6144], P('dp'), parts along dimension 0
- output 7: float32 [6144, 3072], P('dp', 'tp'), parts along dimension 0
- output 8: float32 [6144, 1024], P('dp', 'tp'), parts along dimension 0
- output 9: float32 [6144, 1024], P('dp', 'tp'), parts along dimension 0
- output 10: float32 [6144, 3072], P(('dp', 'tp')), parts along dimension 0
- output 11: float32 [6144, 8192], P('dp', 'tp'), parts along dimension 0
- output 12: float32 [16384, 3072], P(('dp', 'tp')), parts along dimension 0
There are 2 independent parts. A program takes and returns all parts, laid end to end along the dimension named above; an argument that names none is the same for every part.
All inputs are finite; a program needn't handle non-finite values.
Results may differ from a plain program's by a relative error of at most 0.018293.
Values are sent between devices in bfloat16 or wider.
A program may use at most 1 GiB of HBM per device.

v0:
```python
import functools
import jax
import jax.numpy as jnp
from jax import lax
from jax.sharding import PartitionSpec as P

KV_HEADS = 8
LN_EPS = 1e-5
ROPE_BASE = 10000.0


def layer_norm_1p(resid_f, gain, bias):
    mean_val = jnp.mean(resid_f, axis=-1, keepdims=True)
    centred = resid_f - mean_val
    var_val = jnp.mean(centred * centred, axis=-1, keepdims=True)
    return centred * lax.rsqrt(var_val + LN_EPS) * (1.0 + gain) + bias


def rope_tables(positions, head_dim):
    rot_half = head_dim // 4
    inv_freq = ROPE_BASE ** (-jnp.arange(rot_half, dtype=jnp.float32) / rot_half)
    angles = positions.astype(jnp.float32)[..., None] * inv_freq
    return jnp.cos(angles), jnp.sin(angles)


def apply_rope(values, cos_tab, sin_tab):
    rot_half = cos_tab.shape[-1]
    table_shape = cos_tab.shape[:-1] + (1,) * (values.ndim - cos_tab.ndim) + (rot_half,)
    cos_full = cos_tab.reshape(table_shape)
    sin_full = sin_tab.reshape(table_shape)
    first_half = values[..., :rot_half]
    second_half = values[..., rot_half:2 * rot_half]
    return jnp.concatenate([first_half * cos_full - second_half * sin_full, second_half * cos_full + first_half * sin_full, values[..., 2 * rot_half:]], axis=-1)


def causal_softmax(scores, causal):
    scores = jnp.where(causal, scores, -1e30)
    row_max = jnp.max(scores, axis=-1, keepdims=True)
    exp_scores = jnp.exp(scores - row_max)
    return exp_scores / jnp.sum(exp_scores, axis=-1, keepdims=True)


def layer_step(resid_loc, grad_loc, positions, ln1_gain, ln1_bias, ln2_gain, ln2_bias, w_query, w_key, w_value, w_out, w_up, w_down, head_dim):
    seq_len = positions.shape[0]
    n_batch = resid_loc.shape[1]
    kv_loc = w_key.shape[1] // head_dim
    q_loc = w_query.shape[1] // head_dim
    q_per_kv = q_loc // kv_loc
    attn_scale = head_dim ** -0.5
    causal = jnp.arange(seq_len)[:, None] >= jnp.arange(seq_len)[None, :]
    cos_tab, sin_tab = rope_tables(positions, head_dim)
    resid_f = resid_loc.astype(jnp.float32)
    h_one = lax.all_gather(layer_norm_1p(resid_f, ln1_gain, ln1_bias).astype(jnp.bfloat16), 'tp', axis=0, tiled=True)
    q_proj = jnp.dot(h_one, w_query, preferred_element_type=jnp.float32).astype(jnp.bfloat16)
    k_proj = jnp.dot(h_one, w_key, preferred_element_type=jnp.float32).astype(jnp.bfloat16)
    v_proj = jnp.dot(h_one, w_value, preferred_element_type=jnp.float32).astype(jnp.bfloat16).reshape(seq_len, n_batch, kv_loc, head_dim)
    q_rot = apply_rope(q_proj.astype(jnp.float32).reshape(seq_len, n_batch, kv_loc, q_per_kv, head_dim), cos_tab, sin_tab).astype(jnp.bfloat16)
    k_rot = apply_rope(k_proj.astype(jnp.float32).reshape(seq_len, n_batch, kv_loc, head_dim), cos_tab, sin_tab).astype(jnp.bfloat16)
    scores = jnp.einsum('sbkgd,tbkd->bkgst', q_rot, k_rot, preferred_element_type=jnp.float32) * attn_scale
    attn_prob = causal_softmax(scores, causal)
    prob_low = attn_prob.astype(jnp.bfloat16)
    context = jnp.einsum('bkgst,tbkd->sbkgd', prob_low, v_proj, preferred_element_type=jnp.float32).astype(jnp.bfloat16).reshape(seq_len, n_batch, q_loc * head_dim)
    attn_out = lax.psum_scatter(jnp.dot(context, w_out, preferred_element_type=jnp.float32), 'tp', scatter_dimension=0, tiled=True).astype(jnp.bfloat16)
    resid_mid = (resid_f + attn_out.astype(jnp.float32)).astype(jnp.bfloat16)
    mid_f = resid_mid.astype(jnp.float32)
    h_two = lax.all_gather(layer_norm_1p(mid_f, ln2_gain, ln2_bias).astype(jnp.bfloat16), 'tp', axis=0, tiled=True)
    up_proj = jnp.dot(h_two, w_up, preferred_element_type=jnp.float32).astype(jnp.bfloat16)
    relu_up = jnp.maximum(up_proj.astype(jnp.float32), 0.0)
    mlp_act = (relu_up * relu_up).astype(jnp.bfloat16)
    mlp_out = lax.psum_scatter(jnp.dot(mlp_act, w_down, preferred_element_type=jnp.float32), 'tp', scatter_dimension=0, tiled=True).astype(jnp.bfloat16)
    resid_out = (mid_f + mlp_out.astype(jnp.float32)).astype(jnp.bfloat16)

    grad_full = lax.all_gather(grad_loc, 'tp', axis=0, tiled=True)
    grad_w_down = jnp.einsum('sbf,sbm->fm', mlp_act, grad_full, preferred_element_type=jnp.float32)
    grad_up = (jnp.einsum('sbm,fm->sbf', grad_full, w_down, preferred_element_type=jnp.float32) * (2.0 * relu_up)).astype(jnp.bfloat16)
    grad_w_up = jnp.einsum('sbm,sbf->mf', h_two, grad_up, preferred_element_type=jnp.float32)
    grad_h_two = lax.psum_scatter(jnp.einsum('sbf,mf->sbm', grad_up, w_up, preferred_element_type=jnp.float32), 'tp', scatter_dimension=0, tiled=True).astype(jnp.bfloat16)
    ln2_back = jax.vjp(layer_norm_1p, mid_f, ln2_gain, ln2_bias)[1]
    grad_mid_ln, grad_ln2_gain, grad_ln2_bias = ln2_back(grad_h_two.astype(jnp.float32))
    grad_mid = (grad_loc.astype(jnp.float32) + grad_mid_ln).astype(jnp.bfloat16)
    grad_mid_full = lax.all_gather(grad_mid, 'tp', axis=0, tiled=True)
    grad_w_out = jnp.einsum('sbn,sbm->nm', context, grad_mid_full, preferred_element_type=jnp.float32)
    grad_ctx = jnp.einsum('sbm,nm->sbn', grad_mid_full, w_out, preferred_element_type=jnp.float32).astype(jnp.bfloat16).reshape(seq_len, n_batch, kv_loc, q_per_kv, head_dim)
    grad_v = jnp.einsum('bkgst,sbkgd->tbkd', prob_low, grad_ctx, preferred_element_type=jnp.float32).astype(jnp.bfloat16).reshape(seq_len, n_batch, kv_loc * head_dim)
    grad_prob = jnp.einsum('sbkgd,tbkd->bkgst', grad_ctx, v_proj, preferred_element_type=jnp.float32)
    grad_score = (attn_prob * (grad_prob - jnp.sum(grad_prob * attn_prob, axis=-1, keepdims=True)) * attn_scale).astype(jnp.bfloat16)
    grad_q = apply_rope(jnp.einsum('bkgst,tbkd->sbkgd', grad_score, k_rot, preferred_element_type=jnp.float32), cos_tab, -sin_tab).astype(jnp.bfloat16).reshape(seq_len, n_batch, q_loc * head_dim)
    grad_k = apply_rope(jnp.einsum('bkgst,sbkgd->tbkd', grad_score, q_rot, preferred_element_type=jnp.float32), cos_tab, -sin_tab).astype(jnp.bfloat16).reshape(seq_len, n_batch, kv_loc * head_dim)
    grad_w_query = jnp.einsum('sbm,sbn->mn', h_one, grad_q, preferred_element_type=jnp.float32)
    grad_w_key = jnp.einsum('sbm,sbn->mn', h_one, grad_k, preferred_element_type=jnp.float32)
    grad_w_value = jnp.einsum('sbm,sbn->mn', h_one, grad_v, preferred_element_type=jnp.float32)
    grad_h_part = jnp.einsum('sbn,mn->sbm', grad_q, w_query, preferred_element_type=jnp.float32) + jnp.einsum('sbn,mn->sbm', grad_k, w_key, preferred_element_type=jnp.float32) + jnp.einsum('sbn,mn->sbm', grad_v, w_value, preferred_element_type=jnp.float32)
    grad_h_one = lax.psum_scatter(grad_h_part, 'tp', scatter_dimension=0, tiled=True).astype(jnp.bfloat16)
    ln1_back = jax.vjp(layer_norm_1p, resid_f, ln1_gain, ln1_bias)[1]
    grad_in_ln, grad_ln1_gain, grad_ln1_bias = ln1_back(grad_h_one.astype(jnp.float32))
    grad_in = (grad_mid.astype(jnp.float32) + grad_in_ln).astype(jnp.bfloat16)
    ln_grads = lax.psum(jnp.stack([grad_ln1_gain, grad_ln1_bias, grad_ln2_gain, grad_ln2_bias]), 'tp')
    return (resid_out, grad_in, ln_grads[0], ln_grads[1], ln_grads[2], ln_grads[3], grad_w_query, grad_w_key, grad_w_value, grad_w_out, grad_w_up, grad_w_down)


def solution(mesh):
    seq_spec = P(('dp', 'tp'))
    col_spec = P(None, 'tp')
    row_spec = P('tp', None)
    grad_col_spec = P('dp', 'tp')
    grad_row_spec = P(('dp', 'tp'), None)
    in_specs = (seq_spec, seq_spec, P('dp'), P(), P(), P(), P(), col_spec, col_spec, col_spec, row_spec, col_spec, row_spec)
    out_specs = (seq_spec, seq_spec, P('dp'), P('dp'), P('dp'), P('dp'), grad_col_spec, grad_col_spec, grad_col_spec, grad_row_spec, grad_col_spec, grad_row_spec)

    def run_layer(resid_in, grad_out, positions, ln1_gain, ln1_bias, ln2_gain, ln2_bias, w_query, w_key, w_value, w_out, w_up, w_down):
        step_fn = functools.partial(layer_step, head_dim=w_key.shape[1] // KV_HEADS)
        sharded = jax.shard_map(step_fn, mesh=mesh, in_specs=in_specs, out_specs=out_specs, check_vma=False)
        return sharded(resid_in, grad_out, positions, ln1_gain, ln1_bias, ln2_gain, ln2_bias, w_query, w_key, w_value, w_out, w_up, w_down)

    return run_layer
```

profile of v0, /device:TPU:0, one launch (start us, length us, event | category | flops | bytes accessed | tf_op | source)
XLA Modules:
  0.0 223.5 jit_solution(9161629502987482141)
XLA Ops:
  11.4 13.0 %all_gather.12 = bf16[128,1,3072]{2,0,1:T(8,128)(2,1)S(1)} all-gather(bf16[32,1,3072]{2,0,1:T(8,128)(2,1)S(1)} %fusion.40), channel_id=1, replica_groups=mesh['dp'=2,'tp'=4] {'tp'}, dimensions={0}, use_global_device_ids=true | all-gather | bytes 983040 | tf_op jit(solution)/shard_map/all_gather | solution.py:53
  24.4 3.4 %convolution_convert_fusion.3 = bf16[128,768]{1,0:T(8,128)(2,1)S(1)} fusion(bf16[3072,768]{1,0:T(8,128)(2,1)} %param.20, bf16[128,1,3072]{2,0,1:T(8,128)(2,1)S(1)} %all_gather.12), kind=kOutput, calls=%fused_computation.17 | convolution fusion | flops 604078080 | bytes 5701632 | tf_op jit(solution)/shard_map/dot_general | solution.py:54
  33.6 4.4 %convolution_bitcast_fusion.2 = f32[128,1,3072]{2,0,1:T(8,128)} fusion(bf16[128,768]{0,1:T(8,128)(2,1)S(1)} %bitcast.144, bf16[768,3072]{1,0:T(8,128)(2,1)} %param.23), kind=kOutput, calls=%fused_computation.5 | convolution fusion | flops 603979776 | bytes 6488064 | tf_op jit(solution)/shard_map/dot_general | solution.py:63
  38.1 11.7 %all_gather.14 = bf16[128,1,3072]{2,0,1:T(8,128)(2,1)} all-gather(bf16[32,1,3072]{2,0,1:T(8,128)(2,1)S(1)} %copy-done.23), channel_id=1, replica_groups=mesh['dp'=2,'tp'=4] {'tp'}, dimensions={0}, use_global_device_ids=true | all-gather | bytes 983040 | tf_op jit(solution)/shard_map/all_gather | solution.py:73
  49.7 11.8 %reduce-scatter.5.cloned.1.call-done = f32[32,1,3072]{2,0,1:T(8,128)} async-done(((f32[128,1,3072]{2,0,1:T(8,128)}), f32[32,1,3072]{2,0,1:T(8,128)}) %reduce-scatter.5.cloned.1.call-update) | async-done | bytes 393232 | tf_op jit(solution)/shard_map/reduce_scatter | solution.py:63
  63.1 11.6 %all_gather.13 = bf16[128,1,3072]{2,0,1:T(8,128)(2,1)S(1)} all-gather(bf16[32,1,3072]{2,0,1:T(8,128)(2,1)S(1)} %fusion.38), channel_id=1, replica_groups=mesh['dp'=2,'tp'=4] {'tp'}, dimensions={0}, use_global_device_ids=true | all-gather | bytes 983040 | tf_op jit(solution)/shard_map/all_gather | solution.py:66
  75.6 7.5 %fusion.3 = f32[128,2048]{1,0:T(8,128)} fusion(bf16[3072,2048]{1,0:T(8,128)(2,1)} %param.24, bf16[128,1,3072]{2,0,1:T(8,128)(2,1)S(1)} %all_gather.13), kind=kOutput, calls=%fused_computation.10 | convolution fusion | flops 1611399168 | bytes 14417920 | tf_op jit(solution)/shard_map/dot_general | solution.py:67
  83.1 10.3 %fusion.1 = bf16[128,2048]{1,0:T(8,128)(2,1)} fusion(bf16[2048,3072]{1,0:T(8,128)(2,1)} %param.25, f32[128,2048]{1,0:T(8,128)} %fusion.3, bf16[128,1,3072]{2,0,1:T(8,128)(2,1)} %all_gather.14), kind=kOutput, calls=%fused_computation.7 | convolution fusion | flops 1611399168 | bytes 14942208 | tf_op jit(solution)/shard_map/sbm,fm->sbf/dot_general | solution.py:75
  93.4 6.4 %convolution_bitcast_fusion = f32[128,1,3072]{2,0,1:T(8,128)} fusion(bf16[128,2048]{1,0:T(8,128)(2,1)} %fusion.1, bf16[3072,2048]{1,0:T(8,128)(2,1)S(1)} %bitcast.141), kind=kOutput, calls=%fused_computation.3 | convolution fusion | flops 1610612736 | bytes 14680064 | tf_op jit(solution)/shard_map/sbf,mf->sbm/dot_general | solution.py:77
  99.9 7.9 %convolution_bitcast_fusion.1 = f32[128,1,3072]{2,0,1:T(8,128)} fusion(bf16[2048,3072]{1,0:T(8,128)(2,1)} %param.25, f32[128,2048]{1,0:T(8,128)} %fusion.3), kind=kOutput, calls=%fused_computation.4 | convolution fusion | flops 1611137024 | bytes 15204352 | tf_op jit(solution)/shard_map/dot_general | solution.py:70
  107.9 11.9 %fusion.10 = f32[2048,3072]{1,0:T(8,128)} fusion(bf16[128,1,3072]{2,0,1:T(8,128)(2,1)} %all_gather.14, f32[128,2048]{1,0:T(8,128)S(1)} %copy-done.3), kind=kOutput, calls=%fused_computation.28 | convolution fusion | flops 1611137024 | bytes 27000832 | tf_op jit(solution)/shard_map/sbf,sbm->fm/dot_general | solution.py:74
  119.8 2.3 %reduce-scatter.9.cloned.1.call-done = f32[32,1,3072]{2,0,1:T(8,128)} async-done(((f32[128,1,3072]{2,0,1:T(8,128)}), f32[32,1,3072]{2,0,1:T(8,128)}) %reduce-scatter.9.cloned.1.call-update) | async-done | bytes 393232 | tf_op jit(solution)/shard_map/reduce_scatter | solution.py:77
  123.7 23.9 %reduce-scatter.7.cloned.1.call-done = f32[32,1,3072]{2,0,1:T(8,128)} async-done(((f32[128,1,3072]{2,0,1:T(8,128)}), f32[32,1,3072]{2,0,1:T(8,128)}) %reduce-scatter.7.cloned.1.call-update) | async-done | bytes 393232 | tf_op jit(solution)/shard_map/reduce_scatter | solution.py:70
  147.6 1.9 add_convert_fusion.1
  150.1 11.6 %all_gather.15 = bf16[128,1,3072]{2,0,1:T(8,128)(2,1)S(1)} all-gather(bf16[32,1,3072]{2,0,1:T(8,128)(2,1)S(1)} %get-tuple-element.32), channel_id=1, replica_groups=mesh['dp'=2,'tp'=4] {'tp'}, dimensions={0}, use_global_device_ids=true | all-gather | bytes 983040 | tf_op jit(solution)/shard_map/all_gather | solution.py:81
  162.7 4.1 %convolution_convert_fusion.1 = bf16[128,768]{1,0:T(8,128)(2,1)S(1)} fusion(bf16[768,3072]{1,0:T(8,128)(2,1)} %param.23, bf16[128,1,3072]{2,0,1:T(8,128)(2,1)S(1)} %all_gather.15), kind=kOutput, calls=%fused_computation.15 | convolution fusion | flops 604078080 | bytes 5701632 | tf_op jit(solution)/shard_map/sbm,nm->sbn/dot_general | solution.py:83
  170.9 4.1 %fusion.72 = f32[128,3072]{1,0:T(8,128)S(1)} fusion(bf16[128,768]{0,1:T(8,128)(2,1)S(1)} %bitcast.142, bf16[3072,768]{1,0:T(8,128)(2,1)} %param.20), kind=kOutput, calls=%fused_computation.136 | convolution fusion | flops 603979776 | bytes 6488064 | tf_op jit(solution)/shard_map/sbn,mn->sbm/dot_general | solution.py:92
  175.8 1.8 fusion
  177.7 10.8 %fusion.13 = f32[3072,2048]{1,0:T(8,128)} fusion(bf16[128,2048]{1,0:T(8,128)(2,1)S(1)} %copy-done.10, bf16[128,1,3072]{2,0,1:T(8,128)(2,1)S(1)} %copy-done.5), kind=kOutput, calls=%fused_computation.31 | convolution fusion | flops 1610612736 | bytes 26476544 | tf_op jit(solution)/shard_map/sbm,sbf->mf/dot_general | solution.py:76
  188.4 2.3 %fusion.16 = f32[3072,256]{1,0:T(8,128)} fusion(bf16[128,256]{0,1:T(8,128)(2,1)S(1)} %bitcast.150, bf16[128,1,3072]{2,0,1:T(8,128)(2,1)S(1)} %copy-done.2), kind=kOutput, calls=%fused_computation.34 | convolution fusion | flops 201326592 | bytes 3997696 | tf_op jit(solution)/shard_map/sbm,sbn->mn/dot_general | solution.py:91
  190.7 2.3 %fusion.18 = f32[3072,256]{1,0:T(8,128)} fusion(bf16[128,256]{0,1:T(8,128)(2,1)S(1)} %bitcast.148, bf16[128,1,3072]{2,0,1:T(8,128)(2,1)S(1)} %copy-done.2), kind=kOutput, calls=%fused_computation.36 | convolution fusion | flops 201326592 | bytes 3997696 | tf_op jit(solution)/shard_map/sbm,sbn->mn/dot_general | solution.py:90
  193.0 5.2 %fusion.20 = f32[3072,768]{1,0:T(8,128)} fusion(bf16[128,768]{0,1:T(8,128)(2,1)S(1)} %bitcast.143, bf16[128,1,3072]{2,0,1:T(8,128)(2,1)S(1)} %copy-done.2), kind=kOutput, calls=%fused_computation.38 | convolution fusion | flops 603979776 | bytes 10420224 | tf_op jit(solution)/shard_map/sbm,sbn->mn/dot_general | solution.py:89
  198.2 5.1 %fusion.7 = f32[768,3072]{1,0:T(8,128)} fusion(bf16[128,768]{0,1:T(8,128)(2,1)S(1)} %bitcast.145, bf16[128,1,3072]{2,0,1:T(8,128)(2,1)S(1)} %copy-done.8), kind=kOutput, calls=%fused_computation.25 | convolution fusion | flops 603979776 | bytes 10420224 | tf_op jit(solution)/shard_map/sbn,sbm->nm/dot_general | solution.py:82
  204.9 10.6 %psum.7 = f32[4,3072]{1,0:T(4,128)S(1)} all-reduce(f32[4,3072]{1,0:T(4,128)S(1)} %pad_maximum_fusion.1), channel_id=1, replica_groups=mesh['dp'=2,'tp'=4] {'tp'}, use_global_device_ids=true, to_apply=%region_19.20 | all-reduce | flops 12288 | bytes 98304 | tf_op jit(solution)/shard_map/psum | solution.py:97
  (155 shorter events, 23.2 us)
Async XLA Ops:
  7.2 21.2 %copy-start = (bf16[3072,256]{1,0:T(8,128)(2,1)S(1)}, bf16[3072,256]{1,0:T(8,128)(2,1)}, u32[]{:S(2)}) copy-start(bf16[3072,256]{1,0:T(8,128)(2,1)} %param.21) | copy-start | bytes 4718596
  7.2 21.2 %copy-start.40 = (s32[128]{0:T(128)S(1)}, s32[128]{0:T(128)}, u32[]{:S(2)}) copy-start(s32[128]{0:T(128)} %param.15) | copy-start | bytes 1540
  7.2 54.4 %reduce-scatter.5.cloned.1.call-start = ((), (), s32[]{:S(2)}) async-start(), calls=%async_computation.4 | async-start | bytes 1966080 | tf_op jit(solution)/shard_map/reduce_scatter | solution.py:63
  9.6 19.2 %copy-start.36 = (f32[32]{0:T(128)}, f32[32]{0:T(128)S(1)}, u32[]{:S(2)}) copy-start(f32[32]{0:T(128)S(1)} %fusion.41) | copy-start | bytes 388
  30.7 7.3 %copy-start.33 = (bf16[128,2,128]{2,1,0:T(2,128)(2,1)}, bf16[128,2,128]{2,1,0:T(2,128)(2,1)S(1)}, u32[]{:S(2)}) copy-start(bf16[128,2,128]{2,1,0:T(2,128)(2,1)S(1)} %reshape.608) | copy-start | bytes 196612
  33.5 16.2 %copy-start.21 = (bf16[2,128,3,128]{3,1,2,0:T(8,128)(2,1)}, bf16[2,128,3,128]{3,1,2,0:T(8,128)(2,1)S(1)}, u32[]{:S(2)}) copy-start(bf16[2,128,3,128]{3,1,2,0:T(8,128)(2,1)S(1)} %convolution_convert_fusion.2) | copy-start | bytes 589828
  33.5 16.2 %copy-start.35 = (f32[3072]{0:T(1024)S(1)}, f32[3072]{0:T(1024)}, u32[]{:S(2)}) copy-start(f32[3072]{0:T(1024)} %param.18) | copy-start | bytes 36868
  33.5 28.0 %copy-start.6 = (bf16[32,1,3072]{2,0,1:T(8,128)(2,1)S(1)}, bf16[32,1,3072]{2,0,1:T(8,128)(2,1)}, u32[]{:S(2)}) copy-start(bf16[32,1,3072]{2,0,1:T(8,128)(2,1)} %param.13) | copy-start | bytes 589828
  33.6 29.4 %copy-start.34 = (f32[3072]{0:T(1024)S(1)}, f32[3072]{0:T(1024)}, u32[]{:S(2)}) copy-start(f32[3072]{0:T(1024)} %param.19) | copy-start | bytes 36868
  38.0 84.1 %reduce-scatter.9.cloned.1.call-start = ((), (), s32[]{:S(2)}) async-start(), calls=%async_computation.6 | async-start | bytes 1966080 | tf_op jit(solution)/shard_map/reduce_scatter | solution.py:77
  63.0 11.8 %copy-start.38 = (f32[32]{0:T(128)}, f32[32]{0:T(128)S(1)}, u32[]{:S(2)}) copy-start(f32[32]{0:T(128)S(1)} %fusion.44) | copy-start | bytes 388
  75.6 17.8 %slice-start = ((s8[12582912]{0:T(1024)(128)(4,1)}), s8[4194304]{0:T(1024)(128)(4,1)S(1)}, s32[]{:S(2)}) async-start(s8[12582912]{0:T(1024)(128)(4,1)} %bitcast.140), calls=%async_computation.8 | async-start | bytes 8388608
  75.6 17.8 %slice-start.1 = ((s8[12582912]{0:T(1024)(128)(4,1)}), s8[4194304]{0:T(1024)(128)(4,1)S(1)}, s32[]{:S(2)}) async-start(s8[12582912]{0:T(1024)(128)(4,1)} %bitcast.140), calls=%async_computation.9 | async-start | bytes 8388608
  83.1 10.3 %slice-start.2 = ((s8[12582912]{0:T(1024)(128)(4,1)}), s8[4194304]{0:T(1024)(128)(4,1)S(1)}, s32[]{:S(2)}) async-start(s8[12582912]{0:T(1024)(128)(4,1)} %bitcast.140), calls=%async_computation.10 | async-start | bytes 8388608
  99.8 8.1 %copy-start.3 = (f32[128,2048]{1,0:T(8,128)S(1)}, f32[128,2048]{1,0:T(8,128)}, u32[]{:S(2)}) copy-start(f32[128,2048]{1,0:T(8,128)} %fusion.3) | copy-start | bytes 3145732
  99.8 47.8 %reduce-scatter.7.cloned.1.call-start = ((), (), s32[]{:S(2)}) async-start(), calls=%async_computation.5 | async-start | bytes 1966080 | tf_op jit(solution)/shard_map/reduce_scatter | solution.py:70
  107.8 15.6 %copy-start.39 = (f32[32]{0:T(128)S(1)}, f32[32]{0:T(128)}, u32[]{:S(2)}) copy-start(f32[32]{0:T(128)} %copy-done.38) | copy-start | bytes 388
  107.8 39.8 %copy-start.24 = (bf16[32,1,3072]{2,0,1:T(8,128)(2,1)S(1)}, bf16[32,1,3072]{2,0,1:T(8,128)(2,1)}, u32[]{:S(2)}) copy-start(bf16[32,1,3072]{2,0,1:T(8,128)(2,1)} %param.14) | copy-start | bytes 589828
  107.8 95.5 %reduce-scatter.11.cloned.1.call-start = ((), (), s32[]{:S(2)}) async-start(), calls=%async_computation.7 | async-start | bytes 1966080 | tf_op jit(solution)/shard_map/reduce_scatter | solution.py:93
  119.8 47.2 %copy-start.12 = (f32[1,2,3,128,128]{3,4,2,1,0:T(8,128)S(1)}, f32[1,2,3,128,128]{3,4,2,1,0:T(8,128)}, u32[]{:S(2)}) copy-start(f32[1,2,3,128,128]{3,4,2,1,0:T(8,128)} %copy-done.11) | copy-start | bytes 1179652
  162.7 6.8 %copy-start.29 = (bf16[128,2,32]{2,0,1:T(8,128)(2,1)S(1)}, bf16[128,2,32]{2,0,1:T(8,128)(2,1)}, u32[]{:S(2)}) copy-start(bf16[128,2,32]{2,0,1:T(8,128)(2,1)} %copy-done.28) | copy-start | bytes 49156
  162.7 6.8 %copy-start.31 = (bf16[128,2,32]{2,0,1:T(8,128)(2,1)S(1)}, bf16[128,2,32]{2,0,1:T(8,128)(2,1)}, u32[]{:S(2)}) copy-start(bf16[128,2,32]{2,0,1:T(8,128)(2,1)} %copy-done.30) | copy-start | bytes 49156
  177.7 10.8 %copy-start.2 = (bf16[128,1,3072]{2,0,1:T(8,128)(2,1)S(1)}, bf16[128,1,3072]{2,0,1:T(8,128)(2,1)}, u32[]{:S(2)}) copy-start(bf16[128,1,3072]{2,0,1:T(8,128)(2,1)} %copy-done.1) | copy-start | bytes 2359300
  198.2 18.0 %copy-start.20 = (bf16[32,1,3072]{2,0,1:T(8,128)(2,1)S(1)}, bf16[32,1,3072]{2,0,1:T(8,128)(2,1)}, u32[]{:S(2)}) copy-start(bf16[32,1,3072]{2,0,1:T(8,128)(2,1)} %copy-done.19) | copy-start | bytes 589828
  (24 other events, 83.4 us)
Sparse Core Ops, SparseCore 0:
  38.1 23.3 reduce-scatter.4
  99.9 22.1 reduce-scatter.8
  125.2 22.3 reduce-scatter.6
  177.8 22.0 reduce-scatter.10
where the time goes:
time: 224 us
  matrix products  93.5 us (42%)
  blocking collectives  58.4 us (26%)
  waiting for transfers between devices  38.1 us (17%)
  between operations  14.5 us (6%)
  other arithmetic  13.7 us (6%)
  local copies, waits for them, and re-layouts  5.13 us (2%)
    reduce_scatter x1, waiting for transfers between devices, layer_step(): lax.psum_scatter(jnp.dot(mlp_act, w_down, preferred_element_type=jnp.floa...  23.9 us
    all_gather x1, blocking collectives, layer_step(): lax.all_gather(layer_norm_1p(resid_f, ln1_gain, ln1_bias).astype(jnp.bflo...  13 us
    dot_general x1, matrix products, layer_step(): jnp.einsum('sbf,sbm->fm', mlp_act, grad_full, preferred_element_type=jnp....  11.9 us
    reduce_scatter x1, waiting for transfers between devices, layer_step(): lax.psum_scatter(jnp.dot(context, w_out, preferred_element_type=jnp.float...  11.8 us
    all_gather x1, blocking collectives, layer_step(): grad_full = lax.all_gather(grad_loc, 'tp', axis=0, tiled=True)  11.7 us
    all_gather x1, blocking collectives, layer_step(): grad_mid_full = lax.all_gather(grad_mid, 'tp', axis=0, tiled=True)  11.6 us
    all_gather x1, blocking collectives, layer_step(): lax.all_gather(layer_norm_1p(mid_f, ln2_gain, ln2_bias).astype(jnp.bfloat...  11.6 us
    dot_general x1, matrix products, layer_step(): jnp.einsum('sbm,sbf->mf', h_two, grad_up, preferred_element_type=jnp.floa...  10.8 us
  transfers between devices with their start and end apart: 4, of which 3 were waited for; matrix products, arithmetic and copies ran while one was open for 21% of the time, Pallas kernels for 0%

commit v1 on v0

v1 whole, which is shorter than its diff:
```python
import functools
import math
import numpy as np
import jax
import jax.numpy as jnp
from jax import lax
from jax.experimental import pallas as pl
from jax.experimental.pallas import tpu as pltpu
from jax.sharding import PartitionSpec as P

KV_HEADS = 8
LN_EPS = 1e-5
ROPE_BASE = 10000.0
F32 = jnp.float32
BF16 = jnp.bfloat16
ANY = pl.BlockSpec(memory_space=pl.ANY)
VMEM = pl.BlockSpec(memory_space=pltpu.VMEM)
VMEM_LIMIT = 67_043_328
CHUNKS = 4


def mm(a, b):
    return jnp.dot(a, b, preferred_element_type=F32)


def mm_bt(a, b):
    return lax.dot_general(a, b, (((1,), (1,)), ((), ())), preferred_element_type=F32)


def mm_at(a, b):
    return lax.dot_general(a, b, (((0,), (0,)), ((), ())), preferred_element_type=F32)


def centre(rows):
    centred = rows - jnp.mean(rows, axis=-1, keepdims=True)
    scale = lax.rsqrt(jnp.mean(centred * centred, axis=-1, keepdims=True) + LN_EPS)
    return centred * scale, scale


def norm_rows(rows, gain, bias):
    normed, _ = centre(rows)
    return normed * (1.0 + gain) + bias


def norm_rows_back(rows, grad, gain):
    normed, scale = centre(rows)
    weighted = grad * (1.0 + gain)
    inner = jnp.mean(weighted * normed, axis=-1, keepdims=True)
    grad_rows = scale * (weighted - jnp.mean(weighted, axis=-1, keepdims=True) - normed * inner)
    return grad_rows, jnp.sum(grad * normed, axis=0, keepdims=True), jnp.sum(grad, axis=0, keepdims=True)


class Sems:
    def __init__(self):
        self.next = 0

    def take(self, count):
        base = self.next
        self.next += count
        return base


def chain_kernel(dims, x_hbm, dy_hbm, pos_ref, freq_ref, g1_ref, b1_ref, g2_ref, b2_ref, wq_hbm, wk_hbm, wv_hbm, wo_hbm, w1_hbm, w2_hbm,
                 h1_out, h2_out, dy_out, dx1_out, act_out, du_out, ctx_out, dqkv_out, mid_out, dmid_out, ysend_out, ykeep_out, hsend_out, hkeep_out, lng_out,
                 wqkv, wo, w1, w2, h1, h2, dyf, dx1, x_own, mid, tmat, act, du, qs, kv, ctx, prob, cosb, sinb, gcs, dqkv, lng,
                 part_a, part_b, part_c, dr_a, dr_b, dr_c, dr_d, snd_a, snd_b, lnk_a, lnk_b, ysend, ykeep, hsend, hkeep,
                 local_sem, out_sem, send_sem, recv_sem):
    seq, d, hd, nq, nk, f, rows = dims
    grp = nq // nk
    half = rows // 2
    cw = d // CHUNKS
    me = lax.axis_index("tp")
    part, peer, diag = me ^ 1, me ^ 2, me ^ 3
    sems = Sems()

    def block(idx, sub=None):
        if sub is None:
            return pl.ds(pl.multiple_of(idx * rows, rows), rows)
        return pl.ds(pl.multiple_of(idx * rows + sub * half, half), half)

    def remote(src, dst, sem, dev):
        return pltpu.make_async_remote_copy(src, dst, send_sem.at[sem], recv_sem.at[sem], device_id={"tp": dev})

    def local(src, dst, idx):
        return pltpu.make_async_copy(src, dst, local_sem.at[idx])

    x_in = local(x_hbm, x_own, 0)
    dy_in = local(dy_hbm, dyf.at[block(me)], 1)
    nqd, nkd = nq * hd, nk * hd
    weight_in = [
        local(wq_hbm, wqkv.at[:, pl.ds(0, nqd)], 2),
        local(wk_hbm, wqkv.at[:, pl.ds(nqd, nkd)], 3),
        local(wv_hbm, wqkv.at[:, pl.ds(nqd + nkd, nkd)], 4),
        local(wo_hbm, wo, 5),
        local(w2_hbm, w2, 6),
        local(w1_hbm, w1, 7),
    ]
    x_in.start()
    dy_in.start()
    barrier = pltpu.get_barrier_semaphore()
    for dev in (part, peer):
        pl.semaphore_signal(barrier, inc=1, device_id={"tp": dev})
    for copy in weight_in:
        copy.start()

    outs = []

    def put(src, dst):
        copy = pltpu.make_async_copy(src, dst, out_sem.at[len(outs)])
        copy.start()
        outs.append(copy)

    class Gather:
        def __init__(self, buf):
            self.buf, self.base = buf, sems.take(6)

        def copy(self, kind, sub):
            owner = (me, me, peer)[kind]
            dev = (peer, part, part)[kind]
            piece = self.buf.at[block(owner, sub)]
            return remote(piece, piece, self.base + 2 * kind + sub, dev)

        def send(self, sub):
            for kind in (0, 1):
                self.copy(kind, sub).start()

        def forward(self, sub):
            self.copy(0, sub).wait_recv()
            self.copy(2, sub).start()

        def finish(self):
            for sub in (0, 1):
                self.copy(1, sub).wait_recv()
                self.copy(2, sub).wait_recv()

    class Scatter:
        def __init__(self, partial, from_part, summed, from_peer=None):
            self.partial, self.from_part, self.summed, self.from_peer = partial, from_part, summed, from_peer
            self.base = sems.take(2 * CHUNKS)
            self.link = sems.take(CHUNKS + 1) if from_peer is not None else None

        def cols(self, i):
            return pl.ds(pl.multiple_of(i * cw, cw), cw)

        def pair(self, i, kind):
            owner = (diag, part)[kind]
            return remote(self.partial.at[block(owner), self.cols(i)], self.from_part.at[kind, :, self.cols(i)], self.base + CHUNKS * kind + i, part)

        def first(self, i):
            top = pl.ds(0, half)
            return remote(self.summed.at[top, self.cols(i)], self.from_peer.at[top, self.cols(i)], self.link + i, peer)

        def second(self):
            low = pl.ds(half, half)
            return remote(self.summed.at[low], self.from_peer.at[low], self.link + CHUNKS, peer)

        def chip_sum(self, i):
            self.pair(i, 0).wait_recv()
            cols = self.cols(i)
            self.summed[:, cols] = self.partial[block(peer), cols] + self.from_part[0, :, cols]
            if self.from_peer is not None:
                self.first(i).start()

        def run(self, chunk, drain=True):
            def step(i, carry):
                self.partial[:, self.cols(i)] = chunk(self.cols(i))
                self.pair(i, 0).start()
                self.pair(i, 1).start()
                if drain:
                    @pl.when(i > 0)
                    def _():
                        self.chip_sum(i - 1)
                return carry

            lax.fori_loop(0, CHUNKS, step, 0)
            if drain:
                self.chip_sum(CHUNKS - 1)
            if self.from_peer is not None:
                self.second().start()

        def drain(self):
            for i in range(CHUNKS):
                self.chip_sum(i)

        def kept(self):
            for i in range(CHUNKS):
                self.pair(i, 1).wait_recv()

        def rows_sum(self, sub):
            if sub == 0:
                self.kept()
                for i in range(CHUNKS):
                    self.first(i).wait_recv()
            else:
                self.second().wait_recv()
            part_rows = pl.ds(sub * half, half)
            return (self.partial[block(me, sub), :] + self.from_part[1, part_rows, :]) + self.from_peer[part_rows, :]

    x_in.wait()
    h1[block(me), :] = norm_rows(x_own[...].astype(F32), g1_ref[...], b1_ref[...]).astype(BF16)
    pl.semaphore_wait(barrier, 2)
    gather_h1, gather_dy = Gather(h1), Gather(dyf)
    for sub in (0, 1):
        gather_h1.send(sub)
    dy_in.wait()
    for sub in (0, 1):
        gather_dy.send(sub)

    pos_rows = jnp.broadcast_to(pos_ref[...].astype(F32), (hd, seq)).T
    angles = pos_rows * freq_ref[...]
    lane = lax.broadcasted_iota(jnp.int32, (seq, hd), 1)
    rot = hd // 4
    cosb[...] = jnp.cos(angles)
    sinb[...] = jnp.where(lane < rot, -1.0, 1.0) * jnp.sin(angles)

    def turn(v, sign):
        other = jnp.where(lane < rot, pltpu.roll(v, hd - rot, 1), pltpu.roll(v, rot, 1))
        other = jnp.where(lane < 2 * rot, other, 0.0)
        return v * cosb[...] + (sign * sinb[...]) * other

    for sub in (0, 1):
        gather_h1.forward(sub)
    for copy in weight_in[:3]:
        copy.wait()
    gather_h1.finish()

    qkv = mm(h1[...], wqkv[...])
    for k in range(nk):
        for g in range(grp):
            lo = (k * grp + g) * hd
            head = qkv[:, lo:lo + hd].astype(BF16).astype(F32)
            qs[k, g * seq:(g + 1) * seq, :] = turn(head, 1.0).astype(BF16)
        lo = nqd + k * hd
        kv[0, k] = turn(qkv[:, lo:lo + hd].astype(BF16).astype(F32), 1.0).astype(BF16)
        lo = nqd + nkd + k * hd
        kv[1, k] = qkv[:, lo:lo + hd].astype(BF16)
    put(h1, h1_out)
    query = lax.rem(lax.broadcasted_iota(jnp.int32, (grp * seq, seq), 0), seq)
    causal = query >= lax.broadcasted_iota(jnp.int32, (grp * seq, seq), 1)
    for k in range(nk):
        scores = jnp.where(causal, mm_bt(qs[k], kv[0, k]) * hd ** -0.5, -1e30)
        exped = jnp.exp(scores - jnp.max(scores, axis=-1, keepdims=True))
        prob[k] = exped / jnp.sum(exped, axis=-1, keepdims=True)
        head_ctx = mm(prob[k].astype(BF16), kv[1, k]).astype(BF16)
        for g in range(grp):
            lo = (k * grp + g) * hd
            ctx[:, lo:lo + hd] = head_ctx[g * seq:(g + 1) * seq, :]
    put(ctx, ctx_out)
    weight_in[3].wait()
    sum_attn = Scatter(part_a, dr_a, snd_a, lnk_a)
    sum_attn.run(lambda cols: mm(ctx[...], wo[:, cols]))

    for sub in (0, 1):
        gather_dy.forward(sub)
    gather_dy.finish()
    weight_in[4].wait()
    put(dyf, dy_out)
    nb = f // 2

    def down_back(j, carry):
        cols = pl.ds(pl.multiple_of(j * nb, nb), nb)
        tmat[:, cols] = mm_bt(dyf[...], w2[cols, :])
        return carry

    lax.fori_loop(0, f // nb, down_back, 0)

    gather_h2 = Gather(h2)
    for sub in (0, 1):
        own = pl.ds(sub * half, half)
        attn_rows = sum_attn.rows_sum(sub).astype(BF16)
        mid_rows = (x_own[own, :].astype(F32) + attn_rows.astype(F32)).astype(BF16)
        mid[own, :] = mid_rows
        h2[block(me, sub), :] = norm_rows(mid_rows.astype(F32), g2_ref[...], b2_ref[...]).astype(BF16)
        gather_h2.send(sub)
    put(mid, mid_out)
    weight_in[5].wait()
    for sub in (0, 1):
        gather_h2.forward(sub)
    gather_h2.finish()

    def up(j, carry):
        cols = pl.ds(pl.multiple_of(j * nb, nb), nb)
        relu_up = jnp.maximum(mm(h2[...], w1[:, cols]).astype(BF16).astype(F32), 0.0)
        act[:, cols] = (relu_up * relu_up).astype(BF16)
        du[:, cols] = (tmat[:, cols] * (2.0 * relu_up)).astype(BF16)
        return carry

    lax.fori_loop(0, f // nb, up, 0)
    put(h2, h2_out)
    put(act, act_out)
    put(du, du_out)
    sum_dh2 = Scatter(part_b, dr_b, snd_b, lnk_b)
    sum_dh2.run(lambda cols: mm_bt(du[...], w1[cols, :]))

    sum_mlp = Scatter(part_c, dr_c, ysend)
    sum_mlp.run(lambda cols: mm(act[...], w2[:, cols]), drain=False)
    sum_mlp.drain()
    sum_mlp.kept()
    ykeep[...] = part_c[block(me), :] + dr_c[1]
    put(ysend, ysend_out)
    put(ykeep, ykeep_out)

    gather_dx1 = Gather(dx1)
    for sub in (0, 1):
        own = pl.ds(sub * half, half)
        dh2_rows = sum_dh2.rows_sum(sub).astype(BF16).astype(F32)
        grad_rows, grad_gain, grad_bias = norm_rows_back(mid[own, :].astype(F32), dh2_rows, g2_ref[...])
        dx1[block(me, sub), :] = (dyf[block(me, sub), :].astype(F32) + grad_rows).astype(BF16)
        gather_dx1.send(sub)
        if sub == 0:
            lng[0:1, :] = grad_gain
            lng[1:2, :] = grad_bias
        else:
            lng[0:1, :] += grad_gain
            lng[1:2, :] += grad_bias
    put(lng, lng_out)
    put(dx1.at[block(me)], dmid_out)
    for sub in (0, 1):
        gather_dx1.forward(sub)
    gather_dx1.finish()
    put(dx1, dx1_out)

    dctx = mm_bt(dx1[...], wo[...]).astype(BF16)
    for k in range(nk):
        for g in range(grp):
            lo = (k * grp + g) * hd
            gcs[k, g * seq:(g + 1) * seq, :] = dctx[:, lo:lo + hd]
    for k in range(nk):
        grad_v = mm_at(prob[k].astype(BF16), gcs[k]).astype(BF16)
        grad_p = mm_bt(gcs[k], kv[1, k])
        grad_s = (prob[k] * (grad_p - jnp.sum(grad_p * prob[k], axis=-1, keepdims=True)) * hd ** -0.5).astype(BF16)
        grad_q = mm(grad_s, kv[0, k])
        for g in range(grp):
            lo = (k * grp + g) * hd
            dqkv[:, lo:lo + hd] = turn(grad_q[g * seq:(g + 1) * seq, :], -1.0).astype(BF16)
        lo = nqd + k * hd
        dqkv[:, lo:lo + hd] = turn(mm_at(grad_s, qs[k]), -1.0).astype(BF16)
        lo = nqd + nkd + k * hd
        dqkv[:, lo:lo + hd] = grad_v
    put(dqkv, dqkv_out)
    sum_dh1 = Scatter(part_a, dr_d, hsend)
    for i in range(CHUNKS):
        sum_attn.pair(i, 0).wait_send()
        sum_attn.pair(i, 1).wait_send()
    sum_dh1.run(lambda cols: mm_bt(dqkv[...], wqkv[cols, :]))
    put(hsend, hsend_out)
    sum_dh1.kept()
    hkeep[...] = part_a[block(me), :] + dr_d[1]
    put(hkeep, hkeep_out)

    for gather in (gather_h1, gather_dy, gather_h2, gather_dx1):
        for kind in (0, 1, 2):
            for sub in (0, 1):
                gather.copy(kind, sub).wait_send()
    for scatter in (sum_attn, sum_dh2, sum_mlp, sum_dh1):
        for i in range(CHUNKS):
            if scatter is not sum_attn:
                scatter.pair(i, 0).wait_send()
                scatter.pair(i, 1).wait_send()
            if scatter.from_peer is not None:
                scatter.first(i).wait_send()
        if scatter.from_peer is not None:
            scatter.second().wait_send()
    for copy in outs:
        copy.wait()


def chain(dims, x, dy, pos, freq, g1, b1, g2, b2, wq, wk, wv, wo, w1, w2):
    seq, d, hd, nq, nk, f, rows = dims
    grp = nq // nk
    nqd, nkd = nq * hd, nk * hd
    n_all = nqd + 2 * nkd

    def arr(shape, dtype):
        return jax.ShapeDtypeStruct(shape, dtype)

    def vm(*shape, dtype=BF16):
        return pltpu.VMEM(shape, dtype)

    def vf(*shape):
        return pltpu.VMEM(shape, F32)

    out_shape = [arr((seq, d), BF16)] * 4 + [arr((seq, f), BF16)] * 2 + [arr((seq, nqd), BF16), arr((seq, n_all), BF16)] + [arr((rows, d), BF16)] * 2 + [arr((rows, d), F32)] * 4 + [arr((2, d), F32)]
    scratch = [
        vm(d, n_all), vm(nqd, d), vm(d, f), vm(f, d),
        vm(seq, d), vm(seq, d), vm(seq, d), vm(seq, d),
        vm(rows, d), vm(rows, d), vf(seq, f), vm(seq, f), vm(seq, f),
        vm(nk, grp * seq, hd), vm(2, nk, seq, hd), vm(seq, nqd), vf(nk, grp * seq, seq),
        vf(seq, hd), vf(seq, hd), vm(nk, grp * seq, hd), vm(seq, n_all), vf(2, d),
        vf(seq, d), vf(seq, d), vf(seq, d),
        vf(2, rows, d), vf(2, rows, d), vf(2, rows, d), vf(2, rows, d),
        vf(rows, d), vf(rows, d), vf(rows, d), vf(rows, d),
        vf(rows, d), vf(rows, d), vf(rows, d), vf(rows, d),
        pltpu.SemaphoreType.DMA((8,)), pltpu.SemaphoreType.DMA((15,)),
        pltpu.SemaphoreType.DMA((4 * 6 + 4 * 2 * CHUNKS + 2 * (CHUNKS + 1),)),
        pltpu.SemaphoreType.DMA((4 * 6 + 4 * 2 * CHUNKS + 2 * (CHUNKS + 1),)),
    ]
    return pl.pallas_call(
        functools.partial(chain_kernel, dims),
        out_shape=out_shape,
        in_specs=[ANY, ANY] + [VMEM] * 6 + [ANY] * 6,
        out_specs=[ANY] * len(out_shape),
        scratch_shapes=scratch,
        compiler_params=pltpu.CompilerParams(collective_id=0, has_side_effects=True, vmem_limit_bytes=VMEM_LIMIT),
        name="chain",
    )(x, dy, pos, freq, g1, b1, g2, b2, wq, wk, wv, wo, w1, w2)


SLOTS = 4
TILE = 256


def stream_grads(jobs, stage, sem):
    base = 0
    for tiles, width, compute, targets in jobs:
        def copies(i, slot):
            return [pltpu.make_async_copy(stage.at[slot, :, pl.ds(lo, n)], dst, sem.at[slot, c]) for c, (dst, lo, n) in enumerate(targets(i))]

        def step(i, carry):
            slot = lax.rem(i, SLOTS)

            @pl.when(i >= SLOTS)
            def _():
                for copy in copies(i - SLOTS, slot):
                    copy.wait()

            stage[slot, :, :width] = compute(i)
            for copy in copies(i, slot):
                copy.start()
            return carry

        lax.fori_loop(0, tiles, step, 0)
        for i in range(max(tiles - SLOTS, 0), tiles):
            for copy in copies(i, i % SLOTS):
                copy.wait()


def grads_first_kernel(act_hbm, dy_hbm, ctx_hbm, dx1_hbm, dw2, dwo, act, dyf, ctx, dx1, stage, in_sem, sem):
    loads = [pltpu.make_async_copy(s, t, in_sem.at[i]) for i, (s, t) in enumerate(((act_hbm, act), (dy_hbm, dyf), (ctx_hbm, ctx), (dx1_hbm, dx1)))]
    for copy in loads:
        copy.start()
    loads[0].wait()
    loads[1].wait()

    def tile(i):
        return pl.ds(pl.multiple_of(i * TILE, TILE), TILE)

    d = dyf.shape[1]
    stream_grads([(act.shape[1] // TILE, d, lambda i: mm_at(act[:, tile(i)], dyf[...]), lambda i: [(dw2.at[tile(i)], 0, d)])], stage, sem)
    loads[2].wait()
    loads[3].wait()
    stream_grads([(ctx.shape[1] // TILE, d, lambda i: mm_at(ctx[:, tile(i)], dx1[...]), lambda i: [(dwo.at[tile(i)], 0, d)])], stage, sem)


def grads_second_kernel(dims, h2_hbm, du_hbm, h1_hbm, dqkv_hbm, dw1, dwq, dwk, dwv, h2, du, h1, dqkv, stage, in_sem, sem):
    seq, d, hd, nq, nk, f, rows = dims
    loads = [pltpu.make_async_copy(s, t, in_sem.at[i]) for i, (s, t) in enumerate(((h2_hbm, h2), (du_hbm, du), (h1_hbm, h1), (dqkv_hbm, dqkv)))]
    for copy in loads:
        copy.start()
    loads[0].wait()
    loads[1].wait()

    def tile(i):
        return pl.ds(pl.multiple_of(i * TILE, TILE), TILE)

    nqd, nkd = nq * hd, nk * hd
    stream_grads([(d // TILE, f, lambda i: mm_at(h2[:, tile(i)], du[...]), lambda i: [(dw1.at[tile(i)], 0, f)])], stage, sem)
    loads[2].wait()
    loads[3].wait()
    stream_grads([(d // TILE, nqd + 2 * nkd, lambda i: mm_at(h1[:, tile(i)], dqkv[...]),
                   lambda i: [(dwq.at[tile(i)], 0, nqd), (dwk.at[tile(i)], nqd, nkd), (dwv.at[tile(i)], nqd + nkd, nkd)])], stage, sem)


def cost(flops, nbytes):
    return pl.CostEstimate(flops=flops, bytes_accessed=nbytes, transcendentals=0)


def grads_first(dims, act, dyf, ctx, dx1):
    seq, d, hd, nq, nk, f, rows = dims
    nqd = nq * hd
    return pl.pallas_call(
        grads_first_kernel,
        out_shape=[jax.ShapeDtypeStruct((f, d), F32), jax.ShapeDtypeStruct((nqd, d), F32)],
        in_specs=[ANY] * 4, out_specs=[ANY] * 2,
        scratch_shapes=[pltpu.VMEM((seq, f), BF16), pltpu.VMEM((seq, d), BF16), pltpu.VMEM((seq, nqd), BF16), pltpu.VMEM((seq, d), BF16),
                        pltpu.VMEM((SLOTS, TILE, d), F32), pltpu.SemaphoreType.DMA((4,)), pltpu.SemaphoreType.DMA((SLOTS, 3))],
        compiler_params=pltpu.CompilerParams(vmem_limit_bytes=40 << 20),
        cost_estimate=cost(2 * seq * d * (f + nqd), 4 * d * (f + nqd)),
        name="grads_first",
    )(act, dyf, ctx, dx1)


def grads_second(dims, h2, du, h1, dqkv):
    seq, d, hd, nq, nk, f, rows = dims
    nqd, nkd = nq * hd, nk * hd
    n_all = nqd + 2 * nkd
    return pl.pallas_call(
        functools.partial(grads_second_kernel, dims),
        out_shape=[jax.ShapeDtypeStruct((d, f), F32), jax.ShapeDtypeStruct((d, nqd), F32), jax.ShapeDtypeStruct((d, nkd), F32), jax.ShapeDtypeStruct((d, nkd), F32)],
        in_specs=[ANY] * 4, out_specs=[ANY] * 4,
        scratch_shapes=[pltpu.VMEM((seq, d), BF16), pltpu.VMEM((seq, f), BF16), pltpu.VMEM((seq, d), BF16), pltpu.VMEM((seq, n_all), BF16),
                        pltpu.VMEM((SLOTS, TILE, f), F32), pltpu.SemaphoreType.DMA((4,)), pltpu.SemaphoreType.DMA((SLOTS, 3))],
        compiler_params=pltpu.CompilerParams(vmem_limit_bytes=40 << 20),
        cost_estimate=cost(2 * seq * d * (f + n_all), 4 * d * (f + n_all)),
        name="grads_second",
    )(h2, du, h1, dqkv)


def last_norm_kernel(hkeep, hrecv, x, dmid, g1, lng2, dx_out, lng_out):
    dh1 = (hkeep[...] + hrecv[...]).astype(BF16).astype(F32)
    grad_rows, grad_gain, grad_bias = norm_rows_back(x[...].astype(F32), dh1, g1[...])
    dx_out[...] = (dmid[...].astype(F32) + grad_rows).astype(BF16)
    lng_out[0:1, :] = grad_gain
    lng_out[1:2, :] = grad_bias
    lng_out[2:4, :] = lng2[...]


def last_norm(hkeep, hrecv, x, dmid, g1, lng2):
    rows, d = x.shape
    return pl.pallas_call(
        last_norm_kernel,
        out_shape=[jax.ShapeDtypeStruct((rows, d), BF16), jax.ShapeDtypeStruct((4, d), F32)],
        in_specs=[VMEM] * 6, out_specs=[VMEM] * 2,
        cost_estimate=cost(rows * d * 20, rows * d * 16),
        name="last_norm",
    )(hkeep, hrecv, x, dmid, g1, lng2)


def layer_step(x, dy, positions, g1, b1, g2, b2, wq, wk, wv, wo, w1, w2, head_dim, n_tp):
    rows, batch, d = x.shape
    seq = positions.shape[0]
    nq, nk, f = wq.shape[1] // head_dim, wk.shape[1] // head_dim, w1.shape[1]
    dims = (seq, d, head_dim, nq, nk, f, rows)
    rot = head_dim // 4
    freq = np.zeros((1, head_dim), np.float32)
    freq[0, :2 * rot] = np.tile(ROPE_BASE ** (-np.arange(rot) / rot), 2)
    x2, dy2 = x.reshape(rows, d), dy.reshape(rows, d)
    g1, b1, g2, b2 = (v.reshape(1, d) for v in (g1, b1, g2, b2))
    (h1, h2, dyf, dx1, act, du, ctx, dqkv, mid, dmid, ysend, ykeep, hsend, hkeep, lng2) = chain(
        dims, x2, dy2, positions.reshape(1, seq), jnp.asarray(freq), g1, b1, g2, b2, wq, wk, wv, wo, w1, w2)
    def swap(v, bit):
        return lax.ppermute(v, 'tp', [(i, i ^ bit) for i in range(n_tp)])

    hrecv = swap(hsend, 2)
    yrecv = swap(ysend, 2)
    dw2, dwo = grads_first(dims, act, dyf, ctx, dx1)
    dx, lng = last_norm(hkeep, hrecv, x2, dmid, g1, lng2)
    others = [swap(lng, bit) for bit in (1, 2, 3)]
    dw1, dwq, dwk, dwv = grads_second(dims, h2, du, h1, dqkv)
    total = (lng + others[0]) + (others[1] + others[2])
    y = (mid.astype(F32) + (ykeep + yrecv).astype(BF16).astype(F32)).astype(BF16)
    return (y.reshape(x.shape), dx.reshape(x.shape), total[0], total[1], total[2], total[3], dwq, dwk, dwv, dwo, dw1, dw2)


def solution(mesh):
    seq_spec = P(('dp', 'tp'))
    col_spec = P(None, 'tp')
    row_spec = P('tp', None)
    grad_col_spec = P('dp', 'tp')
    grad_row_spec = P(('dp', 'tp'), None)
    in_specs = (seq_spec, seq_spec, P('dp'), P(), P(), P(), P(), col_spec, col_spec, col_spec, row_spec, col_spec, row_spec)
    out_specs = (seq_spec, seq_spec, P('dp'), P('dp'), P('dp'), P('dp'), grad_col_spec, grad_col_spec, grad_col_spec, grad_row_spec, grad_col_spec, grad_row_spec)

    def run_layer(resid_in, grad_out, positions, ln1_gain, ln1_bias, ln2_gain, ln2_bias, w_query, w_key, w_value, w_out, w_up, w_down):
        step_fn = functools.partial(layer_step, head_dim=w_key.shape[1] // KV_HEADS, n_tp=mesh.shape['tp'])
        sharded = jax.shard_map(step_fn, mesh=mesh, in_specs=in_specs, out_specs=out_specs, check_vma=False)
        return sharded(resid_in, grad_out, positions, ln1_gain, ln1_bias, ln2_gain, ln2_bias, w_query, w_key, w_value, w_out, w_up, w_down)

    return run_layer
```

time: 224 us -> 111 us (0.50)
  matrix products: 93.5 us -> 0 us
  Pallas kernels: 0 us -> 91.9 us
  blocking collectives: 58.4 us -> 0 us
  waiting for transfers between devices: 38.1 us -> 2.11 us
  between operations: 14.5 us -> 0.72 us
  other arithmetic: 13.7 us -> 1.55 us
  local copies, waits for them, and re-layouts: 5.13 us -> 9.9 us
  starting transfers between devices: 0.16 us -> 4.19 us
    dot_general x24 -> x0, matrix products: 93.5 us -> none  [the longest x1 11.9 us: layer_step(): jnp.einsum('sbf,sbm->fm', mlp_act, grad_full, preferred_element_type=jnp....]
    pallas_call x0 -> x4, Pallas kernels: none -> 91.9 us  [the longest x1 60.5 us: chain(): pl.pallas_call(functools.partial(chain_kernel, dims), out_shape=out_shape...]
    all_gather x4 -> x0, blocking collectives: 47.9 us -> none  [the longest x1 13 us: layer_step(): lax.all_gather(layer_norm_1p(resid_f, ln1_gain, ln1_bias).astype(jnp.bflo...]
    reduce_scatter x4 -> x0, waiting for transfers between devices: 38 us -> none  [the longest x1 23.9 us: layer_step(): lax.psum_scatter(jnp.dot(mlp_act, w_down, preferred_element_type=jnp.floa...]
    psum x1 -> x0, blocking collectives: 10.6 us -> none  [layer_step(): lax.psum(jnp.stack([grad_ln1_gain, grad_ln1_bias, grad_ln2_gain, grad_ln2...]
    reduce_sum x9 -> x0, other arithmetic: 6.86 us -> none  [the longest x4 3.09 us: layer_norm_1p(): return centred * lax.rsqrt(var_val + LN_EPS) * (1.0 + gain) + bias]
    unnamed x88 -> x22, local copies, waits for them, and re-layouts: 3.24 us -> 9.26 us
    convert_element_type x7 -> x0, other arithmetic: 4.27 us -> none  [the longest x1 1.87 us: layer_step(): grad_mid = (grad_loc.astype(jnp.float32) + grad_mid_ln).astype(jnp.bfloat16)]
  transfers between devices with their start and end apart: 4 -> 5, of which waited for: 3 -> 2; matrix products, arithmetic and copies ran while one was open for 21% -> 1% of each run, Pallas kernels for 0% -> 28%
where the time goes in v1:
time: 111 us; the launch traced here: 110 us
  Pallas kernels  91.9 us (83%)
  local copies, waits for them, and re-layouts  9.9 us (9%)
  starting transfers between devices  4.19 us (4%)
  waiting for transfers between devices  2.11 us (2%)
  other arithmetic  1.55 us (1%)
    pallas_call x1, Pallas kernels, chain(): pl.pallas_call(functools.partial(chain_kernel, dims), out_shape=out_shape...  60.5 us
    pallas_call x1, Pallas kernels, grads_second(): pl.pallas_call(functools.partial(grads_second_kernel, dims), out_shape=[j...  15.1 us
    pallas_call x1, Pallas kernels, grads_first(): pl.pallas_call(grads_first_kernel, out_shape=[jax.ShapeDtypeStruct((f, d)...  13.9 us
    unnamed x22, local copies, waits for them, and re-layouts  9.26 us
    ppermute x5, starting transfers between devices, swap(): return lax.ppermute(v, 'tp', [(i, i ^ bit) for i in range(n_tp)])  4.19 us
    pallas_call x1, Pallas kernels, last_norm(): pl.pallas_call(last_norm_kernel, out_shape=[jax.ShapeDtypeStruct((rows, d...  2.45 us
  transfers between devices with their start and end apart: 5, of which 2 were waited for; matrix products, arithmetic and copies ran while one was open for 1% of the time, Pallas kernels for 28%

profile of v1, /device:TPU:0, one launch (start us, length us, event | category | flops | bytes accessed | tf_op | source)
XLA Modules:
  0.0 110.4 jit_solution(13862675472799235742)
XLA Ops:
  0.6 60.5 %chain.1 = (bf16[128,3072]{1,0:T(8,128)(2,1)}, bf16[128,3072]{1,0:T(8,128)(2,1)}, bf16[128,3072]{1,0:T(8,128)(2,1)}, bf16[128,3072]{1,0:T(8,128)(2,1)}, bf16[128...) custom-call(bf16[32,3072]{1,0:T(8,128)(2,1)} %bitcast.14, ...), custom_call_target="tpu_custom_call" | custom-call | tf_op jit(solution)/shard_map/chain/pallas_call | solution.py:398
  61.1 1.0 collective-permute-start
  62.1 1.1 collective-permute-start.1
  63.2 1.1 %copy-done.2 = bf16[128,3072]{1,0:T(8,128)(2,1)S(1)} copy-done((bf16[128,3072]{1,0:T(8,128)(2,1)S(1)}, bf16[128,3072]{1,0:T(8,128)(2,1)}, u32[]{:S(2)}) %copy-start.2) | copy-done | bytes 786456
  64.3 1.1 %copy-done.3 = bf16[128,3072]{1,0:T(8,128)(2,1)S(1)} copy-done((bf16[128,3072]{1,0:T(8,128)(2,1)S(1)}, bf16[128,3072]{1,0:T(8,128)(2,1)}, u32[]{:S(2)}) %copy-start.3) | copy-done | bytes 786456
  65.5 1.0 copy-done.5
  66.5 0.9 copy-done.7
  67.4 13.9 %grads_first.1 = (f32[2048,3072]{1,0:T(8,128)}, f32[768,3072]{1,0:T(8,128)}) custom-call(bf16[128,2048]{1,0:T(8,128)(2,1)S(1)} %copy-done.5, bf16[128,3072]{1,0:T(8,128)(2,1)S(1)} %copy-done.2, bf16[128,768]{1,0:T(8,128)(2,1)S(1)} %copy-done.7, bf16[128,3072]{1,0:T(8,128)(2,1)S(1)} %copy-done.3), custom_call_target="tpu_custom_call" | custom-call | flops 2214592512 | bytes 34603008 | tf_op jit(solution)/shard_map/grads_first/pallas_call | solution.py:481
  81.4 1.1 %copy-done = bf16[128,3072]{1,0:T(8,128)(2,1)S(1)} copy-done((bf16[128,3072]{1,0:T(8,128)(2,1)S(1)}, bf16[128,3072]{1,0:T(8,128)(2,1)}, u32[]{:S(2)}) %copy-start) | copy-done | bytes 786456
  82.5 1.1 %copy-done.1 = bf16[128,3072]{1,0:T(8,128)(2,1)S(1)} copy-done((bf16[128,3072]{1,0:T(8,128)(2,1)S(1)}, bf16[128,3072]{1,0:T(8,128)(2,1)}, u32[]{:S(2)}) %copy-start.1) | copy-done | bytes 786456
  83.6 1.0 copy-done.4
  84.7 1.0 copy-done.6
  85.7 15.1 %grads_second.1 = (f32[3072,2048]{1,0:T(8,128)}, f32[3072,768]{1,0:T(8,128)}, f32[3072,256]{1,0:T(8,128)}, f32[3072,256]{1,0:T(8,128)}) custom-call(bf16[128,3072]{1,0:T(8,128)(2,1)S(1)} %copy-done.1, bf16[128,2048]{1,0:T(8,128)(2,1)S(1)} %copy-done.4, bf16[128,3072]{1,0:T(8,128)(2,1)S(1)} %copy-done, bf16[128,1280]{1,0:T(8,128)(2,1)S(1)} %copy-done.6), custom_call_target="tpu_custom_call" | custom-call | flops 2617245696 | bytes 40894464 | tf_op jit(solution)/shard_map/grads_second/pallas_call | solution.py:497
  100.7 0.7 copy-done.9
  101.5 2.5 %last_norm.1 = (bf16[32,3072]{1,0:T(8,128)(2,1)}, f32[4,3072]{1,0:T(4,128)}) custom-call(f32[32,3072]{1,0:T(8,128)} %get-tuple-element.38.hkeep, f32[32,3072]{1,0:T(8,128)} %copy-done.9, bf16[32,3072]{1,0:T(8,128)(2,1)} %bitcast.15, bf16[32,3072]{1,0:T(8,128)(2,1)} %get-tuple-element.40.dmid, f32[1,3072]{1,0:T(1,128)} %bitcast.18, ...), custom_call_target="tpu_custom_call" | custom-call | flops 1966080 | bytes 1572864 | tf_op jit(solution)/shard_map/last_norm/pallas_call | solution.py:520
  103.9 0.9 collective-permute-start.3
  104.9 0.4 collective-permute-start.4
  105.2 0.8 collective-permute-start.2
  106.1 0.7 fusion
  106.8 1.4 %collective-permute-done.3 = f32[4,3072]{1,0:T(4,128)S(1)} collective-permute-done((f32[4,3072]{1,0:T(4,128)}, f32[4,3072]{1,0:T(4,128)S(1)}, u32[]{:S(2)}, u32[]{:S(2)}) %collective-permute-start.3) | collective-permute-done | bytes 49184 | tf_op jit(solution)/shard_map/ppermute | solution.py:542
  108.2 0.7 collective-permute-done.4
  108.9 0.0 collective-permute-done.2
  108.9 0.8 add_add_fusion
  109.7 0.6 fusion.1
  (15 shorter events, 0.0 us)
Async XLA Ops:
  61.1 44.9 %collective-permute-start = (f32[32,3072]{1,0:T(8,128)}, f32[32,3072]{1,0:T(8,128)S(1)}, u32[]{:S(2)}, u32[]{:S(2)}) collective-permute-start(f32[32,3072]{1,0:T(8,128)} %get-tuple-element.37), channel_id=1, source_target_pairs={{0,2},{1,3},{2,0},{3,1},{4,6},{5,7},{6,4},{7,5}} | collective-permute-start | bytes 1179656 | tf_op jit(solution)/shard_map/ppermute | solution.py:542
  62.1 38.6 %collective-permute-start.1 = (f32[32,3072]{1,0:T(8,128)}, f32[32,3072]{1,0:T(8,128)S(1)}, u32[]{:S(2)}, u32[]{:S(2)}) collective-permute-start(f32[32,3072]{1,0:T(8,128)} %get-tuple-element.39), channel_id=1, source_target_pairs={{0,2},{1,3},{2,0},{3,1},{4,6},{5,7},{6,4},{7,5}} | collective-permute-start | bytes 1179656 | tf_op jit(solution)/shard_map/ppermute | solution.py:542
  63.2 1.1 %copy-start.2 = (bf16[128,3072]{1,0:T(8,128)(2,1)S(1)}, bf16[128,3072]{1,0:T(8,128)(2,1)}, u32[]{:S(2)}) copy-start(bf16[128,3072]{1,0:T(8,128)(2,1)} %get-tuple-element.52.dy_hbm) | copy-start | bytes 2359300
  64.3 1.1 %copy-start.3 = (bf16[128,3072]{1,0:T(8,128)(2,1)S(1)}, bf16[128,3072]{1,0:T(8,128)(2,1)}, u32[]{:S(2)}) copy-start(bf16[128,3072]{1,0:T(8,128)(2,1)} %get-tuple-element.54.dx1_hbm) | copy-start | bytes 2359300
  65.5 1.0 copy-start.5
  66.5 0.9 copy-start.7
  67.4 38.6 %copy-start.8 = (f32[32,3072]{1,0:T(8,128)S(1)}, f32[32,3072]{1,0:T(8,128)}, u32[]{:S(2)}) copy-start(f32[32,3072]{1,0:T(8,128)} %get-tuple-element.36) | copy-start | bytes 1179652
  67.4 38.6 %copy-start.10 = (bf16[32,3072]{1,0:T(8,128)(2,1)S(1)}, bf16[32,3072]{1,0:T(8,128)(2,1)}, u32[]{:S(2)}) copy-start(bf16[32,3072]{1,0:T(8,128)(2,1)} %get-tuple-element.35) | copy-start | bytes 589828
  81.4 1.1 %copy-start = (bf16[128,3072]{1,0:T(8,128)(2,1)S(1)}, bf16[128,3072]{1,0:T(8,128)(2,1)}, u32[]{:S(2)}) copy-start(bf16[128,3072]{1,0:T(8,128)(2,1)} %get-tuple-element.46.h1_hbm) | copy-start | bytes 2359300
  82.5 1.1 %copy-start.1 = (bf16[128,3072]{1,0:T(8,128)(2,1)S(1)}, bf16[128,3072]{1,0:T(8,128)(2,1)}, u32[]{:S(2)}) copy-start(bf16[128,3072]{1,0:T(8,128)(2,1)} %get-tuple-element.44.h2_hbm) | copy-start | bytes 2359300
  83.6 1.0 copy-start.4
  84.7 1.0 copy-start.6
  100.7 0.8 copy-start.9
  103.9 4.3 %collective-permute-start.3 = (f32[4,3072]{1,0:T(4,128)}, f32[4,3072]{1,0:T(4,128)S(1)}, u32[]{:S(2)}, u32[]{:S(2)}) collective-permute-start(f32[4,3072]{1,0:T(4,128)} %get-tuple-element.43), channel_id=1, source_target_pairs={{0,2},{1,3},{2,0},{3,1},{4,6},{5,7},{6,4},{7,5}} | collective-permute-start | bytes 147464 | tf_op jit(solution)/shard_map/ppermute | solution.py:542
  104.9 4.0 %collective-permute-start.4 = (f32[4,3072]{1,0:T(4,128)}, f32[4,3072]{1,0:T(4,128)S(1)}, u32[]{:S(2)}, u32[]{:S(2)}) collective-permute-start(f32[4,3072]{1,0:T(4,128)} %get-tuple-element.43), channel_id=1, source_target_pairs={{0,3},{1,2},{2,1},{3,0},{4,7},{5,6},{6,5},{7,4}} | collective-permute-start | bytes 147464 | tf_op jit(solution)/shard_map/ppermute | solution.py:542
  105.2 3.7 %collective-permute-start.2 = (f32[4,3072]{1,0:T(4,128)}, f32[4,3072]{1,0:T(4,128)S(1)}, u32[]{:S(2)}, u32[]{:S(2)}) collective-permute-start(f32[4,3072]{1,0:T(4,128)} %get-tuple-element.43), channel_id=1, source_target_pairs={{0,1},{1,0},{2,3},{3,2},{4,5},{5,4},{6,7},{7,6}} | collective-permute-start | bytes 147464 | tf_op jit(solution)/shard_map/ppermute | solution.py:542

commit v2 on v1

--- a/solution.py
+++ b/solution.py
@@ -60,10 +60,11 @@
         return base
 
 
-def chain_kernel(dims, x_hbm, dy_hbm, pos_ref, freq_ref, g1_ref, b1_ref, g2_ref, b2_ref, wq_hbm, wk_hbm, wv_hbm, wo_hbm, w1_hbm, w2_hbm,
-                 h1_out, h2_out, dy_out, dx1_out, act_out, du_out, ctx_out, dqkv_out, mid_out, dmid_out, ysend_out, ykeep_out, hsend_out, hkeep_out, lng_out,
-                 wqkv, wo, w1, w2, h1, h2, dyf, dx1, x_own, mid, tmat, act, du, qs, kv, ctx, prob, cosb, sinb, gcs, dqkv, lng,
-                 part_a, part_b, part_c, dr_a, dr_b, dr_c, dr_d, snd_a, snd_b, lnk_a, lnk_b, ysend, ykeep, hsend, hkeep,
+def chain_kernel(dims, x_hbm, dy_hbm, pos_hbm, freq_hbm, g1_hbm, b1_hbm, g2_hbm, b2_hbm, wq_hbm, wk_hbm, wv_hbm, wo_hbm, w1_hbm, w2_hbm,
+                 h1_out, h2_out, dy_out, dx1_out, act_out, du_out, ctx_out, dqkv_out, y_out, dmid_out, hsend_out, hkeep_out, lng_out,
+                 pos_ref, freq_ref, g1_ref, b1_ref, g2_ref, b2_ref,
+                 wqkv, wo, w1, w2, h1, h2, dyf, dx1, x_own, mid, y_own, tmat, act, du, qs, kv, ctx, prob, cosb, sinb, gcs, dqkv, lng,
+                 part_a, part_b, part_c, dr_a, dr_b, dr_c, dr_d, snd_a, snd_b, snd_c, lnk_a, lnk_b, lnk_c, hsend, hkeep,
                  local_sem, out_sem, send_sem, recv_sem):
     seq, d, hd, nq, nk, f, rows = dims
     grp = nq // nk
@@ -95,7 +96,11 @@
         local(w2_hbm, w2, 6),
         local(w1_hbm, w1, 7),
     ]
+    small_in = [local(src, dst, 8 + i) for i, (src, dst) in enumerate((
+        (g1_hbm, g1_ref), (b1_hbm, b1_ref), (pos_hbm, pos_ref), (freq_hbm, freq_ref), (g2_hbm, g2_ref), (b2_hbm, b2_ref)))]
     x_in.start()
+    for copy in small_in:
+        copy.start()
     dy_in.start()
     barrier = pltpu.get_barrier_semaphore()
     for dev in (part, peer):
@@ -111,27 +116,40 @@
         outs.append(copy)
 
     class Gather:
-        def __init__(self, buf):
-            self.buf, self.base = buf, sems.take(6)
-
-        def copy(self, kind, sub):
+        def __init__(self, buf, pieces):
+            self.buf, self.pieces, self.base = buf, pieces, sems.take(3 * len(pieces))
+
+        def copy(self, kind, i):
             owner = (me, me, peer)[kind]
             dev = (peer, part, part)[kind]
-            piece = self.buf.at[block(owner, sub)]
-            return remote(piece, piece, self.base + 2 * kind + sub, dev)
-
-        def send(self, sub):
-            for kind in (0, 1):
-                self.copy(kind, sub).start()
-
-        def forward(self, sub):
-            self.copy(0, sub).wait_recv()
-            self.copy(2, sub).start()
-
-        def finish(self):
-            for sub in (0, 1):
-                self.copy(1, sub).wait_recv()
-                self.copy(2, sub).wait_recv()
+            row, n_rows, col, n_cols = self.pieces[i]
+            at = self.buf.at[pl.ds(pl.multiple_of(owner * rows + row, half), n_rows), pl.ds(col, n_cols)]
+            return remote(at, at, self.base + len(self.pieces) * kind + i, dev)
+
+        def send(self, i):
+            self.copy(0, i).start()
+            self.copy(1, i).start()
+
+        def forward(self, i):
+            self.copy(0, i).wait_recv()
+            self.copy(2, i).start()
+
+        def finish(self, i):
+            self.copy(1, i).wait_recv()
+            self.copy(2, i).wait_recv()
+
+        def feed(self, first, use):
+            count = len(self.pieces)
+            for i in range(first):
+                self.forward(i)
+            self.forward(first)
+            for i in range(first):
+                self.finish(i)
+            for i in range(first, count):
+                if i + 1 < count:
+                    self.forward(i + 1)
+                self.finish(i)
+                use(i - first, pl.ds(self.pieces[i][2], self.pieces[i][3]))
 
     class Scatter:
         def __init__(self, partial, from_part, summed, from_peer=None):
@@ -175,12 +193,13 @@
             lax.fori_loop(0, CHUNKS, step, 0)
             if drain:
                 self.chip_sum(CHUNKS - 1)
-            if self.from_peer is not None:
-                self.second().start()
+                if self.from_peer is not None:
+                    self.second().start()
 
         def drain(self):
             for i in range(CHUNKS):
                 self.chip_sum(i)
+            self.second().start()
 
         def kept(self):
             for i in range(CHUNKS):
@@ -197,15 +216,20 @@
             return (self.partial[block(me, sub), :] + self.from_part[1, part_rows, :]) + self.from_peer[part_rows, :]
 
     x_in.wait()
+    small_in[0].wait()
+    small_in[1].wait()
     h1[block(me), :] = norm_rows(x_own[...].astype(F32), g1_ref[...], b1_ref[...]).astype(BF16)
     pl.semaphore_wait(barrier, 2)
-    gather_h1, gather_dy = Gather(h1), Gather(dyf)
-    for sub in (0, 1):
-        gather_h1.send(sub)
+    wide = [(0, rows, i * cw, cw) for i in range(CHUNKS)]
+    late = [(0, half, 0, d)] + [(half, half, i * cw, cw) for i in range(CHUNKS)]
+    gather_h1, gather_dy = Gather(h1, wide), Gather(dyf, [(0, rows, 0, d)])
+    for i in range(CHUNKS):
+        gather_h1.send(i)
     dy_in.wait()
-    for sub in (0, 1):
-        gather_dy.send(sub)
-
+    gather_dy.send(0)
+
+    small_in[2].wait()
+    small_in[3].wait()
     pos_rows = jnp.broadcast_to(pos_ref[...].astype(F32), (hd, seq)).T
     angles = pos_rows * freq_ref[...]
     lane = lax.broadcasted_iota(jnp.int32, (seq, hd), 1)
@@ -218,13 +242,17 @@
         other = jnp.where(lane < 2 * rot, other, 0.0)
         return v * cosb[...] + (sign * sinb[...]) * other
 
-    for sub in (0, 1):
-        gather_h1.forward(sub)
     for copy in weight_in[:3]:
         copy.wait()
-    gather_h1.finish()
-
-    qkv = mm(h1[...], wqkv[...])
+    n_all = nqd + 2 * nkd
+
+    def add(total, j, piece):
+        total[...] = piece if j == 0 else total[...] + piece
+
+    qkv_sum = part_c.at[:, pl.ds(0, n_all)]
+    gather_h1.feed(0, lambda j, cols: add(qkv_sum, j, mm(h1[:, cols], wqkv[cols, :])))
+
+    qkv = qkv_sum
     for k in range(nk):
         for g in range(grp):
             lo = (k * grp + g) * hd
@@ -250,9 +278,8 @@
     sum_attn = Scatter(part_a, dr_a, snd_a, lnk_a)
     sum_attn.run(lambda cols: mm(ctx[...], wo[:, cols]))
 
-    for sub in (0, 1):
-        gather_dy.forward(sub)
-    gather_dy.finish()
+    gather_dy.forward(0)
+    gather_dy.finish(0)
     weight_in[4].wait()
     put(dyf, dy_out)
     nb = f // 2
@@ -264,49 +291,53 @@
 
     lax.fori_loop(0, f // nb, down_back, 0)
 
-    gather_h2 = Gather(h2)
+    gather_h2 = Gather(h2, late)
+    small_in[4].wait()
+    small_in[5].wait()
     for sub in (0, 1):
         own = pl.ds(sub * half, half)
         attn_rows = sum_attn.rows_sum(sub).astype(BF16)
         mid_rows = (x_own[own, :].astype(F32) + attn_rows.astype(F32)).astype(BF16)
         mid[own, :] = mid_rows
         h2[block(me, sub), :] = norm_rows(mid_rows.astype(F32), g2_ref[...], b2_ref[...]).astype(BF16)
-        gather_h2.send(sub)
-    put(mid, mid_out)
+        for i in ((0,) if sub == 0 else range(1, 1 + CHUNKS)):
+            gather_h2.send(i)
     weight_in[5].wait()
-    for sub in (0, 1):
-        gather_h2.forward(sub)
-    gather_h2.finish()
-
-    def up(j, carry):
-        cols = pl.ds(pl.multiple_of(j * nb, nb), nb)
-        relu_up = jnp.maximum(mm(h2[...], w1[:, cols]).astype(BF16).astype(F32), 0.0)
-        act[:, cols] = (relu_up * relu_up).astype(BF16)
-        du[:, cols] = (tmat[:, cols] * (2.0 * relu_up)).astype(BF16)
-        return carry
-
-    lax.fori_loop(0, f // nb, up, 0)
+
+    def up(j, depth):
+        def step(i, carry):
+            cols = pl.ds(pl.multiple_of(i * nb, nb), nb)
+            piece = mm(h2[:, depth], w1[depth, cols])
+            if j == 0:
+                part_c[:, cols] = piece
+            elif j < CHUNKS - 1:
+                part_c[:, cols] += piece
+            else:
+                relu_up = jnp.maximum((part_c[:, cols] + piece).astype(BF16).astype(F32), 0.0)
+                act[:, cols] = (relu_up * relu_up).astype(BF16)
+                du[:, cols] = (tmat[:, cols] * (2.0 * relu_up)).astype(BF16)
+            return carry
+
+        lax.fori_loop(0, f // nb, step, 0)
+
+    gather_h2.feed(1, up)
     put(h2, h2_out)
     put(act, act_out)
     put(du, du_out)
     sum_dh2 = Scatter(part_b, dr_b, snd_b, lnk_b)
     sum_dh2.run(lambda cols: mm_bt(du[...], w1[cols, :]))
 
-    sum_mlp = Scatter(part_c, dr_c, ysend)
+    sum_mlp = Scatter(part_c, dr_c, snd_c, lnk_c)
     sum_mlp.run(lambda cols: mm(act[...], w2[:, cols]), drain=False)
-    sum_mlp.drain()
-    sum_mlp.kept()
-    ykeep[...] = part_c[block(me), :] + dr_c[1]
-    put(ysend, ysend_out)
-    put(ykeep, ykeep_out)
-
-    gather_dx1 = Gather(dx1)
+
+    gather_dx1 = Gather(dx1, late)
     for sub in (0, 1):
         own = pl.ds(sub * half, half)
         dh2_rows = sum_dh2.rows_sum(sub).astype(BF16).astype(F32)
         grad_rows, grad_gain, grad_bias = norm_rows_back(mid[own, :].astype(F32), dh2_rows, g2_ref[...])
         dx1[block(me, sub), :] = (dyf[block(me, sub), :].astype(F32) + grad_rows).astype(BF16)
-        gather_dx1.send(sub)
+        for i in ((0,) if sub == 0 else range(1, 1 + CHUNKS)):
+            gather_dx1.send(i)
         if sub == 0:
             lng[0:1, :] = grad_gain
             lng[1:2, :] = grad_bias
@@ -315,12 +346,12 @@
             lng[1:2, :] += grad_bias
     put(lng, lng_out)
     put(dx1.at[block(me)], dmid_out)
-    for sub in (0, 1):
-        gather_dx1.forward(sub)
-    gather_dx1.finish()
+    sum_mlp.drain()
+    dctx_sum = tmat.at[:, pl.ds(0, nqd)]
+    gather_dx1.feed(1, lambda j, cols: add(dctx_sum, j, mm_bt(dx1[:, cols], wo[:, cols])))
     put(dx1, dx1_out)
 
-    dctx = mm_bt(dx1[...], wo[...]).astype(BF16)
+    dctx = dctx_sum[...].astype(BF16)
     for k in range(nk):
         for g in range(grp):
             lo = (k * grp + g) * hd
@@ -347,11 +378,15 @@
     sum_dh1.kept()
     hkeep[...] = part_a[block(me), :] + dr_d[1]
     put(hkeep, hkeep_out)
+    for sub in (0, 1):
+        own = pl.ds(sub * half, half)
+        y_own[own, :] = (mid[own, :].astype(F32) + sum_mlp.rows_sum(sub).astype(BF16).astype(F32)).astype(BF16)
+    put(y_own, y_out)
 
     for gather in (gather_h1, gather_dy, gather_h2, gather_dx1):
         for kind in (0, 1, 2):
-            for sub in (0, 1):
-                gather.copy(kind, sub).wait_send()
+            for i in range(len(gather.pieces)):
+                gather.copy(kind, i).wait_send()
     for scatter in (sum_attn, sum_dh2, sum_mlp, sum_dh1):
         for i in range(CHUNKS):
             if scatter is not sum_attn:
@@ -380,25 +415,27 @@
     def vf(*shape):
         return pltpu.VMEM(shape, F32)
 
-    out_shape = [arr((seq, d), BF16)] * 4 + [arr((seq, f), BF16)] * 2 + [arr((seq, nqd), BF16), arr((seq, n_all), BF16)] + [arr((rows, d), BF16)] * 2 + [arr((rows, d), F32)] * 4 + [arr((2, d), F32)]
+    out_shape = [arr((seq, d), BF16)] * 4 + [arr((seq, f), BF16)] * 2 + [arr((seq, nqd), BF16), arr((seq, n_all), BF16)] + [arr((rows, d), BF16)] * 2 + [arr((rows, d), F32)] * 2 + [arr((2, d), F32)]
+    n_sems = CHUNKS + 1 + 2 * (CHUNKS + 1)
+    n_sems = 3 * n_sems + 4 * 2 * CHUNKS + 3 * (CHUNKS + 1)
     scratch = [
+        pltpu.VMEM((1, seq), jnp.int32), vf(1, hd), vf(1, d), vf(1, d), vf(1, d), vf(1, d),
         vm(d, n_all), vm(nqd, d), vm(d, f), vm(f, d),
         vm(seq, d), vm(seq, d), vm(seq, d), vm(seq, d),
-        vm(rows, d), vm(rows, d), vf(seq, f), vm(seq, f), vm(seq, f),
+        vm(rows, d), vm(rows, d), vm(rows, d), vf(seq, f), vm(seq, f), vm(seq, f),
         vm(nk, grp * seq, hd), vm(2, nk, seq, hd), vm(seq, nqd), vf(nk, grp * seq, seq),
         vf(seq, hd), vf(seq, hd), vm(nk, grp * seq, hd), vm(seq, n_all), vf(2, d),
         vf(seq, d), vf(seq, d), vf(seq, d),
         vf(2, rows, d), vf(2, rows, d), vf(2, rows, d), vf(2, rows, d),
         vf(rows, d), vf(rows, d), vf(rows, d), vf(rows, d),
         vf(rows, d), vf(rows, d), vf(rows, d), vf(rows, d),
-        pltpu.SemaphoreType.DMA((8,)), pltpu.SemaphoreType.DMA((15,)),
-        pltpu.SemaphoreType.DMA((4 * 6 + 4 * 2 * CHUNKS + 2 * (CHUNKS + 1),)),
-        pltpu.SemaphoreType.DMA((4 * 6 + 4 * 2 * CHUNKS + 2 * (CHUNKS + 1),)),
+        pltpu.SemaphoreType.DMA((14,)), pltpu.SemaphoreType.DMA((len(out_shape),)),
+        pltpu.SemaphoreType.DMA((n_sems,)), pltpu.SemaphoreType.DMA((n_sems,)),
     ]
     return pl.pallas_call(
         functools.partial(chain_kernel, dims),
         out_shape=out_shape,
-        in_specs=[ANY, ANY] + [VMEM] * 6 + [ANY] * 6,
+        in_specs=[ANY] * 14,
         out_specs=[ANY] * len(out_shape),
         scratch_shapes=scratch,
         compiler_params=pltpu.CompilerParams(collective_id=0, has_side_effects=True, vmem_limit_bytes=VMEM_LIMIT),
@@ -411,64 +448,87 @@
 
 
 def stream_grads(jobs, stage, sem):
-    base = 0
-    for tiles, width, compute, targets in jobs:
-        def copies(i, slot):
-            return [pltpu.make_async_copy(stage.at[slot, :, pl.ds(lo, n)], dst, sem.at[slot, c]) for c, (dst, lo, n) in enumerate(targets(i))]
-
-        def step(i, carry):
-            slot = lax.rem(i, SLOTS)
-
-            @pl.when(i >= SLOTS)
-            def _():
-                for copy in copies(i - SLOTS, slot):
+    def copies(targets, i, slot):
+        return [pltpu.make_async_copy(stage.at[slot, :, pl.ds(lo, n)], dst, sem.at[slot, c]) for c, (dst, lo, n) in enumerate(targets(i))]
+
+    done, pending = 0, []
+    for ready, tiles, width, compute, targets in jobs:
+        ready()
+
+        def fill(i, slot):
+            stage[slot, :, :width] = compute(i)
+            for copy in copies(targets, i, slot):
+                copy.start()
+
+        lead = min(SLOTS, tiles)
+        for i in range(lead):
+            slot = (done + i) % SLOTS
+            if len(pending) == SLOTS:
+                for copy in pending.pop(0):
                     copy.wait()
-
-            stage[slot, :, :width] = compute(i)
-            for copy in copies(i, slot):
-                copy.start()
+            fill(i, slot)
+            pending.append(copies(targets, i, slot))
+
+        def step(i, carry, base=done):
+            slot = lax.rem(base + i, SLOTS)
+            for copy in copies(targets, i - SLOTS, slot):
+                copy.wait()
+            fill(i, slot)
             return carry
 
-        lax.fori_loop(0, tiles, step, 0)
-        for i in range(max(tiles - SLOTS, 0), tiles):
-            for copy in copies(i, i % SLOTS):
-                copy.wait()
+        lax.fori_loop(lead, tiles, step, 0)
+        if tiles > SLOTS:
+            pending = [copies(targets, i, (done + i) % SLOTS) for i in range(tiles - SLOTS, tiles)]
+        done += tiles
+    for group in pending:
+        for copy in group:
+            copy.wait()
 
 
 def grads_first_kernel(act_hbm, dy_hbm, ctx_hbm, dx1_hbm, dw2, dwo, act, dyf, ctx, dx1, stage, in_sem, sem):
     loads = [pltpu.make_async_copy(s, t, in_sem.at[i]) for i, (s, t) in enumerate(((act_hbm, act), (dy_hbm, dyf), (ctx_hbm, ctx), (dx1_hbm, dx1)))]
     for copy in loads:
         copy.start()
-    loads[0].wait()
-    loads[1].wait()
+
+    def ready(*which):
+        return lambda: [loads[i].wait() for i in which]
 
     def tile(i):
         return pl.ds(pl.multiple_of(i * TILE, TILE), TILE)
 
     d = dyf.shape[1]
-    stream_grads([(act.shape[1] // TILE, d, lambda i: mm_at(act[:, tile(i)], dyf[...]), lambda i: [(dw2.at[tile(i)], 0, d)])], stage, sem)
-    loads[2].wait()
-    loads[3].wait()
-    stream_grads([(ctx.shape[1] // TILE, d, lambda i: mm_at(ctx[:, tile(i)], dx1[...]), lambda i: [(dwo.at[tile(i)], 0, d)])], stage, sem)
-
-
-def grads_second_kernel(dims, h2_hbm, du_hbm, h1_hbm, dqkv_hbm, dw1, dwq, dwk, dwv, h2, du, h1, dqkv, stage, in_sem, sem):
+    stream_grads([
+        (ready(0, 1), act.shape[1] // TILE, d, lambda i: mm_at(act[:, tile(i)], dyf[...]), lambda i: [(dw2.at[tile(i)], 0, d)]),
+        (ready(2, 3), ctx.shape[1] // TILE, d, lambda i: mm_at(ctx[:, tile(i)], dx1[...]), lambda i: [(dwo.at[tile(i)], 0, d)]),
+    ], stage, sem)
+
+
+def grads_second_kernel(dims, order, y_hbm, h2_hbm, du_hbm, h1_hbm, dqkv_hbm, y_out, dw1, dwq, dwk, dwv, y, h2, du, h1, dqkv, stage, in_sem, sem):
     seq, d, hd, nq, nk, f, rows = dims
-    loads = [pltpu.make_async_copy(s, t, in_sem.at[i]) for i, (s, t) in enumerate(((h2_hbm, h2), (du_hbm, du), (h1_hbm, h1), (dqkv_hbm, dqkv)))]
+    loads = [pltpu.make_async_copy(s, t, in_sem.at[i]) for i, (s, t) in enumerate(((h2_hbm, h2), (du_hbm, du), (h1_hbm, h1), (dqkv_hbm, dqkv), (y_hbm, y)))]
     for copy in loads:
         copy.start()
-    loads[0].wait()
-    loads[1].wait()
+
+    def ready(*which):
+        return lambda: [loads[i].wait() for i in which]
 
     def tile(i):
         return pl.ds(pl.multiple_of(i * TILE, TILE), TILE)
 
     nqd, nkd = nq * hd, nk * hd
-    stream_grads([(d // TILE, f, lambda i: mm_at(h2[:, tile(i)], du[...]), lambda i: [(dw1.at[tile(i)], 0, f)])], stage, sem)
-    loads[2].wait()
-    loads[3].wait()
-    stream_grads([(d // TILE, nqd + 2 * nkd, lambda i: mm_at(h1[:, tile(i)], dqkv[...]),
-                   lambda i: [(dwq.at[tile(i)], 0, nqd), (dwk.at[tile(i)], nqd, nkd), (dwv.at[tile(i)], nqd + nkd, nkd)])], stage, sem)
+    y_copy = pltpu.make_async_copy(y, y_out, in_sem.at[5])
+
+    def ready_rest():
+        for i in (2, 3, 4):
+            loads[i].wait()
+        y_copy.start()
+
+    stream_grads([
+        (ready(0, 1), d // TILE, f, lambda i: mm_at(h2[:, tile(i)], du[...]), lambda i: [(dw1.at[tile(i)], 0, f)]),
+        (ready_rest, d // TILE, nqd + 2 * nkd, lambda i: mm_at(h1[:, tile(i)], dqkv[...]),
+         lambda i: [(dwq.at[tile(i)], 0, nqd), (dwk.at[tile(i)], nqd, nkd), (dwv.at[tile(i)], nqd + nkd, nkd)]),
+    ], stage, sem)
+    y_copy.wait()
 
 
 def cost(flops, nbytes):
@@ -484,29 +544,29 @@
         in_specs=[ANY] * 4, out_specs=[ANY] * 2,
         scratch_shapes=[pltpu.VMEM((seq, f), BF16), pltpu.VMEM((seq, d), BF16), pltpu.VMEM((seq, nqd), BF16), pltpu.VMEM((seq, d), BF16),
                         pltpu.VMEM((SLOTS, TILE, d), F32), pltpu.SemaphoreType.DMA((4,)), pltpu.SemaphoreType.DMA((SLOTS, 3))],
-        compiler_params=pltpu.CompilerParams(vmem_limit_bytes=40 << 20),
+        compiler_params=pltpu.CompilerParams(vmem_limit_bytes=VMEM_LIMIT),
         cost_estimate=cost(2 * seq * d * (f + nqd), 4 * d * (f + nqd)),
         name="grads_first",
     )(act, dyf, ctx, dx1)
 
 
-def grads_second(dims, h2, du, h1, dqkv):
+def grads_second(dims, order, y, h2, du, h1, dqkv):
     seq, d, hd, nq, nk, f, rows = dims
     nqd, nkd = nq * hd, nk * hd
     n_all = nqd + 2 * nkd
     return pl.pallas_call(
         functools.partial(grads_second_kernel, dims),
-        out_shape=[jax.ShapeDtypeStruct((d, f), F32), jax.ShapeDtypeStruct((d, nqd), F32), jax.ShapeDtypeStruct((d, nkd), F32), jax.ShapeDtypeStruct((d, nkd), F32)],
-        in_specs=[ANY] * 4, out_specs=[ANY] * 4,
-        scratch_shapes=[pltpu.VMEM((seq, d), BF16), pltpu.VMEM((seq, f), BF16), pltpu.VMEM((seq, d), BF16), pltpu.VMEM((seq, n_all), BF16),
-                        pltpu.VMEM((SLOTS, TILE, f), F32), pltpu.SemaphoreType.DMA((4,)), pltpu.SemaphoreType.DMA((SLOTS, 3))],
-        compiler_params=pltpu.CompilerParams(vmem_limit_bytes=40 << 20),
+        out_shape=[jax.ShapeDtypeStruct((rows, d), BF16), jax.ShapeDtypeStruct((d, f), F32), jax.ShapeDtypeStruct((d, nqd), F32), jax.ShapeDtypeStruct((d, nkd), F32), jax.ShapeDtypeStruct((d, nkd), F32)],
+        in_specs=[ANY] * 6, out_specs=[ANY] * 5,
+        scratch_shapes=[pltpu.VMEM((rows, d), BF16), pltpu.VMEM((seq, d), BF16), pltpu.VMEM((seq, f), BF16), pltpu.VMEM((seq, d), BF16), pltpu.VMEM((seq, n_all), BF16),
+                        pltpu.VMEM((SLOTS, TILE, f), F32), pltpu.SemaphoreType.DMA((6,)), pltpu.SemaphoreType.DMA((SLOTS, 3))],
+        compiler_params=pltpu.CompilerParams(vmem_limit_bytes=VMEM_LIMIT),
         cost_estimate=cost(2 * seq * d * (f + n_all), 4 * d * (f + n_all)),
         name="grads_second",
-    )(h2, du, h1, dqkv)
-
-
-def last_norm_kernel(hkeep, hrecv, x, dmid, g1, lng2, dx_out, lng_out):
+    )(order, y, h2, du, h1, dqkv)
+
+
+def last_norm_kernel(order, hkeep, hrecv, x, dmid, g1, lng2, dx_out, lng_out):
     dh1 = (hkeep[...] + hrecv[...]).astype(BF16).astype(F32)
     grad_rows, grad_gain, grad_bias = norm_rows_back(x[...].astype(F32), dh1, g1[...])
     dx_out[...] = (dmid[...].astype(F32) + grad_rows).astype(BF16)
@@ -515,15 +575,15 @@
     lng_out[2:4, :] = lng2[...]
 
 
-def last_norm(hkeep, hrecv, x, dmid, g1, lng2):
+def last_norm(order, hkeep, hrecv, x, dmid, g1, lng2):
     rows, d = x.shape
     return pl.pallas_call(
         last_norm_kernel,
         out_shape=[jax.ShapeDtypeStruct((rows, d), BF16), jax.ShapeDtypeStruct((4, d), F32)],
-        in_specs=[VMEM] * 6, out_specs=[VMEM] * 2,
+        in_specs=[ANY] + [VMEM] * 6, out_specs=[VMEM] * 2,
         cost_estimate=cost(rows * d * 20, rows * d * 16),
         name="last_norm",
-    )(hkeep, hrecv, x, dmid, g1, lng2)
+    )(order, hkeep, hrecv, x, dmid, g1, lng2)
 
 
 def layer_step(x, dy, positions, g1, b1, g2, b2, wq, wk, wv, wo, w1, w2, head_dim, n_tp):
@@ -536,19 +596,18 @@
     freq[0, :2 * rot] = np.tile(ROPE_BASE ** (-np.arange(rot) / rot), 2)
     x2, dy2 = x.reshape(rows, d), dy.reshape(rows, d)
     g1, b1, g2, b2 = (v.reshape(1, d) for v in (g1, b1, g2, b2))
-    (h1, h2, dyf, dx1, act, du, ctx, dqkv, mid, dmid, ysend, ykeep, hsend, hkeep, lng2) = chain(
+    (h1, h2, dyf, dx1, act, du, ctx, dqkv, y, dmid, hsend, hkeep, lng2) = chain(
         dims, x2, dy2, positions.reshape(1, seq), jnp.asarray(freq), g1, b1, g2, b2, wq, wk, wv, wo, w1, w2)
+
     def swap(v, bit):
         return lax.ppermute(v, 'tp', [(i, i ^ bit) for i in range(n_tp)])
 
     hrecv = swap(hsend, 2)
-    yrecv = swap(ysend, 2)
     dw2, dwo = grads_first(dims, act, dyf, ctx, dx1)
-    dx, lng = last_norm(hkeep, hrecv, x2, dmid, g1, lng2)
+    dx, lng = last_norm(dwo, hkeep, hrecv, x2, dmid, g1, lng2)
     others = [swap(lng, bit) for bit in (1, 2, 3)]
-    dw1, dwq, dwk, dwv = grads_second(dims, h2, du, h1, dqkv)
+    y, dw1, dwq, dwk, dwv = grads_second(dims, lng, y, h2, du, h1, dqkv)
     total = (lng + others[0]) + (others[1] + others[2])
-    y = (mid.astype(F32) + (ykeep + yrecv).astype(BF16).astype(F32)).astype(BF16)
     return (y.reshape(x.shape), dx.reshape(x.shape), total[0], total[1], total[2], total[3], dwq, dwk, dwv, dwo, dw1, dw2)
 
 

time: 111 us -> 96.7 us (0.87)
  local copies, waits for them, and re-layouts: 9.9 us -> 0.64 us
  waiting for transfers between devices: 2.11 us -> 0.01 us
  starting transfers between devices: 4.19 us -> 3.01 us
    unnamed x22 -> x0, local copies, waits for them, and re-layouts: 9.26 us -> none
    ppermute x5 -> x4, waiting for transfers between devices: 2.11 us -> 0.01 us  [swap(): return lax.ppermute(v, 'tp', [(i, i ^ bit) for i in range(n_tp)])]
    ppermute x5 -> x4, starting transfers between devices: 4.19 us -> 3.01 us  [swap(): return lax.ppermute(v, 'tp', [(i, i ^ bit) for i in range(n_tp)])]
  transfers between devices with their start and end apart: 5 -> 4, of which waited for: 2 -> 0; matrix products, arithmetic and copies ran while one was open for 1% -> 0% of each run, Pallas kernels for 28% -> 29%
where the time goes in v2:
time: 96.7 us; the launch traced here: 96.5 us
  Pallas kernels  91.2 us (94%)
  starting transfers between devices  3.01 us (3%)
    pallas_call x1, Pallas kernels, chain(): pl.pallas_call(functools.partial(chain_kernel, dims), out_shape=out_shape...  60.5 us
    pallas_call x1, Pallas kernels, grads_second(): pl.pallas_call(functools.partial(grads_second_kernel, dims), out_shape=[j...  15 us
    pallas_call x1, Pallas kernels, grads_first(): pl.pallas_call(grads_first_kernel, out_shape=[jax.ShapeDtypeStruct((f, d)...  13.3 us
    ppermute x4, starting transfers between devices, swap(): return lax.ppermute(v, 'tp', [(i, i ^ bit) for i in range(n_tp)])  3.01 us
    pallas_call x1, Pallas kernels, last_norm(): pl.pallas_call(last_norm_kernel, out_shape=[jax.ShapeDtypeStruct((rows, d...  2.46 us
  transfers between devices with their start and end apart: 4, of which 0 were waited for; matrix products, arithmetic and copies ran while one was open for 0% of the time, Pallas kernels for 29%

profile of v2, /device:TPU:0, one launch (start us, length us, event | category | flops | bytes accessed | tf_op | source)
XLA Modules:
  0.0 96.5 jit_solution(5550305510968776454)
XLA Ops:
  0.6 60.5 %chain.1 = (bf16[128,3072]{1,0:T(8,128)(2,1)}, bf16[128,3072]{1,0:T(8,128)(2,1)}, bf16[128,3072]{1,0:T(8,128)(2,1)}, bf16[128,3072]{1,0:T(8,128)(2,1)}, bf16[128...) custom-call(bf16[32,3072]{1,0:T(8,128)(2,1)} %bitcast.13, ...), custom_call_target="tpu_custom_call" | custom-call | tf_op jit(solution)/shard_map/chain/pallas_call | solution.py:435
  61.1 0.9 collective-permute-start
  62.0 13.3 %grads_first.1 = (f32[2048,3072]{1,0:T(8,128)}, f32[768,3072]{1,0:T(8,128)}) custom-call(bf16[128,2048]{1,0:T(8,128)(2,1)} %get-tuple-element.34.act_hbm, bf16[128,3072]{1,0:T(8,128)(2,1)} %get-tuple-element.35.dy_hbm, bf16[128,768]{1,0:T(8,128)(2,1)} %get-tuple-element.36.ctx_hbm, bf16[128,3072]{1,0:T(8,128)(2,1)} %get-tuple-element.37.dx1_hbm), custom_call_target="tpu_custom_call" | custom-call | flops 2214592512 | bytes 34603008 | tf_op jit(solution)/shard_map/grads_first/pallas_call | solution.py:541
  75.3 0.0 collective-permute-done.hrecv
  75.4 2.5 %last_norm.1 = (bf16[32,3072]{1,0:T(8,128)(2,1)}, f32[4,3072]{1,0:T(4,128)}) custom-call(f32[768,3072]{1,0:T(8,128)} %get-tuple-element.31.order, f32[32,3072]{1,0:T(8,128)} %get-tuple-element.39.hkeep, f32[32,3072]{1,0:T(8,128)} %collective-permute-done.hrecv, bf16[32,3072]{1,0:T(8,128)(2,1)} %bitcast.14, bf16[32,3072]{1,0:T(8,128)(2,1)} %get-tuple-element.41.dmid, ...), custom_call_target="tpu_custom_call" | custom-call | flops 1966080 | bytes 1572864 | tf_op jit(solution)/shard_map/last_norm/pallas_call | solution.py:580
  77.8 1.2 %collective-permute-start.2 = (f32[4,3072]{1,0:T(4,128)}, f32[4,3072]{1,0:T(4,128)}, u32[]{:S(2)}, u32[]{:S(2)}) collective-permute-start(f32[4,3072]{1,0:T(4,128)} %get-tuple-element.43.order), channel_id=1, source_target_pairs={{0,2},{1,3},{2,0},{3,1},{4,6},{5,7},{6,4},{7,5}} | collective-permute-start | bytes 147464 | tf_op jit(solution)/shard_map/ppermute | solution.py:603
  79.0 0.0 collective-permute-start.3
  79.0 1.0 collective-permute-start.1
  80.0 15.0 %grads_second.1 = (bf16[32,3072]{1,0:T(8,128)(2,1)}, f32[3072,2048]{1,0:T(8,128)}, f32[3072,768]{1,0:T(8,128)}, f32[3072,256]{1,0:T(8,128)}, f32[3072,256]{1,0:T(8,128)}) custom-call(f32[4,3072]{1,0:T(4,128)} %get-tuple-element.43.order, bf16[32,3072]{1,0:T(8,128)(2,1)} %get-tuple-element.44.y_hbm, bf16[128,3072]{1,0:T(8,128)(2,1)} %get-tuple-element.45.h2_hbm, ...), custom_call_target="tpu_custom_call" | custom-call | flops 2617245696 | bytes 40894464 | tf_op jit(solution)/shard_map/grads_second/pallas_call | solution.py:557
  94.9 0.0 collective-permute-done.2
  94.9 0.0 collective-permute-done.3
  95.0 0.0 collective-permute-done.1
  95.0 0.9 add_add_fusion
  95.9 0.6 fusion
Async XLA Ops:
  61.1 14.2 %collective-permute-start = (f32[32,3072]{1,0:T(8,128)}, f32[32,3072]{1,0:T(8,128)}, u32[]{:S(2)}, u32[]{:S(2)}) collective-permute-start(f32[32,3072]{1,0:T(8,128)} %get-tuple-element.40), channel_id=1, source_target_pairs={{0,2},{1,3},{2,0},{3,1},{4,6},{5,7},{6,4},{7,5}} | collective-permute-start | bytes 1179656 | tf_op jit(solution)/shard_map/ppermute | solution.py:603
  77.8 17.1 %collective-permute-start.2 = (f32[4,3072]{1,0:T(4,128)}, f32[4,3072]{1,0:T(4,128)}, u32[]{:S(2)}, u32[]{:S(2)}) collective-permute-start(f32[4,3072]{1,0:T(4,128)} %get-tuple-element.43.order), channel_id=1, source_target_pairs={{0,2},{1,3},{2,0},{3,1},{4,6},{5,7},{6,4},{7,5}} | collective-permute-start | bytes 147464 | tf_op jit(solution)/shard_map/ppermute | solution.py:603
  79.0 16.0 %collective-permute-start.3 = (f32[4,3072]{1,0:T(4,128)}, f32[4,3072]{1,0:T(4,128)}, u32[]{:S(2)}, u32[]{:S(2)}) collective-permute-start(f32[4,3072]{1,0:T(4,128)} %get-tuple-element.43.order), channel_id=1, source_target_pairs={{0,3},{1,2},{2,1},{3,0},{4,7},{5,6},{6,5},{7,4}} | collective-permute-start | bytes 147464 | tf_op jit(solution)/shard_map/ppermute | solution.py:603
  79.0 16.0 %collective-permute-start.1 = (f32[4,3072]{1,0:T(4,128)}, f32[4,3072]{1,0:T(4,128)}, u32[]{:S(2)}, u32[]{:S(2)}) collective-permute-start(f32[4,3072]{1,0:T(4,128)} %get-tuple-element.43.order), channel_id=1, source_target_pairs={{0,1},{1,0},{2,3},{3,2},{4,5},{5,4},{6,7},{7,6}} | collective-permute-start | bytes 147464 | tf_op jit(solution)/shard_map/ppermute | solution.py:603

commit v3 on v2

--- a/solution.py
+++ b/solution.py
@@ -16,7 +16,6 @@
 ANY = pl.BlockSpec(memory_space=pl.ANY)
 VMEM = pl.BlockSpec(memory_space=pltpu.VMEM)
 VMEM_LIMIT = 67_043_328
-CHUNKS = 4
 
 
 def mm(a, b):
@@ -61,15 +60,14 @@
 
 
 def chain_kernel(dims, x_hbm, dy_hbm, pos_hbm, freq_hbm, g1_hbm, b1_hbm, g2_hbm, b2_hbm, wq_hbm, wk_hbm, wv_hbm, wo_hbm, w1_hbm, w2_hbm,
-                 h1_out, h2_out, dy_out, dx1_out, act_out, du_out, ctx_out, dqkv_out, y_out, dmid_out, hsend_out, hkeep_out, lng_out,
+                 h1_out, h2_out, dy_out, dx1_out, act_out, du_out, ctx_out, dqkv_out, y_out, mid_out, dmid_out, send_out, hkeep_out, ykeep_out, lng_out,
                  pos_ref, freq_ref, g1_ref, b1_ref, g2_ref, b2_ref,
                  wqkv, wo, w1, w2, h1, h2, dyf, dx1, x_own, mid, y_own, tmat, act, du, qs, kv, ctx, prob, cosb, sinb, gcs, dqkv, lng,
-                 part_a, part_b, part_c, dr_a, dr_b, dr_c, dr_d, snd_a, snd_b, snd_c, lnk_a, lnk_b, lnk_c, hsend, hkeep,
+                 part_a, part_b, part_c, dr_a, dr_b, dr_c, dr_d, snd_a, snd_b, snd_c, lnk_a, lnk_b, lnk_c, send, hkeep, ykeep,
                  local_sem, out_sem, send_sem, recv_sem):
     seq, d, hd, nq, nk, f, rows = dims
     grp = nq // nk
     half = rows // 2
-    cw = d // CHUNKS
     me = lax.axis_index("tp")
     part, peer, diag = me ^ 1, me ^ 2, me ^ 3
     sems = Sems()
@@ -152,17 +150,18 @@
                 use(i - first, pl.ds(self.pieces[i][2], self.pieces[i][3]))
 
     class Scatter:
-        def __init__(self, partial, from_part, summed, from_peer=None):
+        def __init__(self, chunks, partial, from_part, summed, from_peer=None, link_rows=0):
+            self.chunks, self.cw, self.link_rows = chunks, d // chunks, link_rows
             self.partial, self.from_part, self.summed, self.from_peer = partial, from_part, summed, from_peer
-            self.base = sems.take(2 * CHUNKS)
-            self.link = sems.take(CHUNKS + 1) if from_peer is not None else None
+            self.base = sems.take(2 * chunks)
+            self.link = sems.take(chunks + 1) if link_rows else None
 
         def cols(self, i):
-            return pl.ds(pl.multiple_of(i * cw, cw), cw)
+            return pl.ds(pl.multiple_of(i * self.cw, self.cw), self.cw)
 
         def pair(self, i, kind):
             owner = (diag, part)[kind]
-            return remote(self.partial.at[block(owner), self.cols(i)], self.from_part.at[kind, :, self.cols(i)], self.base + CHUNKS * kind + i, part)
+            return remote(self.partial.at[block(owner), self.cols(i)], self.from_part.at[kind, :, self.cols(i)], self.base + self.chunks * kind + i, part)
 
         def first(self, i):
             top = pl.ds(0, half)
@@ -170,13 +169,13 @@
 
         def second(self):
             low = pl.ds(half, half)
-            return remote(self.summed.at[low], self.from_peer.at[low], self.link + CHUNKS, peer)
+            return remote(self.summed.at[low], self.from_peer.at[low], self.link + self.chunks, peer)
 
         def chip_sum(self, i):
             self.pair(i, 0).wait_recv()
             cols = self.cols(i)
             self.summed[:, cols] = self.partial[block(peer), cols] + self.from_part[0, :, cols]
-            if self.from_peer is not None:
+            if self.link_rows:
                 self.first(i).start()
 
         def run(self, chunk, drain=True):
@@ -190,40 +189,52 @@
                         self.chip_sum(i - 1)
                 return carry
 
-            lax.fori_loop(0, CHUNKS, step, 0)
+            lax.fori_loop(0, self.chunks, step, 0)
             if drain:
-                self.chip_sum(CHUNKS - 1)
-                if self.from_peer is not None:
-                    self.second().start()
-
-        def drain(self):
-            for i in range(CHUNKS):
+                self.drain(self.chunks - 1)
+
+        def drain(self, start=0):
+            for i in range(start, self.chunks):
                 self.chip_sum(i)
-            self.second().start()
+            if self.link_rows == rows:
+                self.second().start()
 
         def kept(self):
-            for i in range(CHUNKS):
+            for i in range(self.chunks):
                 self.pair(i, 1).wait_recv()
+
+        def kept_rows(self, sub):
+            return self.partial[block(me, sub), :] + self.from_part[1, pl.ds(sub * half, half), :]
 
         def rows_sum(self, sub):
             if sub == 0:
-                self.kept()
-                for i in range(CHUNKS):
+                for i in range(self.chunks):
                     self.first(i).wait_recv()
             else:
                 self.second().wait_recv()
-            part_rows = pl.ds(sub * half, half)
-            return (self.partial[block(me, sub), :] + self.from_part[1, part_rows, :]) + self.from_peer[part_rows, :]
+            return self.kept_rows(sub) + self.from_peer[pl.ds(sub * half, half), :]
+
+        def pair_sent(self):
+            for i in range(self.chunks):
+                self.pair(i, 0).wait_send()
+                self.pair(i, 1).wait_send()
+
+        def link_sent(self):
+            if self.link_rows:
+                for i in range(self.chunks):
+                    self.first(i).wait_send()
+            if self.link_rows == rows:
+                self.second().wait_send()
 
     x_in.wait()
     small_in[0].wait()
     small_in[1].wait()
     h1[block(me), :] = norm_rows(x_own[...].astype(F32), g1_ref[...], b1_ref[...]).astype(BF16)
     pl.semaphore_wait(barrier, 2)
-    wide = [(0, rows, i * cw, cw) for i in range(CHUNKS)]
-    late = [(0, half, 0, d)] + [(half, half, i * cw, cw) for i in range(CHUNKS)]
-    gather_h1, gather_dy = Gather(h1, wide), Gather(dyf, [(0, rows, 0, d)])
-    for i in range(CHUNKS):
+    gather_h1 = Gather(h1, [(0, rows) + cut for cut in cuts(d, (1, 1, 1, 1))])
+    gather_dy = Gather(dyf, [(0, rows, 0, d)])
+    late = [(0, half, 0, d)] + [(half, half) + cut for cut in cuts(d, (1, 1, 1, 1))]
+    for i in range(len(gather_h1.pieces)):
         gather_h1.send(i)
     dy_in.wait()
     gather_dy.send(0)
@@ -275,7 +286,7 @@
             ctx[:, lo:lo + hd] = head_ctx[g * seq:(g + 1) * seq, :]
     put(ctx, ctx_out)
     weight_in[3].wait()
-    sum_attn = Scatter(part_a, dr_a, snd_a, lnk_a)
+    sum_attn = Scatter(4, part_a, dr_a, snd_a, lnk_a, rows)
     sum_attn.run(lambda cols: mm(ctx[...], wo[:, cols]))
 
     gather_dy.forward(0)
@@ -295,12 +306,14 @@
     small_in[4].wait()
     small_in[5].wait()
     for sub in (0, 1):
+        if sub == 0:
+            sum_attn.kept()
         own = pl.ds(sub * half, half)
         attn_rows = sum_attn.rows_sum(sub).astype(BF16)
         mid_rows = (x_own[own, :].astype(F32) + attn_rows.astype(F32)).astype(BF16)
         mid[own, :] = mid_rows
         h2[block(me, sub), :] = norm_rows(mid_rows.astype(F32), g2_ref[...], b2_ref[...]).astype(BF16)
-        for i in ((0,) if sub == 0 else range(1, 1 + CHUNKS)):
+        for i in ((0,) if sub == 0 else range(1, len(late))):
             gather_h2.send(i)
     weight_in[5].wait()
 
@@ -310,7 +323,7 @@
             piece = mm(h2[:, depth], w1[depth, cols])
             if j == 0:
                 part_c[:, cols] = piece
-            elif j < CHUNKS - 1:
+            elif j < len(late) - 2:
                 part_c[:, cols] += piece
             else:
                 relu_up = jnp.maximum((part_c[:, cols] + piece).astype(BF16).astype(F32), 0.0)
@@ -324,19 +337,21 @@
     put(h2, h2_out)
     put(act, act_out)
     put(du, du_out)
-    sum_dh2 = Scatter(part_b, dr_b, snd_b, lnk_b)
+    sum_dh2 = Scatter(4, part_b, dr_b, snd_b, lnk_b, rows)
     sum_dh2.run(lambda cols: mm_bt(du[...], w1[cols, :]))
 
-    sum_mlp = Scatter(part_c, dr_c, snd_c, lnk_c)
+    sum_mlp = Scatter(4, part_c, dr_c, snd_c, lnk_c, half)
     sum_mlp.run(lambda cols: mm(act[...], w2[:, cols]), drain=False)
 
     gather_dx1 = Gather(dx1, late)
     for sub in (0, 1):
+        if sub == 0:
+            sum_dh2.kept()
         own = pl.ds(sub * half, half)
         dh2_rows = sum_dh2.rows_sum(sub).astype(BF16).astype(F32)
         grad_rows, grad_gain, grad_bias = norm_rows_back(mid[own, :].astype(F32), dh2_rows, g2_ref[...])
         dx1[block(me, sub), :] = (dyf[block(me, sub), :].astype(F32) + grad_rows).astype(BF16)
-        for i in ((0,) if sub == 0 else range(1, 1 + CHUNKS)):
+        for i in ((0,) if sub == 0 else range(1, len(late))):
             gather_dx1.send(i)
         if sub == 0:
             lng[0:1, :] = grad_gain
@@ -347,6 +362,12 @@
     put(lng, lng_out)
     put(dx1.at[block(me)], dmid_out)
     sum_mlp.drain()
+    low = pl.ds(half, half)
+    send[pl.ds(rows, half), :] = snd_c[low, :]
+    sum_mlp.kept()
+    ykeep[...] = sum_mlp.kept_rows(1)
+    put(ykeep, ykeep_out)
+    put(mid.at[low], mid_out)
     dctx_sum = tmat.at[:, pl.ds(0, nqd)]
     gather_dx1.feed(1, lambda j, cols: add(dctx_sum, j, mm_bt(dx1[:, cols], wo[:, cols])))
     put(dx1, dx1_out)
@@ -369,35 +390,36 @@
         lo = nqd + nkd + k * hd
         dqkv[:, lo:lo + hd] = grad_v
     put(dqkv, dqkv_out)
-    sum_dh1 = Scatter(part_a, dr_d, hsend)
-    for i in range(CHUNKS):
-        sum_attn.pair(i, 0).wait_send()
-        sum_attn.pair(i, 1).wait_send()
+    top = pl.ds(0, half)
+    y_own[...] = (mid[top, :].astype(F32) + sum_mlp.rows_sum(0).astype(BF16).astype(F32)).astype(BF16)
+    put(y_own, y_out)
+    sum_dh1 = Scatter(3, part_a, dr_d, send.at[pl.ds(0, rows)])
+    sum_attn.pair_sent()
     sum_dh1.run(lambda cols: mm_bt(dqkv[...], wqkv[cols, :]))
-    put(hsend, hsend_out)
+    put(send, send_out)
     sum_dh1.kept()
-    hkeep[...] = part_a[block(me), :] + dr_d[1]
+    for sub in (0, 1):
+        hkeep[pl.ds(sub * half, half), :] = sum_dh1.kept_rows(sub)
     put(hkeep, hkeep_out)
-    for sub in (0, 1):
-        own = pl.ds(sub * half, half)
-        y_own[own, :] = (mid[own, :].astype(F32) + sum_mlp.rows_sum(sub).astype(BF16).astype(F32)).astype(BF16)
-    put(y_own, y_out)
 
     for gather in (gather_h1, gather_dy, gather_h2, gather_dx1):
         for kind in (0, 1, 2):
             for i in range(len(gather.pieces)):
                 gather.copy(kind, i).wait_send()
-    for scatter in (sum_attn, sum_dh2, sum_mlp, sum_dh1):
-        for i in range(CHUNKS):
-            if scatter is not sum_attn:
-                scatter.pair(i, 0).wait_send()
-                scatter.pair(i, 1).wait_send()
-            if scatter.from_peer is not None:
-                scatter.first(i).wait_send()
-        if scatter.from_peer is not None:
-            scatter.second().wait_send()
+    for scatter in (sum_dh2, sum_mlp, sum_dh1):
+        scatter.pair_sent()
+    for scatter in (sum_attn, sum_dh2, sum_mlp):
+        scatter.link_sent()
     for copy in outs:
         copy.wait()
+
+
+def cuts(d, parts):
+    unit, first, out = d // sum(parts), 0, []
+    for n in parts:
+        out.append((first, n * unit))
+        first += n * unit
+    return out
 
 
 def chain(dims, x, dy, pos, freq, g1, b1, g2, b2, wq, wk, wv, wo, w1, w2):
@@ -405,6 +427,7 @@
     grp = nq // nk
     nqd, nkd = nq * hd, nk * hd
     n_all = nqd + 2 * nkd
+    half = rows // 2
 
     def arr(shape, dtype):
         return jax.ShapeDtypeStruct(shape, dtype)
@@ -415,20 +438,19 @@
     def vf(*shape):
         return pltpu.VMEM(shape, F32)
 
-    out_shape = [arr((seq, d), BF16)] * 4 + [arr((seq, f), BF16)] * 2 + [arr((seq, nqd), BF16), arr((seq, n_all), BF16)] + [arr((rows, d), BF16)] * 2 + [arr((rows, d), F32)] * 2 + [arr((2, d), F32)]
-    n_sems = CHUNKS + 1 + 2 * (CHUNKS + 1)
-    n_sems = 3 * n_sems + 4 * 2 * CHUNKS + 3 * (CHUNKS + 1)
+    out_shape = [arr((seq, d), BF16)] * 4 + [arr((seq, f), BF16)] * 2 + [arr((seq, nqd), BF16), arr((seq, n_all), BF16)] + [arr((half, d), BF16)] * 2 + [arr((rows, d), BF16), arr((rows + half, d), F32), arr((rows, d), F32), arr((half, d), F32), arr((2, d), F32)]
+    n_sems = 3 * (4 + 1 + 5 + 5) + 2 * (4 + 4 + 4 + 3) + (5 + 5 + 5)
     scratch = [
         pltpu.VMEM((1, seq), jnp.int32), vf(1, hd), vf(1, d), vf(1, d), vf(1, d), vf(1, d),
         vm(d, n_all), vm(nqd, d), vm(d, f), vm(f, d),
         vm(seq, d), vm(seq, d), vm(seq, d), vm(seq, d),
-        vm(rows, d), vm(rows, d), vm(rows, d), vf(seq, f), vm(seq, f), vm(seq, f),
+        vm(rows, d), vm(rows, d), vm(half, d), vf(seq, f), vm(seq, f), vm(seq, f),
         vm(nk, grp * seq, hd), vm(2, nk, seq, hd), vm(seq, nqd), vf(nk, grp * seq, seq),
         vf(seq, hd), vf(seq, hd), vm(nk, grp * seq, hd), vm(seq, n_all), vf(2, d),
         vf(seq, d), vf(seq, d), vf(seq, d),
         vf(2, rows, d), vf(2, rows, d), vf(2, rows, d), vf(2, rows, d),
-        vf(rows, d), vf(rows, d), vf(rows, d), vf(rows, d),
-        vf(rows, d), vf(rows, d), vf(rows, d), vf(rows, d),
+        vf(rows, d), vf(rows, d), vf(rows, d), vf(rows, d), vf(rows, d), vf(half, d),
+        vf(rows + half, d), vf(rows, d), vf(half, d),
         pltpu.SemaphoreType.DMA((14,)), pltpu.SemaphoreType.DMA((len(out_shape),)),
         pltpu.SemaphoreType.DMA((n_sems,)), pltpu.SemaphoreType.DMA((n_sems,)),
     ]
@@ -448,16 +470,17 @@
 
 
 def stream_grads(jobs, stage, sem):
-    def copies(targets, i, slot):
-        return [pltpu.make_async_copy(stage.at[slot, :, pl.ds(lo, n)], dst, sem.at[slot, c]) for c, (dst, lo, n) in enumerate(targets(i))]
+    def copies(job, i, slot):
+        return [pltpu.make_async_copy(stage.at[slot, pl.ds(0, job[1]), pl.ds(lo, n)], dst, sem.at[slot, c]) for c, (dst, lo, n) in enumerate(job[5](i))]
 
     done, pending = 0, []
-    for ready, tiles, width, compute, targets in jobs:
+    for job in jobs:
+        ready, tile, tiles, width, compute, targets = job
         ready()
 
         def fill(i, slot):
-            stage[slot, :, :width] = compute(i)
-            for copy in copies(targets, i, slot):
+            stage[slot, :tile, :width] = compute(i)
+            for copy in copies(job, i, slot):
                 copy.start()
 
         lead = min(SLOTS, tiles)
@@ -467,123 +490,140 @@
                 for copy in pending.pop(0):
                     copy.wait()
             fill(i, slot)
-            pending.append(copies(targets, i, slot))
+            pending.append(copies(job, i, slot))
 
         def step(i, carry, base=done):
             slot = lax.rem(base + i, SLOTS)
-            for copy in copies(targets, i - SLOTS, slot):
+            for copy in copies(job, i - SLOTS, slot):
                 copy.wait()
             fill(i, slot)
             return carry
 
         lax.fori_loop(lead, tiles, step, 0)
         if tiles > SLOTS:
-            pending = [copies(targets, i, (done + i) % SLOTS) for i in range(tiles - SLOTS, tiles)]
+            pending = [copies(job, i, (done + i) % SLOTS) for i in range(tiles - SLOTS, tiles)]
         done += tiles
     for group in pending:
         for copy in group:
             copy.wait()
 
 
-def grads_first_kernel(act_hbm, dy_hbm, ctx_hbm, dx1_hbm, dw2, dwo, act, dyf, ctx, dx1, stage, in_sem, sem):
-    loads = [pltpu.make_async_copy(s, t, in_sem.at[i]) for i, (s, t) in enumerate(((act_hbm, act), (dy_hbm, dyf), (ctx_hbm, ctx), (dx1_hbm, dx1)))]
+def tile_at(i, tile, first=0):
+    return pl.ds(pl.multiple_of(first + i * tile, tile), tile)
+
+
+def outer_jobs(ready, left, right, targets, total, lead=0):
+    jobs = []
+    width = right.shape[1]
+    if lead:
+        small = TILE // 2
+        jobs.append((ready, small, lead // small, width, lambda i: mm_at(left[:, tile_at(i, small)], right[...]), lambda i: targets(tile_at(i, small))))
+        ready = lambda: None
+    jobs.append((ready, TILE, (total - lead) // TILE, width, lambda i: mm_at(left[:, tile_at(i, TILE, lead)], right[...]), lambda i: targets(tile_at(i, TILE, lead))))
+    return jobs
+
+
+def start_loads(pairs, sem):
+    loads = [pltpu.make_async_copy(src, dst, sem.at[i]) for i, (src, dst) in enumerate(pairs)]
     for copy in loads:
         copy.start()
 
     def ready(*which):
-        return lambda: [loads[i].wait() for i in which]
-
-    def tile(i):
-        return pl.ds(pl.multiple_of(i * TILE, TILE), TILE)
-
-    d = dyf.shape[1]
-    stream_grads([
-        (ready(0, 1), act.shape[1] // TILE, d, lambda i: mm_at(act[:, tile(i)], dyf[...]), lambda i: [(dw2.at[tile(i)], 0, d)]),
-        (ready(2, 3), ctx.shape[1] // TILE, d, lambda i: mm_at(ctx[:, tile(i)], dx1[...]), lambda i: [(dwo.at[tile(i)], 0, d)]),
-    ], stage, sem)
-
-
-def grads_second_kernel(dims, order, y_hbm, h2_hbm, du_hbm, h1_hbm, dqkv_hbm, y_out, dw1, dwq, dwk, dwv, y, h2, du, h1, dqkv, stage, in_sem, sem):
+        return lambda: [loads[i].wait() for i in which] and None
+
+    return ready
+
+
+def grads_first_kernel(dims, act_hbm, dy_hbm, h1_hbm, dqkv_hbm, dw2, dwq, dwk, dwv, act, dyf, h1, dqkv, stage, in_sem, sem):
     seq, d, hd, nq, nk, f, rows = dims
-    loads = [pltpu.make_async_copy(s, t, in_sem.at[i]) for i, (s, t) in enumerate(((h2_hbm, h2), (du_hbm, du), (h1_hbm, h1), (dqkv_hbm, dqkv), (y_hbm, y)))]
-    for copy in loads:
-        copy.start()
-
-    def ready(*which):
-        return lambda: [loads[i].wait() for i in which]
-
-    def tile(i):
-        return pl.ds(pl.multiple_of(i * TILE, TILE), TILE)
-
     nqd, nkd = nq * hd, nk * hd
-    y_copy = pltpu.make_async_copy(y, y_out, in_sem.at[5])
-
-    def ready_rest():
-        for i in (2, 3, 4):
-            loads[i].wait()
-        y_copy.start()
-
-    stream_grads([
-        (ready(0, 1), d // TILE, f, lambda i: mm_at(h2[:, tile(i)], du[...]), lambda i: [(dw1.at[tile(i)], 0, f)]),
-        (ready_rest, d // TILE, nqd + 2 * nkd, lambda i: mm_at(h1[:, tile(i)], dqkv[...]),
-         lambda i: [(dwq.at[tile(i)], 0, nqd), (dwk.at[tile(i)], nqd, nkd), (dwv.at[tile(i)], nqd + nkd, nkd)]),
-    ], stage, sem)
-    y_copy.wait()
+    ready = start_loads(((act_hbm, act), (dy_hbm, dyf), (h1_hbm, h1), (dqkv_hbm, dqkv)), in_sem)
+    stream_grads(
+        outer_jobs(ready(0, 1), act, dyf, lambda at: [(dw2.at[at], 0, d)], f, TILE)
+        + outer_jobs(ready(2, 3), h1, dqkv, lambda at: [(dwq.at[at], 0, nqd), (dwk.at[at], nqd, nkd), (dwv.at[at], nqd + nkd, nkd)], d),
+        stage, sem)
+
+
+def grads_second_kernel(dims, order, h2_hbm, du_hbm, ctx_hbm, dx1_hbm, hkeep_hbm, recv_hbm, x_hbm, dmid_hbm, g1_hbm, lng2_hbm, ykeep_hbm, mid_hbm, y_hbm,
+                        y_out, dx_out, lng_out, dw1, dwo,
+                        h2, du, ctx, dx1, hkeep, recv, x, dmid, g1, ykeep, mid, y, lng, stage, in_sem, end_sem, sem):
+    seq, d, hd, nq, nk, f, rows = dims
+    half = rows // 2
+    top, low = pl.ds(0, half), pl.ds(half, half)
+    ready = start_loads(((h2_hbm, h2), (du_hbm, du), (hkeep_hbm, hkeep), (recv_hbm, recv), (x_hbm, x), (dmid_hbm, dmid), (g1_hbm, g1),
+                         (lng2_hbm, lng.at[pl.ds(2, 2)]), (ykeep_hbm, ykeep), (mid_hbm, mid), (y_hbm, y.at[top]), (ctx_hbm, ctx), (dx1_hbm, dx1)), in_sem)
+    ends = [pltpu.make_async_copy(src, dst, end_sem.at[i]) for i, (src, dst) in enumerate(((y, y_out), (dmid, dx_out), (lng, lng_out)))]
+
+    def first_norm_back():
+        ready(2, 3, 4, 5, 6, 7, 8, 9, 10)()
+        dh1 = (hkeep[...] + recv[pl.ds(0, rows), :]).astype(BF16).astype(F32)
+        grad_rows, grad_gain, grad_bias = norm_rows_back(x[...].astype(F32), dh1, g1[...])
+        dmid[...] = (dmid[...].astype(F32) + grad_rows).astype(BF16)
+        lng[0:1, :] = grad_gain
+        lng[1:2, :] = grad_bias
+        mlp = (ykeep[...] + recv[pl.ds(rows, half), :]).astype(BF16)
+        y[low, :] = (mid[...].astype(F32) + mlp.astype(F32)).astype(BF16)
+        for copy in ends:
+            copy.start()
+
+    def dw1_jobs(after, first, total):
+        at = functools.partial(tile_at, tile=TILE, first=first)
+        return [(after, TILE, total // TILE, f, lambda i: mm_at(h2[:, at(i)], du[...]), lambda i: [(dw1.at[at(i)], 0, f)])]
+
+    lead = SLOTS * TILE
+    stream_grads(
+        dw1_jobs(ready(0, 1), 0, lead) + dw1_jobs(first_norm_back, lead, d - lead)
+        + outer_jobs(ready(11, 12), ctx, dx1, lambda at: [(dwo.at[at], 0, d)], ctx.shape[1]),
+        stage, sem)
+    for copy in ends:
+        copy.wait()
 
 
 def cost(flops, nbytes):
     return pl.CostEstimate(flops=flops, bytes_accessed=nbytes, transcendentals=0)
 
 
-def grads_first(dims, act, dyf, ctx, dx1):
-    seq, d, hd, nq, nk, f, rows = dims
-    nqd = nq * hd
-    return pl.pallas_call(
-        grads_first_kernel,
-        out_shape=[jax.ShapeDtypeStruct((f, d), F32), jax.ShapeDtypeStruct((nqd, d), F32)],
-        in_specs=[ANY] * 4, out_specs=[ANY] * 2,
-        scratch_shapes=[pltpu.VMEM((seq, f), BF16), pltpu.VMEM((seq, d), BF16), pltpu.VMEM((seq, nqd), BF16), pltpu.VMEM((seq, d), BF16),
-                        pltpu.VMEM((SLOTS, TILE, d), F32), pltpu.SemaphoreType.DMA((4,)), pltpu.SemaphoreType.DMA((SLOTS, 3))],
-        compiler_params=pltpu.CompilerParams(vmem_limit_bytes=VMEM_LIMIT),
-        cost_estimate=cost(2 * seq * d * (f + nqd), 4 * d * (f + nqd)),
-        name="grads_first",
-    )(act, dyf, ctx, dx1)
-
-
-def grads_second(dims, order, y, h2, du, h1, dqkv):
+def arr(shape, dtype=F32):
+    return jax.ShapeDtypeStruct(shape, dtype)
+
+
+def grads_first(dims, act, dyf, h1, dqkv):
     seq, d, hd, nq, nk, f, rows = dims
     nqd, nkd = nq * hd, nk * hd
     n_all = nqd + 2 * nkd
     return pl.pallas_call(
-        functools.partial(grads_second_kernel, dims),
-        out_shape=[jax.ShapeDtypeStruct((rows, d), BF16), jax.ShapeDtypeStruct((d, f), F32), jax.ShapeDtypeStruct((d, nqd), F32), jax.ShapeDtypeStruct((d, nkd), F32), jax.ShapeDtypeStruct((d, nkd), F32)],
-        in_specs=[ANY] * 6, out_specs=[ANY] * 5,
-        scratch_shapes=[pltpu.VMEM((rows, d), BF16), pltpu.VMEM((seq, d), BF16), pltpu.VMEM((seq, f), BF16), pltpu.VMEM((seq, d), BF16), pltpu.VMEM((seq, n_all), BF16),
-                        pltpu.VMEM((SLOTS, TILE, f), F32), pltpu.SemaphoreType.DMA((6,)), pltpu.SemaphoreType.DMA((SLOTS, 3))],
+        functools.partial(grads_first_kernel, dims),
+        out_shape=[arr((f, d)), arr((d, nqd)), arr((d, nkd)), arr((d, nkd))],
+        in_specs=[ANY] * 4, out_specs=[ANY] * 4,
+        scratch_shapes=[pltpu.VMEM((seq, f), BF16), pltpu.VMEM((seq, d), BF16), pltpu.VMEM((seq, d), BF16), pltpu.VMEM((seq, n_all), BF16),
+                        pltpu.VMEM((SLOTS, TILE, d), F32), pltpu.SemaphoreType.DMA((4,)), pltpu.SemaphoreType.DMA((SLOTS, 3))],
         compiler_params=pltpu.CompilerParams(vmem_limit_bytes=VMEM_LIMIT),
         cost_estimate=cost(2 * seq * d * (f + n_all), 4 * d * (f + n_all)),
+        name="grads_first",
+    )(act, dyf, h1, dqkv)
+
+
+def grads_second(dims, order, h2, du, ctx, dx1, hkeep, recv, x, dmid, g1, lng2, ykeep, mid, y):
+    seq, d, hd, nq, nk, f, rows = dims
+    nqd, half = nq * hd, rows // 2
+
+    def vb(*shape):
+        return pltpu.VMEM(shape, BF16)
+
+    def vf(*shape):
+        return pltpu.VMEM(shape, F32)
+
+    return pl.pallas_call(
+        functools.partial(grads_second_kernel, dims),
+        out_shape=[arr((rows, d), BF16), arr((rows, d), BF16), arr((4, d)), arr((d, f)), arr((nqd, d))],
+        in_specs=[ANY] * 14, out_specs=[ANY] * 5,
+        scratch_shapes=[vb(seq, d), vb(seq, f), vb(seq, nqd), vb(seq, d), vf(rows, d), vf(rows + half, d), vb(rows, d), vb(rows, d), vf(1, d),
+                        vf(half, d), vb(half, d), vb(rows, d), vf(4, d),
+                        vf(SLOTS, TILE, d), pltpu.SemaphoreType.DMA((13,)), pltpu.SemaphoreType.DMA((3,)), pltpu.SemaphoreType.DMA((SLOTS, 3))],
+        compiler_params=pltpu.CompilerParams(vmem_limit_bytes=VMEM_LIMIT),
+        cost_estimate=cost(2 * seq * d * (f + nqd), 4 * d * (f + nqd)),
         name="grads_second",
-    )(order, y, h2, du, h1, dqkv)
-
-
-def last_norm_kernel(order, hkeep, hrecv, x, dmid, g1, lng2, dx_out, lng_out):
-    dh1 = (hkeep[...] + hrecv[...]).astype(BF16).astype(F32)
-    grad_rows, grad_gain, grad_bias = norm_rows_back(x[...].astype(F32), dh1, g1[...])
-    dx_out[...] = (dmid[...].astype(F32) + grad_rows).astype(BF16)
-    lng_out[0:1, :] = grad_gain
-    lng_out[1:2, :] = grad_bias
-    lng_out[2:4, :] = lng2[...]
-
-
-def last_norm(order, hkeep, hrecv, x, dmid, g1, lng2):
-    rows, d = x.shape
-    return pl.pallas_call(
-        last_norm_kernel,
-        out_shape=[jax.ShapeDtypeStruct((rows, d), BF16), jax.ShapeDtypeStruct((4, d), F32)],
-        in_specs=[ANY] + [VMEM] * 6, out_specs=[VMEM] * 2,
-        cost_estimate=cost(rows * d * 20, rows * d * 16),
-        name="last_norm",
-    )(order, hkeep, hrecv, x, dmid, g1, lng2)
+    )(order, h2, du, ctx, dx1, hkeep, recv, x, dmid, g1, lng2, ykeep, mid, y)
 
 
 def layer_step(x, dy, positions, g1, b1, g2, b2, wq, wk, wv, wo, w1, w2, head_dim, n_tp):
@@ -596,19 +636,18 @@
     freq[0, :2 * rot] = np.tile(ROPE_BASE ** (-np.arange(rot) / rot), 2)
     x2, dy2 = x.reshape(rows, d), dy.reshape(rows, d)
     g1, b1, g2, b2 = (v.reshape(1, d) for v in (g1, b1, g2, b2))
-    (h1, h2, dyf, dx1, act, du, ctx, dqkv, y, dmid, hsend, hkeep, lng2) = chain(
+    (h1, h2, dyf, dx1, act, du, ctx, dqkv, y, mid, dmid, send, hkeep, ykeep, lng2) = chain(
         dims, x2, dy2, positions.reshape(1, seq), jnp.asarray(freq), g1, b1, g2, b2, wq, wk, wv, wo, w1, w2)
 
     def swap(v, bit):
         return lax.ppermute(v, 'tp', [(i, i ^ bit) for i in range(n_tp)])
 
-    hrecv = swap(hsend, 2)
-    dw2, dwo = grads_first(dims, act, dyf, ctx, dx1)
-    dx, lng = last_norm(dwo, hkeep, hrecv, x2, dmid, g1, lng2)
+    recv = swap(send, 2)
+    dw2, dwq, dwk, dwv = grads_first(dims, act, dyf, h1, dqkv)
+    y, dx, lng, dw1, dwo = grads_second(dims, dw2, h2, du, ctx, dx1, hkeep, recv, x2, dmid, g1, lng2, ykeep, mid, y)
     others = [swap(lng, bit) for bit in (1, 2, 3)]
-    y, dw1, dwq, dwk, dwv = grads_second(dims, lng, y, h2, du, h1, dqkv)
-    total = (lng + others[0]) + (others[1] + others[2])
-    return (y.reshape(x.shape), dx.reshape(x.shape), total[0], total[1], total[2], total[3], dwq, dwk, dwv, dwo, dw1, dw2)
+    sums = [(lng[i] + others[0][i]) + (others[1][i] + others[2][i]) for i in range(4)]
+    return (y.reshape(x.shape), dx.reshape(x.shape), sums[0], sums[1], sums[2], sums[3], dwq, dwk, dwv, dwo, dw1, dw2)
 
 
 def solution(mesh):

time: 96.7 us -> 97.5 us (level)
  waiting for transfers between devices: 0.01 us -> 3.24 us
  Pallas kernels: 91.2 us -> 88.8 us
    ppermute x4, waiting for transfers between devices: 0.01 us -> 3.24 us  [swap(): return lax.ppermute(v, 'tp', [(i, i ^ bit) for i in range(n_tp)])]
    pallas_call x3 -> x2, Pallas kernels: 30.8 us -> 28.3 us  [the longest x1 14.9 us: grads_first(): pl.pallas_call(functools.partial(grads_first_kernel, dims), out_shape=[ar...]
  transfers between devices with their start and end apart: 4 -> 4, of which waited for: 0 -> 2; matrix products, arithmetic and copies ran while one was open for 0% -> 0% of each run, Pallas kernels for 29% -> 15%
where the time goes in v3:
time: 97.5 us; the launch traced here: 97.4 us
  Pallas kernels  88.8 us (91%)
  waiting for transfers between devices  3.24 us (3%)
  starting transfers between devices  2.99 us (3%)
  other arithmetic  1.68 us (2%)
    pallas_call x1, Pallas kernels, chain(): pl.pallas_call(functools.partial(chain_kernel, dims), out_shape=out_shape...  60.5 us
    pallas_call x1, Pallas kernels, grads_first(): pl.pallas_call(functools.partial(grads_first_kernel, dims), out_shape=[ar...  14.9 us
    pallas_call x1, Pallas kernels, grads_second(): pl.pallas_call(functools.partial(grads_second_kernel, dims), out_shape=[a...  13.4 us
    ppermute x4, waiting for transfers between devices, swap(): return lax.ppermute(v, 'tp', [(i, i ^ bit) for i in range(n_tp)])  3.24 us
    ppermute x4, starting transfers between devices, swap(): return lax.ppermute(v, 'tp', [(i, i ^ bit) for i in range(n_tp)])  2.99 us
  transfers between devices with their start and end apart: 4, of which 2 were waited for; matrix products, arithmetic and copies ran while one was open for 0% of the time, Pallas kernels for 15%

profile of v3, /device:TPU:0, one launch (start us, length us, event | category | flops | bytes accessed | tf_op | source)
XLA Modules:
  0.0 97.4 jit_solution(5012146282483547328)
XLA Ops:
  0.6 60.5 %chain.1 = (bf16[128,3072]{1,0:T(8,128)(2,1)}, bf16[128,3072]{1,0:T(8,128)(2,1)}, bf16[128,3072]{1,0:T(8,128)(2,1)}, bf16[128,3072]{1,0:T(8,128)(2,1)}, bf16[128...) custom-call(bf16[32,3072]{1,0:T(8,128)(2,1)} %bitcast.13, ...), custom_call_target="tpu_custom_call" | custom-call | tf_op jit(solution)/shard_map/chain/pallas_call | solution.py:457
  61.2 1.1 %collective-permute-start = (f32[48,3072]{1,0:T(8,128)}, f32[48,3072]{1,0:T(8,128)}, u32[]{:S(2)}, u32[]{:S(2)}) collective-permute-start(f32[48,3072]{1,0:T(8,128)} %get-tuple-element.46), channel_id=1, source_target_pairs={{0,2},{1,3},{2,0},{3,1},{4,6},{5,7},{6,4},{7,5}} | collective-permute-start | bytes 1769480 | tf_op jit(solution)/shard_map/ppermute | solution.py:643
  62.3 14.9 %grads_first.1 = (f32[2048,3072]{1,0:T(8,128)}, f32[3072,768]{1,0:T(8,128)}, f32[3072,256]{1,0:T(8,128)}, f32[3072,256]{1,0:T(8,128)}) custom-call(bf16[128,2048]{1,0:T(8,128)(2,1)} %get-tuple-element.36.act_hbm, bf16[128,3072]{1,0:T(8,128)(2,1)} %get-tuple-element.37.dy_hbm, bf16[128,3072]{1,0:T(8,128)(2,1)} %get-tuple-element.38.h1_hbm, ...), custom_call_target="tpu_custom_call" | custom-call | flops 2617245696 | bytes 40894464 | tf_op jit(solution)/shard_map/grads_first/pallas_call | solution.py:594
  77.2 0.0 collective-permute-done.recv_hbm
  77.2 13.4 %grads_second.1 = (bf16[32,3072]{1,0:T(8,128)(2,1)}, bf16[32,3072]{1,0:T(8,128)(2,1)}, f32[4,3072]{1,0:T(4,128)}, f32[3072,2048]{1,0:T(8,128)}, f32[768,3072]{1,0:T(8,128)}) custom-call(f32[2048,3072]{1,0:T(8,128)} %get-tuple-element.35.order, bf16[128,3072]{1,0:T(8,128)(2,1)} %get-tuple-element.41.h2_hbm, bf16[128,2048]{1,0:T(8,128)(2,1)} %get-tuple-element.42.du_hbm, ...), custom_call_target="tpu_custom_call" | custom-call | flops 2214592512 | bytes 34603008 | tf_op jit(solution)/shard_map/grads_second/pallas_call | solution.py:616
  90.6 0.4 collective-permute-start.3
  91.0 1.1 %collective-permute-start.2 = (f32[4,3072]{1,0:T(4,128)}, f32[4,3072]{1,0:T(4,128)S(1)}, u32[]{:S(2)}, u32[]{:S(2)}) collective-permute-start(f32[4,3072]{1,0:T(4,128)} %get-tuple-element.54), channel_id=1, source_target_pairs={{0,2},{1,3},{2,0},{3,1},{4,6},{5,7},{6,4},{7,5}} | collective-permute-start | bytes 147464 | tf_op jit(solution)/shard_map/ppermute | solution.py:643
  92.1 0.4 collective-permute-start.1
  92.4 2.1 %collective-permute-done.3 = f32[4,3072]{1,0:T(4,128)S(1)} collective-permute-done((f32[4,3072]{1,0:T(4,128)}, f32[4,3072]{1,0:T(4,128)S(1)}, u32[]{:S(2)}, u32[]{:S(2)}) %collective-permute-start.3) | collective-permute-done | bytes 49184 | tf_op jit(solution)/shard_map/ppermute | solution.py:643
  94.6 1.1 %collective-permute-done.2 = f32[4,3072]{1,0:T(4,128)S(1)} collective-permute-done((f32[4,3072]{1,0:T(4,128)}, f32[4,3072]{1,0:T(4,128)S(1)}, u32[]{:S(2)}, u32[]{:S(2)}) %collective-permute-start.2) | collective-permute-done | bytes 49184 | tf_op jit(solution)/shard_map/ppermute | solution.py:643
  95.7 0.0 collective-permute-done.1
  95.7 1.7 %fusion = (f32[1,3072]{1,0:T(1,128)}, f32[1,3072]{1,0:T(1,128)}, f32[1,3072]{1,0:T(1,128)}, f32[1,3072]{1,0:T(1,128)}) fusion(f32[4,3072]{1,0:T(4,128)S(1)} %collective-permute-done.3, f32[4,3072]{1,0:T(4,128)S(1)} %collective-permute-done.2, f32[4,3072]{1,0:T(4,128)S(1)} %collective-permute-done.1, f32[4,3072]{1,0:T(4,128)} %get-tuple-element.54), kind=kLoop, calls=%fused_computation.1 | loop fusion | flops 36864 | bytes 245760 | tf_op jit(solution)/shard_map/add | solution.py:649
Async XLA Ops:
  61.2 16.0 %collective-permute-start = (f32[48,3072]{1,0:T(8,128)}, f32[48,3072]{1,0:T(8,128)}, u32[]{:S(2)}, u32[]{:S(2)}) collective-permute-start(f32[48,3072]{1,0:T(8,128)} %get-tuple-element.46), channel_id=1, source_target_pairs={{0,2},{1,3},{2,0},{3,1},{4,6},{5,7},{6,4},{7,5}} | collective-permute-start | bytes 1769480 | tf_op jit(solution)/shard_map/ppermute | solution.py:643
  90.6 4.0 %collective-permute-start.3 = (f32[4,3072]{1,0:T(4,128)}, f32[4,3072]{1,0:T(4,128)S(1)}, u32[]{:S(2)}, u32[]{:S(2)}) collective-permute-start(f32[4,3072]{1,0:T(4,128)} %get-tuple-element.54), channel_id=1, source_target_pairs={{0,3},{1,2},{2,1},{3,0},{4,7},{5,6},{6,5},{7,4}} | collective-permute-start | bytes 147464 | tf_op jit(solution)/shard_map/ppermute | solution.py:643
  91.0 4.7 %collective-permute-start.2 = (f32[4,3072]{1,0:T(4,128)}, f32[4,3072]{1,0:T(4,128)S(1)}, u32[]{:S(2)}, u32[]{:S(2)}) collective-permute-start(f32[4,3072]{1,0:T(4,128)} %get-tuple-element.54), channel_id=1, source_target_pairs={{0,2},{1,3},{2,0},{3,1},{4,6},{5,7},{6,4},{7,5}} | collective-permute-start | bytes 147464 | tf_op jit(solution)/shard_map/ppermute | solution.py:643
  92.1 3.6 %collective-permute-start.1 = (f32[4,3072]{1,0:T(4,128)}, f32[4,3072]{1,0:T(4,128)S(1)}, u32[]{:S(2)}, u32[]{:S(2)}) collective-permute-start(f32[4,3072]{1,0:T(4,128)} %get-tuple-element.54), channel_id=1, source_target_pairs={{0,1},{1,0},{2,3},{3,2},{4,5},{5,4},{6,7},{7,6}} | collective-permute-start | bytes 147464 | tf_op jit(solution)/shard_map/ppermute | solution.py:643

commit v4 on v3

--- a/solution.py
+++ b/solution.py
@@ -42,7 +42,10 @@
 
 
 def norm_rows_back(rows, grad, gain):
-    normed, scale = centre(rows)
+    return norm_back(*centre(rows), grad, gain)
+
+
+def norm_back(normed, scale, grad, gain):
     weighted = grad * (1.0 + gain)
     inner = jnp.mean(weighted * normed, axis=-1, keepdims=True)
     grad_rows = scale * (weighted - jnp.mean(weighted, axis=-1, keepdims=True) - normed * inner)
@@ -60,10 +63,10 @@
 
 
 def chain_kernel(dims, x_hbm, dy_hbm, pos_hbm, freq_hbm, g1_hbm, b1_hbm, g2_hbm, b2_hbm, wq_hbm, wk_hbm, wv_hbm, wo_hbm, w1_hbm, w2_hbm,
-                 h1_out, h2_out, dy_out, dx1_out, act_out, du_out, ctx_out, dqkv_out, y_out, mid_out, dmid_out, send_out, hkeep_out, ykeep_out, lng_out,
+                 h1_out, h2_out, dy_out, dx1_out, act_out, du_out, ctx_out, dqkv_out, y_out, mid_out, dmid_out, send_out, hkeep_out, ykeep_out, dg2_out, db2_out,
                  pos_ref, freq_ref, g1_ref, b1_ref, g2_ref, b2_ref,
                  wqkv, wo, w1, w2, h1, h2, dyf, dx1, x_own, mid, y_own, tmat, act, du, qs, kv, ctx, prob, cosb, sinb, gcs, dqkv, lng,
-                 part_a, part_b, part_c, dr_a, dr_b, dr_c, dr_d, snd_a, snd_b, snd_c, lnk_a, lnk_b, lnk_c, send, hkeep, ykeep,
+                 part_a, part_b, part_c, dr_a, dr_b, dr_c, dr_d, snd_a, snd_b, snd_c, lnk_a, lnk_b, lnk_c, send, hkeep, ykeep, lng_in, lng_chip, dg2, db2,
                  local_sem, out_sem, send_sem, recv_sem):
     seq, d, hd, nq, nk, f, rows = dims
     grp = nq // nk
@@ -150,11 +153,11 @@
                 use(i - first, pl.ds(self.pieces[i][2], self.pieces[i][3]))
 
     class Scatter:
-        def __init__(self, chunks, partial, from_part, summed, from_peer=None, link_rows=0):
-            self.chunks, self.cw, self.link_rows = chunks, d // chunks, link_rows
+        def __init__(self, chunks, partial, from_part, summed, from_peer=None, link_rows=0, early=0):
+            self.chunks, self.cw, self.link_rows, self.early = chunks, d // chunks, link_rows, early
             self.partial, self.from_part, self.summed, self.from_peer = partial, from_part, summed, from_peer
             self.base = sems.take(2 * chunks)
-            self.link = sems.take(chunks + 1) if link_rows else None
+            self.link = sems.take(chunks + 1 + early) if link_rows else None
 
         def cols(self, i):
             return pl.ds(pl.multiple_of(i * self.cw, self.cw), self.cw)
@@ -168,8 +171,12 @@
             return remote(self.summed.at[top, self.cols(i)], self.from_peer.at[top, self.cols(i)], self.link + i, peer)
 
         def second(self):
-            low = pl.ds(half, half)
-            return remote(self.summed.at[low], self.from_peer.at[low], self.link + self.chunks, peer)
+            at = (pl.ds(half, half), pl.ds(self.early * self.cw, d - self.early * self.cw))
+            return remote(self.summed.at[at], self.from_peer.at[at], self.link + self.chunks, peer)
+
+        def ahead(self, i):
+            at = (pl.ds(half, half), self.cols(i))
+            return remote(self.summed.at[at], self.from_peer.at[at], self.link + self.chunks + 1 + i, peer)
 
         def chip_sum(self, i):
             self.pair(i, 0).wait_recv()
@@ -177,6 +184,10 @@
             self.summed[:, cols] = self.partial[block(peer), cols] + self.from_part[0, :, cols]
             if self.link_rows:
                 self.first(i).start()
+            if self.early:
+                @pl.when(i < self.early)
+                def _():
+                    self.ahead(i).start()
 
         def run(self, chunk, drain=True):
             def step(i, carry):
@@ -211,6 +222,8 @@
                 for i in range(self.chunks):
                     self.first(i).wait_recv()
             else:
+                for i in range(self.early):
+                    self.ahead(i).wait_recv()
                 self.second().wait_recv()
             return self.kept_rows(sub) + self.from_peer[pl.ds(sub * half, half), :]
 
@@ -225,15 +238,17 @@
                     self.first(i).wait_send()
             if self.link_rows == rows:
                 self.second().wait_send()
+            for i in range(self.early):
+                self.ahead(i).wait_send()
 
     x_in.wait()
     small_in[0].wait()
     small_in[1].wait()
     h1[block(me), :] = norm_rows(x_own[...].astype(F32), g1_ref[...], b1_ref[...]).astype(BF16)
     pl.semaphore_wait(barrier, 2)
-    gather_h1 = Gather(h1, [(0, rows) + cut for cut in cuts(d, (1, 1, 1, 1))])
+    gather_h1 = Gather(h1, [(0, rows) + cut for cut in cuts(d, (4, 3, 3, 2))])
     gather_dy = Gather(dyf, [(0, rows, 0, d)])
-    late = [(0, half, 0, d)] + [(half, half) + cut for cut in cuts(d, (1, 1, 1, 1))]
+    late = [(0, half, 0, d)] + [(half, half) + cut for cut in cuts(d, (4, 3, 3, 2))]
     for i in range(len(gather_h1.pieces)):
         gather_h1.send(i)
     dy_in.wait()
@@ -318,8 +333,8 @@
     weight_in[5].wait()
 
     def up(j, depth):
-        def step(i, carry):
-            cols = pl.ds(pl.multiple_of(i * nb, nb), nb)
+        for i in range(f // nb):
+            cols = pl.ds(i * nb, nb)
             piece = mm(h2[:, depth], w1[depth, cols])
             if j == 0:
                 part_c[:, cols] = piece
@@ -329,27 +344,25 @@
                 relu_up = jnp.maximum((part_c[:, cols] + piece).astype(BF16).astype(F32), 0.0)
                 act[:, cols] = (relu_up * relu_up).astype(BF16)
                 du[:, cols] = (tmat[:, cols] * (2.0 * relu_up)).astype(BF16)
-            return carry
-
-        lax.fori_loop(0, f // nb, step, 0)
 
     gather_h2.feed(1, up)
     put(h2, h2_out)
     put(act, act_out)
     put(du, du_out)
-    sum_dh2 = Scatter(4, part_b, dr_b, snd_b, lnk_b, rows)
+    sum_dh2 = Scatter(6, part_b, dr_b, snd_b, lnk_b, rows, 2)
     sum_dh2.run(lambda cols: mm_bt(du[...], w1[cols, :]))
 
     sum_mlp = Scatter(4, part_c, dr_c, snd_c, lnk_c, half)
     sum_mlp.run(lambda cols: mm(act[...], w2[:, cols]), drain=False)
 
     gather_dx1 = Gather(dx1, late)
+    normed2, scale2 = centre(mid[...].astype(F32))
     for sub in (0, 1):
         if sub == 0:
             sum_dh2.kept()
-        own = pl.ds(sub * half, half)
         dh2_rows = sum_dh2.rows_sum(sub).astype(BF16).astype(F32)
-        grad_rows, grad_gain, grad_bias = norm_rows_back(mid[own, :].astype(F32), dh2_rows, g2_ref[...])
+        own = slice(sub * half, (sub + 1) * half)
+        grad_rows, grad_gain, grad_bias = norm_back(normed2[own], scale2[own], dh2_rows, g2_ref[...])
         dx1[block(me, sub), :] = (dyf[block(me, sub), :].astype(F32) + grad_rows).astype(BF16)
         for i in ((0,) if sub == 0 else range(1, len(late))):
             gather_dx1.send(i)
@@ -359,8 +372,10 @@
         else:
             lng[0:1, :] += grad_gain
             lng[1:2, :] += grad_bias
-    put(lng, lng_out)
     put(dx1.at[block(me)], dmid_out)
+    lng_base = sems.take(2)
+    lng_pair = remote(lng, lng_in.at[0], lng_base, part)
+    lng_pair.start()
     sum_mlp.drain()
     low = pl.ds(half, half)
     send[pl.ds(rows, half), :] = snd_c[low, :]
@@ -368,6 +383,10 @@
     ykeep[...] = sum_mlp.kept_rows(1)
     put(ykeep, ykeep_out)
     put(mid.at[low], mid_out)
+    lng_pair.wait_recv()
+    lng_chip[...] = lng[...] + lng_in[0]
+    lng_link = remote(lng_chip, lng_in.at[1], lng_base + 1, peer)
+    lng_link.start()
     dctx_sum = tmat.at[:, pl.ds(0, nqd)]
     gather_dx1.feed(1, lambda j, cols: add(dctx_sum, j, mm_bt(dx1[:, cols], wo[:, cols])))
     put(dx1, dx1_out)
@@ -393,8 +412,13 @@
     top = pl.ds(0, half)
     y_own[...] = (mid[top, :].astype(F32) + sum_mlp.rows_sum(0).astype(BF16).astype(F32)).astype(BF16)
     put(y_own, y_out)
-    sum_dh1 = Scatter(3, part_a, dr_d, send.at[pl.ds(0, rows)])
+    sum_dh1 = Scatter(4, part_a, dr_d, send.at[pl.ds(0, rows)])
     sum_attn.pair_sent()
+    lng_link.wait_recv()
+    dg2[...] = lng_chip[0:1, :] + lng_in[1, 0:1, :]
+    db2[...] = lng_chip[1:2, :] + lng_in[1, 1:2, :]
+    put(dg2, dg2_out)
+    put(db2, db2_out)
     sum_dh1.run(lambda cols: mm_bt(dqkv[...], wqkv[cols, :]))
     put(send, send_out)
     sum_dh1.kept()
@@ -410,6 +434,8 @@
         scatter.pair_sent()
     for scatter in (sum_attn, sum_dh2, sum_mlp):
         scatter.link_sent()
+    lng_pair.wait_send()
+    lng_link.wait_send()
     for copy in outs:
         copy.wait()
 
@@ -438,8 +464,8 @@
     def vf(*shape):
         return pltpu.VMEM(shape, F32)
 
-    out_shape = [arr((seq, d), BF16)] * 4 + [arr((seq, f), BF16)] * 2 + [arr((seq, nqd), BF16), arr((seq, n_all), BF16)] + [arr((half, d), BF16)] * 2 + [arr((rows, d), BF16), arr((rows + half, d), F32), arr((rows, d), F32), arr((half, d), F32), arr((2, d), F32)]
-    n_sems = 3 * (4 + 1 + 5 + 5) + 2 * (4 + 4 + 4 + 3) + (5 + 5 + 5)
+    out_shape = [arr((seq, d), BF16)] * 4 + [arr((seq, f), BF16)] * 2 + [arr((seq, nqd), BF16), arr((seq, n_all), BF16)] + [arr((half, d), BF16)] * 2 + [arr((rows, d), BF16), arr((rows + half, d), F32), arr((rows, d), F32), arr((half, d), F32)] + [arr((1, d), F32)] * 2
+    n_sems = 3 * (4 + 1 + 5 + 5) + 2 * (4 + 6 + 4 + 4) + (5 + 9 + 5) + 2
     scratch = [
         pltpu.VMEM((1, seq), jnp.int32), vf(1, hd), vf(1, d), vf(1, d), vf(1, d), vf(1, d),
         vm(d, n_all), vm(nqd, d), vm(d, f), vm(f, d),
@@ -450,7 +476,7 @@
         vf(seq, d), vf(seq, d), vf(seq, d),
         vf(2, rows, d), vf(2, rows, d), vf(2, rows, d), vf(2, rows, d),
         vf(rows, d), vf(rows, d), vf(rows, d), vf(rows, d), vf(rows, d), vf(half, d),
-        vf(rows + half, d), vf(rows, d), vf(half, d),
+        vf(rows + half, d), vf(rows, d), vf(half, d), vf(2, 2, d), vf(2, d), vf(1, d), vf(1, d),
         pltpu.SemaphoreType.DMA((14,)), pltpu.SemaphoreType.DMA((len(out_shape),)),
         pltpu.SemaphoreType.DMA((n_sems,)), pltpu.SemaphoreType.DMA((n_sems,)),
     ]
@@ -544,18 +570,18 @@
         stage, sem)
 
 
-def grads_second_kernel(dims, order, h2_hbm, du_hbm, ctx_hbm, dx1_hbm, hkeep_hbm, recv_hbm, x_hbm, dmid_hbm, g1_hbm, lng2_hbm, ykeep_hbm, mid_hbm, y_hbm,
-                        y_out, dx_out, lng_out, dw1, dwo,
-                        h2, du, ctx, dx1, hkeep, recv, x, dmid, g1, ykeep, mid, y, lng, stage, in_sem, end_sem, sem):
+def grads_second_kernel(dims, order, h2_hbm, du_hbm, ctx_hbm, dx1_hbm, hkeep_hbm, recv_hbm, x_hbm, dmid_hbm, g1_hbm, dg2_hbm, db2_hbm, ykeep_hbm, mid_hbm, y_hbm,
+                        y_out, dx_out, lng_out, dg2_out, db2_out, dw1, dwo,
+                        h2, du, ctx, dx1, hkeep, recv, x, dmid, g1, ykeep, mid, y, lng, dg2, db2, stage, in_sem, end_sem, sem):
     seq, d, hd, nq, nk, f, rows = dims
     half = rows // 2
     top, low = pl.ds(0, half), pl.ds(half, half)
     ready = start_loads(((h2_hbm, h2), (du_hbm, du), (hkeep_hbm, hkeep), (recv_hbm, recv), (x_hbm, x), (dmid_hbm, dmid), (g1_hbm, g1),
-                         (lng2_hbm, lng.at[pl.ds(2, 2)]), (ykeep_hbm, ykeep), (mid_hbm, mid), (y_hbm, y.at[top]), (ctx_hbm, ctx), (dx1_hbm, dx1)), in_sem)
-    ends = [pltpu.make_async_copy(src, dst, end_sem.at[i]) for i, (src, dst) in enumerate(((y, y_out), (dmid, dx_out), (lng, lng_out)))]
+                         (dg2_hbm, dg2), (db2_hbm, db2), (ykeep_hbm, ykeep), (mid_hbm, mid), (y_hbm, y.at[top]), (ctx_hbm, ctx), (dx1_hbm, dx1)), in_sem)
+    ends = [pltpu.make_async_copy(src, dst, end_sem.at[i]) for i, (src, dst) in enumerate(((y, y_out), (dmid, dx_out), (lng, lng_out), (dg2, dg2_out), (db2, db2_out)))]
 
     def first_norm_back():
-        ready(2, 3, 4, 5, 6, 7, 8, 9, 10)()
+        ready(2, 3, 4, 5, 6, 7, 8, 9, 10, 11)()
         dh1 = (hkeep[...] + recv[pl.ds(0, rows), :]).astype(BF16).astype(F32)
         grad_rows, grad_gain, grad_bias = norm_rows_back(x[...].astype(F32), dh1, g1[...])
         dmid[...] = (dmid[...].astype(F32) + grad_rows).astype(BF16)
@@ -573,7 +599,7 @@
     lead = SLOTS * TILE
     stream_grads(
         dw1_jobs(ready(0, 1), 0, lead) + dw1_jobs(first_norm_back, lead, d - lead)
-        + outer_jobs(ready(11, 12), ctx, dx1, lambda at: [(dwo.at[at], 0, d)], ctx.shape[1]),
+        + outer_jobs(ready(12, 13), ctx, dx1, lambda at: [(dwo.at[at], 0, d)], ctx.shape[1]),
         stage, sem)
     for copy in ends:
         copy.wait()
@@ -603,7 +629,7 @@
     )(act, dyf, h1, dqkv)
 
 
-def grads_second(dims, order, h2, du, ctx, dx1, hkeep, recv, x, dmid, g1, lng2, ykeep, mid, y):
+def grads_second(dims, order, h2, du, ctx, dx1, hkeep, recv, x, dmid, g1, dg2, db2, ykeep, mid, y):
     seq, d, hd, nq, nk, f, rows = dims
     nqd, half = nq * hd, rows // 2
 
@@ -615,15 +641,15 @@
 
     return pl.pallas_call(
         functools.partial(grads_second_kernel, dims),
-        out_shape=[arr((rows, d), BF16), arr((rows, d), BF16), arr((4, d)), arr((d, f)), arr((nqd, d))],
-        in_specs=[ANY] * 14, out_specs=[ANY] * 5,
+        out_shape=[arr((rows, d), BF16), arr((rows, d), BF16), arr((2, d)), arr((1, d)), arr((1, d)), arr((d, f)), arr((nqd, d))],
+        in_specs=[ANY] * 15, out_specs=[ANY] * 7,
         scratch_shapes=[vb(seq, d), vb(seq, f), vb(seq, nqd), vb(seq, d), vf(rows, d), vf(rows + half, d), vb(rows, d), vb(rows, d), vf(1, d),
-                        vf(half, d), vb(half, d), vb(rows, d), vf(4, d),
-                        vf(SLOTS, TILE, d), pltpu.SemaphoreType.DMA((13,)), pltpu.SemaphoreType.DMA((3,)), pltpu.SemaphoreType.DMA((SLOTS, 3))],
+                        vf(half, d), vb(half, d), vb(rows, d), vf(2, d), vf(1, d), vf(1, d),
+                        vf(SLOTS, TILE, d), pltpu.SemaphoreType.DMA((14,)), pltpu.SemaphoreType.DMA((5,)), pltpu.SemaphoreType.DMA((SLOTS, 3))],
         compiler_params=pltpu.CompilerParams(vmem_limit_bytes=VMEM_LIMIT),
         cost_estimate=cost(2 * seq * d * (f + nqd), 4 * d * (f + nqd)),
         name="grads_second",
-    )(order, h2, du, ctx, dx1, hkeep, recv, x, dmid, g1, lng2, ykeep, mid, y)
+    )(order, h2, du, ctx, dx1, hkeep, recv, x, dmid, g1, dg2, db2, ykeep, mid, y)
 
 
 def layer_step(x, dy, positions, g1, b1, g2, b2, wq, wk, wv, wo, w1, w2, head_dim, n_tp):
@@ -636,7 +662,7 @@
     freq[0, :2 * rot] = np.tile(ROPE_BASE ** (-np.arange(rot) / rot), 2)
     x2, dy2 = x.reshape(rows, d), dy.reshape(rows, d)
     g1, b1, g2, b2 = (v.reshape(1, d) for v in (g1, b1, g2, b2))
-    (h1, h2, dyf, dx1, act, du, ctx, dqkv, y, mid, dmid, send, hkeep, ykeep, lng2) = chain(
+    (h1, h2, dyf, dx1, act, du, ctx, dqkv, y, mid, dmid, send, hkeep, ykeep, dg2, db2) = chain(
         dims, x2, dy2, positions.reshape(1, seq), jnp.asarray(freq), g1, b1, g2, b2, wq, wk, wv, wo, w1, w2)
 
     def swap(v, bit):
@@ -644,10 +670,10 @@
 
     recv = swap(send, 2)
     dw2, dwq, dwk, dwv = grads_first(dims, act, dyf, h1, dqkv)
-    y, dx, lng, dw1, dwo = grads_second(dims, dw2, h2, du, ctx, dx1, hkeep, recv, x2, dmid, g1, lng2, ykeep, mid, y)
+    y, dx, lng, dg2, db2, dw1, dwo = grads_second(dims, dw2, h2, du, ctx, dx1, hkeep, recv, x2, dmid, g1, dg2, db2, ykeep, mid, y)
     others = [swap(lng, bit) for bit in (1, 2, 3)]
-    sums = [(lng[i] + others[0][i]) + (others[1][i] + others[2][i]) for i in range(4)]
-    return (y.reshape(x.shape), dx.reshape(x.shape), sums[0], sums[1], sums[2], sums[3], dwq, dwk, dwv, dwo, dw1, dw2)
+    sums = [(lng[i] + others[0][i]) + (others[1][i] + others[2][i]) for i in range(2)]
+    return (y.reshape(x.shape), dx.reshape(x.shape), sums[0], sums[1], dg2.reshape(d), db2.reshape(d), dwq, dwk, dwv, dwo, dw1, dw2)
 
 
 def solution(mesh):

time: 97.5 us -> 96.3 us (0.988)
  transfers between devices with their start and end apart: 4 -> 4, of which waited for: 2 -> 2; matrix products, arithmetic and copies ran while one was open for 0% -> 0% of each run, Pallas kernels for 15% -> 16%
where the time goes in v4:
time: 96.3 us; the launch traced here: 96.1 us
  Pallas kernels  88.7 us (92%)
  starting transfers between devices  2.88 us (3%)
  waiting for transfers between devices  2.43 us (3%)
  other arithmetic  1.47 us (2%)
    pallas_call x1, Pallas kernels, chain(): pl.pallas_call(functools.partial(chain_kernel, dims), out_shape=out_shape...  60.2 us
    pallas_call x1, Pallas kernels, grads_first(): pl.pallas_call(functools.partial(grads_first_kernel, dims), out_shape=[ar...  15 us
    pallas_call x1, Pallas kernels, grads_second(): pl.pallas_call(functools.partial(grads_second_kernel, dims), out_shape=[a...  13.4 us
    ppermute x4, starting transfers between devices, swap(): return lax.ppermute(v, 'tp', [(i, i ^ bit) for i in range(n_tp)])  2.88 us
    ppermute x4, waiting for transfers between devices, swap(): return lax.ppermute(v, 'tp', [(i, i ^ bit) for i in range(n_tp)])  2.43 us
  transfers between devices with their start and end apart: 4, of which 2 were waited for; matrix products, arithmetic and copies ran while one was open for 0% of the time, Pallas kernels for 16%

profile of v4, /device:TPU:0, one launch (start us, length us, event | category | flops | bytes accessed | tf_op | source)
XLA Modules:
  0.0 96.1 jit_solution(14706557983915288565)
XLA Ops:
  0.6 60.2 %chain.1 = (bf16[128,3072]{1,0:T(8,128)(2,1)}, bf16[128,3072]{1,0:T(8,128)(2,1)}, bf16[128,3072]{1,0:T(8,128)(2,1)}, bf16[128,3072]{1,0:T(8,128)(2,1)}, bf16[128...) custom-call(bf16[32,3072]{1,0:T(8,128)(2,1)} %bitcast.13, ...), custom_call_target="tpu_custom_call" | custom-call | tf_op jit(solution)/shard_map/chain/pallas_call | solution.py:483
  60.9 1.0 %collective-permute-start = (f32[48,3072]{1,0:T(8,128)}, f32[48,3072]{1,0:T(8,128)}, u32[]{:S(2)}, u32[]{:S(2)}) collective-permute-start(f32[48,3072]{1,0:T(8,128)} %get-tuple-element.49), channel_id=1, source_target_pairs={{0,2},{1,3},{2,0},{3,1},{4,6},{5,7},{6,4},{7,5}} | collective-permute-start | bytes 1769480 | tf_op jit(solution)/shard_map/ppermute | solution.py:669
  61.9 15.0 %grads_first.1 = (f32[2048,3072]{1,0:T(8,128)}, f32[3072,768]{1,0:T(8,128)}, f32[3072,256]{1,0:T(8,128)}, f32[3072,256]{1,0:T(8,128)}) custom-call(bf16[128,2048]{1,0:T(8,128)(2,1)} %get-tuple-element.39.act_hbm, bf16[128,3072]{1,0:T(8,128)(2,1)} %get-tuple-element.40.dy_hbm, bf16[128,3072]{1,0:T(8,128)(2,1)} %get-tuple-element.41.h1_hbm, ...), custom_call_target="tpu_custom_call" | custom-call | flops 2617245696 | bytes 40894464 | tf_op jit(solution)/shard_map/grads_first/pallas_call | solution.py:620
  76.9 0.0 collective-permute-done.recv_hbm
  76.9 13.4 %grads_second.1 = (bf16[32,3072]{1,0:T(8,128)(2,1)}, bf16[32,3072]{1,0:T(8,128)(2,1)}, f32[2,3072]{1,0:T(2,128)}, f32[1,3072]{1,0:T(1,128)}, f32[1,3072]{1,0:T(1...) custom-call(f32[2048,3072]{1,0:T(8,128)} %get-tuple-element.38.order, bf16[128,3072]{1,0:T(8,128)(2,1)} %get-tuple-element.44.h2_hbm, ...), custom_call_target="tpu_custom_call" | custom-call | flops 2214592512 | bytes 34603008 | tf_op jit(solution)/shard_map/grads_second/pallas_call | solution.py:642
  90.3 0.4 collective-permute-start.3
  90.7 1.0 %collective-permute-start.2 = (f32[2,3072]{1,0:T(2,128)}, f32[2,3072]{1,0:T(2,128)S(1)}, u32[]{:S(2)}, u32[]{:S(2)}) collective-permute-start(f32[2,3072]{1,0:T(2,128)} %get-tuple-element.58), channel_id=1, source_target_pairs={{0,2},{1,3},{2,0},{3,1},{4,6},{5,7},{6,4},{7,5}} | collective-permute-start | bytes 73736 | tf_op jit(solution)/shard_map/ppermute | solution.py:669
  91.7 0.5 collective-permute-start.1
  92.2 1.5 %collective-permute-done.3 = f32[2,3072]{1,0:T(2,128)S(1)} collective-permute-done((f32[2,3072]{1,0:T(2,128)}, f32[2,3072]{1,0:T(2,128)S(1)}, u32[]{:S(2)}, u32[]{:S(2)}) %collective-permute-start.3) | collective-permute-done | bytes 24608 | tf_op jit(solution)/shard_map/ppermute | solution.py:669
  93.8 0.9 collective-permute-done.2
  94.6 0.0 collective-permute-done.1
  94.7 1.5 %fusion = (f32[1,3072]{1,0:T(1,128)}, f32[1,3072]{1,0:T(1,128)}) fusion(f32[2,3072]{1,0:T(2,128)S(1)} %collective-permute-done.3, f32[2,3072]{1,0:T(2,128)S(1)} %collective-permute-done.2, f32[2,3072]{1,0:T(2,128)S(1)} %collective-permute-done.1, f32[2,3072]{1,0:T(2,128)} %get-tuple-element.58), kind=kLoop, calls=%fused_computation.1 | loop fusion | flops 18432 | bytes 122880 | tf_op jit(solution)/shard_map/add | solution.py:675
Async XLA Ops:
  60.9 16.0 %collective-permute-start = (f32[48,3072]{1,0:T(8,128)}, f32[48,3072]{1,0:T(8,128)}, u32[]{:S(2)}, u32[]{:S(2)}) collective-permute-start(f32[48,3072]{1,0:T(8,128)} %get-tuple-element.49), channel_id=1, source_target_pairs={{0,2},{1,3},{2,0},{3,1},{4,6},{5,7},{6,4},{7,5}} | collective-permute-start | bytes 1769480 | tf_op jit(solution)/shard_map/ppermute | solution.py:669
  90.3 3.4 %collective-permute-start.3 = (f32[2,3072]{1,0:T(2,128)}, f32[2,3072]{1,0:T(2,128)S(1)}, u32[]{:S(2)}, u32[]{:S(2)}) collective-permute-start(f32[2,3072]{1,0:T(2,128)} %get-tuple-element.58), channel_id=1, source_target_pairs={{0,3},{1,2},{2,1},{3,0},{4,7},{5,6},{6,5},{7,4}} | collective-permute-start | bytes 73736 | tf_op jit(solution)/shard_map/ppermute | solution.py:669
  90.7 3.9 %collective-permute-start.2 = (f32[2,3072]{1,0:T(2,128)}, f32[2,3072]{1,0:T(2,128)S(1)}, u32[]{:S(2)}, u32[]{:S(2)}) collective-permute-start(f32[2,3072]{1,0:T(2,128)} %get-tuple-element.58), channel_id=1, source_target_pairs={{0,2},{1,3},{2,0},{3,1},{4,6},{5,7},{6,4},{7,5}} | collective-permute-start | bytes 73736 | tf_op jit(solution)/shard_map/ppermute | solution.py:669
  91.7 2.9 %collective-permute-start.1 = (f32[2,3072]{1,0:T(2,128)}, f32[2,3072]{1,0:T(2,128)S(1)}, u32[]{:S(2)}, u32[]{:S(2)}) collective-permute-start(f32[2,3072]{1,0:T(2,128)} %get-tuple-element.58), channel_id=1, source_target_pairs={{0,1},{1,0},{2,3},{3,2},{4,5},{5,4},{6,7},{7,6}} | collective-permute-start | bytes 73736 | tf_op jit(solution)/shard_map/ppermute | solution.py:669

commit v5 on v4

--- a/solution.py
+++ b/solution.py
@@ -248,7 +248,7 @@
     pl.semaphore_wait(barrier, 2)
     gather_h1 = Gather(h1, [(0, rows) + cut for cut in cuts(d, (4, 3, 3, 2))])
     gather_dy = Gather(dyf, [(0, rows, 0, d)])
-    late = [(0, half, 0, d)] + [(half, half) + cut for cut in cuts(d, (4, 3, 3, 2))]
+    late = [(0, half, 0, d)] + [(half, half) + cut for cut in cuts(d, (2, 1))]
     for i in range(len(gather_h1.pieces)):
         gather_h1.send(i)
     dy_in.wait()
@@ -409,22 +409,23 @@
         lo = nqd + nkd + k * hd
         dqkv[:, lo:lo + hd] = grad_v
     put(dqkv, dqkv_out)
+    sum_dh1 = Scatter(4, part_a, dr_d, send.at[pl.ds(0, rows)])
+    sum_attn.pair_sent()
+    sum_dh1.run(lambda cols: mm_bt(dqkv[...], wqkv[cols, :]), drain=False)
+    sum_dh1.drain()
+    put(send, send_out)
+    sum_dh1.kept()
+    for sub in (0, 1):
+        hkeep[pl.ds(sub * half, half), :] = sum_dh1.kept_rows(sub)
+    put(hkeep, hkeep_out)
     top = pl.ds(0, half)
     y_own[...] = (mid[top, :].astype(F32) + sum_mlp.rows_sum(0).astype(BF16).astype(F32)).astype(BF16)
     put(y_own, y_out)
-    sum_dh1 = Scatter(4, part_a, dr_d, send.at[pl.ds(0, rows)])
-    sum_attn.pair_sent()
     lng_link.wait_recv()
     dg2[...] = lng_chip[0:1, :] + lng_in[1, 0:1, :]
     db2[...] = lng_chip[1:2, :] + lng_in[1, 1:2, :]
     put(dg2, dg2_out)
     put(db2, db2_out)
-    sum_dh1.run(lambda cols: mm_bt(dqkv[...], wqkv[cols, :]))
-    put(send, send_out)
-    sum_dh1.kept()
-    for sub in (0, 1):
-        hkeep[pl.ds(sub * half, half), :] = sum_dh1.kept_rows(sub)
-    put(hkeep, hkeep_out)
 
     for gather in (gather_h1, gather_dy, gather_h2, gather_dx1):
         for kind in (0, 1, 2):
@@ -465,7 +466,7 @@
         return pltpu.VMEM(shape, F32)
 
     out_shape = [arr((seq, d), BF16)] * 4 + [arr((seq, f), BF16)] * 2 + [arr((seq, nqd), BF16), arr((seq, n_all), BF16)] + [arr((half, d), BF16)] * 2 + [arr((rows, d), BF16), arr((rows + half, d), F32), arr((rows, d), F32), arr((half, d), F32)] + [arr((1, d), F32)] * 2
-    n_sems = 3 * (4 + 1 + 5 + 5) + 2 * (4 + 6 + 4 + 4) + (5 + 9 + 5) + 2
+    n_sems = 3 * (4 + 1 + 3 + 3) + 2 * (4 + 6 + 4 + 4) + (5 + 9 + 5) + 2
     scratch = [
         pltpu.VMEM((1, seq), jnp.int32), vf(1, hd), vf(1, d), vf(1, d), vf(1, d), vf(1, d),
         vm(d, n_all), vm(nqd, d), vm(d, f), vm(f, d),
@@ -585,8 +586,11 @@
         dh1 = (hkeep[...] + recv[pl.ds(0, rows), :]).astype(BF16).astype(F32)
         grad_rows, grad_gain, grad_bias = norm_rows_back(x[...].astype(F32), dh1, g1[...])
         dmid[...] = (dmid[...].astype(F32) + grad_rows).astype(BF16)
-        lng[0:1, :] = grad_gain
-        lng[1:2, :] = grad_bias
+        lanes = lng.shape[1]
+        for i, total in enumerate((grad_gain, grad_bias)):
+            for j in range(d // lanes):
+                at = i * (d // lanes) + j
+                lng[at:at + 1, :] = total[:, j * lanes:(j + 1) * lanes]
         mlp = (ykeep[...] + recv[pl.ds(rows, half), :]).astype(BF16)
         y[low, :] = (mid[...].astype(F32) + mlp.astype(F32)).astype(BF16)
         for copy in ends:
@@ -641,10 +645,10 @@
 
     return pl.pallas_call(
         functools.partial(grads_second_kernel, dims),
-        out_shape=[arr((rows, d), BF16), arr((rows, d), BF16), arr((2, d)), arr((1, d)), arr((1, d)), arr((d, f)), arr((nqd, d))],
+        out_shape=[arr((rows, d), BF16), arr((rows, d), BF16), arr((2 * d // 128, 128)), arr((1, d)), arr((1, d)), arr((d, f)), arr((nqd, d))],
         in_specs=[ANY] * 15, out_specs=[ANY] * 7,
         scratch_shapes=[vb(seq, d), vb(seq, f), vb(seq, nqd), vb(seq, d), vf(rows, d), vf(rows + half, d), vb(rows, d), vb(rows, d), vf(1, d),
-                        vf(half, d), vb(half, d), vb(rows, d), vf(2, d), vf(1, d), vf(1, d),
+                        vf(half, d), vb(half, d), vb(rows, d), vf(2 * d // 128, 128), vf(1, d), vf(1, d),
                         vf(SLOTS, TILE, d), pltpu.SemaphoreType.DMA((14,)), pltpu.SemaphoreType.DMA((5,)), pltpu.SemaphoreType.DMA((SLOTS, 3))],
         compiler_params=pltpu.CompilerParams(vmem_limit_bytes=VMEM_LIMIT),
         cost_estimate=cost(2 * seq * d * (f + nqd), 4 * d * (f + nqd)),
@@ -672,7 +676,7 @@
     dw2, dwq, dwk, dwv = grads_first(dims, act, dyf, h1, dqkv)
     y, dx, lng, dg2, db2, dw1, dwo = grads_second(dims, dw2, h2, du, ctx, dx1, hkeep, recv, x2, dmid, g1, dg2, db2, ykeep, mid, y)
     others = [swap(lng, bit) for bit in (1, 2, 3)]
-    sums = [(lng[i] + others[0][i]) + (others[1][i] + others[2][i]) for i in range(2)]
+    sums = ((lng + others[0]) + (others[1] + others[2])).reshape(2, d)
     return (y.reshape(x.shape), dx.reshape(x.shape), sums[0], sums[1], dg2.reshape(d), db2.reshape(d), dwq, dwk, dwv, dwo, dw1, dw2)
 
 

time: 96.3 us -> 94.4 us (0.980)
  Pallas kernels: 88.7 us -> 86.9 us
    pallas_call x1, Pallas kernels: 60.2 us -> 58.5 us  [chain(): pl.pallas_call(functools.partial(chain_kernel, dims), out_shape=out_shape...]
where the time goes in v5:
time: 94.4 us; the launch traced here: 94.2 us
  Pallas kernels  86.9 us (92%)
  starting transfers between devices  2.97 us (3%)
  waiting for transfers between devices  2.34 us (2%)
    pallas_call x1, Pallas kernels, chain(): pl.pallas_call(functools.partial(chain_kernel, dims), out_shape=out_shape...  58.5 us
    pallas_call x1, Pallas kernels, grads_first(): pl.pallas_call(functools.partial(grads_first_kernel, dims), out_shape=[ar...  14.9 us
    pallas_call x1, Pallas kernels, grads_second(): pl.pallas_call(functools.partial(grads_second_kernel, dims), out_shape=[a...  13.4 us
    ppermute x4, starting transfers between devices, swap(): return lax.ppermute(v, 'tp', [(i, i ^ bit) for i in range(n_tp)])  2.97 us
    ppermute x4, waiting for transfers between devices, swap(): return lax.ppermute(v, 'tp', [(i, i ^ bit) for i in range(n_tp)])  2.34 us
  transfers between devices with their start and end apart: 4, of which 2 were waited for; matrix products, arithmetic and copies ran while one was open for 0% of the time, Pallas kernels for 16%

profile of v5, /device:TPU:0, one launch (start us, length us, event | category | flops | bytes accessed | tf_op | source)
XLA Modules:
  0.0 94.2 jit_solution(13978783470672745361)
XLA Ops:
  0.6 58.5 %chain.1 = (bf16[128,3072]{1,0:T(8,128)(2,1)}, bf16[128,3072]{1,0:T(8,128)(2,1)}, bf16[128,3072]{1,0:T(8,128)(2,1)}, bf16[128,3072]{1,0:T(8,128)(2,1)}, bf16[128...) custom-call(bf16[32,3072]{1,0:T(8,128)(2,1)} %bitcast.15, ...), custom_call_target="tpu_custom_call" | custom-call | tf_op jit(solution)/shard_map/chain/pallas_call | solution.py:484
  59.2 1.1 %collective-permute-start = (f32[48,3072]{1,0:T(8,128)}, f32[48,3072]{1,0:T(8,128)}, u32[]{:S(2)}, u32[]{:S(2)}) collective-permute-start(f32[48,3072]{1,0:T(8,128)} %get-tuple-element.49), channel_id=1, source_target_pairs={{0,2},{1,3},{2,0},{3,1},{4,6},{5,7},{6,4},{7,5}} | collective-permute-start | bytes 1769480 | tf_op jit(solution)/shard_map/ppermute | solution.py:673
  60.3 14.9 %grads_first.1 = (f32[2048,3072]{1,0:T(8,128)}, f32[3072,768]{1,0:T(8,128)}, f32[3072,256]{1,0:T(8,128)}, f32[3072,256]{1,0:T(8,128)}) custom-call(bf16[128,2048]{1,0:T(8,128)(2,1)} %get-tuple-element.39.act_hbm, bf16[128,3072]{1,0:T(8,128)(2,1)} %get-tuple-element.40.dy_hbm, bf16[128,3072]{1,0:T(8,128)(2,1)} %get-tuple-element.41.h1_hbm, ...), custom_call_target="tpu_custom_call" | custom-call | flops 2617245696 | bytes 40894464 | tf_op jit(solution)/shard_map/grads_first/pallas_call | solution.py:624
  75.2 0.0 collective-permute-done.recv_hbm
  75.2 13.4 %grads_second.1 = (bf16[32,3072]{1,0:T(8,128)(2,1)}, bf16[32,3072]{1,0:T(8,128)(2,1)}, f32[48,128]{1,0:T(8,128)}, f32[1,3072]{1,0:T(1,128)}, f32[1,3072]{1,0:T(1...) custom-call(f32[2048,3072]{1,0:T(8,128)} %get-tuple-element.38.order, bf16[128,3072]{1,0:T(8,128)(2,1)} %get-tuple-element.44.h2_hbm, ...), custom_call_target="tpu_custom_call" | custom-call | flops 2214592512 | bytes 34603008 | tf_op jit(solution)/shard_map/grads_second/pallas_call | solution.py:646
  88.6 0.3 collective-permute-start.3
  88.9 1.1 %collective-permute-start.2 = (f32[48,128]{1,0:T(8,128)}, f32[48,128]{1,0:T(8,128)S(1)}, u32[]{:S(2)}, u32[]{:S(2)}) collective-permute-start(f32[48,128]{1,0:T(8,128)} %get-tuple-element.58), channel_id=1, source_target_pairs={{0,2},{1,3},{2,0},{3,1},{4,6},{5,7},{6,4},{7,5}} | collective-permute-start | bytes 73736 | tf_op jit(solution)/shard_map/ppermute | solution.py:673
  90.0 0.6 collective-permute-start.1
  90.5 1.5 %collective-permute-done.3 = f32[48,128]{1,0:T(8,128)S(1)} collective-permute-done((f32[48,128]{1,0:T(8,128)}, f32[48,128]{1,0:T(8,128)S(1)}, u32[]{:S(2)}, u32[]{:S(2)}) %collective-permute-start.3) | collective-permute-done | bytes 24608 | tf_op jit(solution)/shard_map/ppermute | solution.py:673
  92.0 0.8 collective-permute-done.2
  92.8 0.0 collective-permute-done.1
  92.8 0.7 add_add_fusion
  93.6 0.6 slice_bitcast_fusion
Async XLA Ops:
  59.2 16.0 %collective-permute-start = (f32[48,3072]{1,0:T(8,128)}, f32[48,3072]{1,0:T(8,128)}, u32[]{:S(2)}, u32[]{:S(2)}) collective-permute-start(f32[48,3072]{1,0:T(8,128)} %get-tuple-element.49), channel_id=1, source_target_pairs={{0,2},{1,3},{2,0},{3,1},{4,6},{5,7},{6,4},{7,5}} | collective-permute-start | bytes 1769480 | tf_op jit(solution)/shard_map/ppermute | solution.py:673
  88.6 3.4 %collective-permute-start.3 = (f32[48,128]{1,0:T(8,128)}, f32[48,128]{1,0:T(8,128)S(1)}, u32[]{:S(2)}, u32[]{:S(2)}) collective-permute-start(f32[48,128]{1,0:T(8,128)} %get-tuple-element.58), channel_id=1, source_target_pairs={{0,3},{1,2},{2,1},{3,0},{4,7},{5,6},{6,5},{7,4}} | collective-permute-start | bytes 73736 | tf_op jit(solution)/shard_map/ppermute | solution.py:673
  88.9 4.0 %collective-permute-start.2 = (f32[48,128]{1,0:T(8,128)}, f32[48,128]{1,0:T(8,128)S(1)}, u32[]{:S(2)}, u32[]{:S(2)}) collective-permute-start(f32[48,128]{1,0:T(8,128)} %get-tuple-element.58), channel_id=1, source_target_pairs={{0,2},{1,3},{2,0},{3,1},{4,6},{5,7},{6,4},{7,5}} | collective-permute-start | bytes 73736 | tf_op jit(solution)/shard_map/ppermute | solution.py:673
  90.0 2.9 %collective-permute-start.1 = (f32[48,128]{1,0:T(8,128)}, f32[48,128]{1,0:T(8,128)S(1)}, u32[]{:S(2)}, u32[]{:S(2)}) collective-permute-start(f32[48,128]{1,0:T(8,128)} %get-tuple-element.58), channel_id=1, source_target_pairs={{0,1},{1,0},{2,3},{3,2},{4,5},{5,4},{6,7},{7,6}} | collective-permute-start | bytes 73736 | tf_op jit(solution)/shard_map/ppermute | solution.py:673

commit v6 on v5

--- a/solution.py
+++ b/solution.py
@@ -72,7 +72,7 @@
     grp = nq // nk
     half = rows // 2
     me = lax.axis_index("tp")
-    part, peer, diag = me ^ 1, me ^ 2, me ^ 3
+    part, peer, diag = me ^ 1, me ^ 3, me ^ 2
     sems = Sems()
 
     def block(idx, sub=None):
@@ -189,20 +189,20 @@
                 def _():
                     self.ahead(i).start()
 
-        def run(self, chunk, drain=True):
+        def run(self, chunk, lag=0):
             def step(i, carry):
                 self.partial[:, self.cols(i)] = chunk(self.cols(i))
                 self.pair(i, 0).start()
                 self.pair(i, 1).start()
-                if drain:
-                    @pl.when(i > 0)
+                if lag:
+                    @pl.when(i >= lag)
                     def _():
-                        self.chip_sum(i - 1)
+                        self.chip_sum(i - lag)
                 return carry
 
             lax.fori_loop(0, self.chunks, step, 0)
-            if drain:
-                self.drain(self.chunks - 1)
+            if lag:
+                self.drain(self.chunks - lag)
 
         def drain(self, start=0):
             for i in range(start, self.chunks):
@@ -248,7 +248,7 @@
     pl.semaphore_wait(barrier, 2)
     gather_h1 = Gather(h1, [(0, rows) + cut for cut in cuts(d, (4, 3, 3, 2))])
     gather_dy = Gather(dyf, [(0, rows, 0, d)])
-    late = [(0, half, 0, d)] + [(half, half) + cut for cut in cuts(d, (2, 1))]
+    late = [(0, half, 0, d)] + [(half, half) + cut for cut in cuts(d, (1, 1))]
     for i in range(len(gather_h1.pieces)):
         gather_h1.send(i)
     dy_in.wait()
@@ -301,8 +301,8 @@
             ctx[:, lo:lo + hd] = head_ctx[g * seq:(g + 1) * seq, :]
     put(ctx, ctx_out)
     weight_in[3].wait()
-    sum_attn = Scatter(4, part_a, dr_a, snd_a, lnk_a, rows)
-    sum_attn.run(lambda cols: mm(ctx[...], wo[:, cols]))
+    sum_attn = Scatter(6, part_a, dr_a, snd_a, lnk_a, rows)
+    sum_attn.run(lambda cols: mm(ctx[...], wo[:, cols]), lag=2)
 
     gather_dy.forward(0)
     gather_dy.finish(0)
@@ -333,27 +333,26 @@
     weight_in[5].wait()
 
     def up(j, depth):
-        for i in range(f // nb):
-            cols = pl.ds(i * nb, nb)
-            piece = mm(h2[:, depth], w1[depth, cols])
-            if j == 0:
-                part_c[:, cols] = piece
-            elif j < len(late) - 2:
-                part_c[:, cols] += piece
-            else:
-                relu_up = jnp.maximum((part_c[:, cols] + piece).astype(BF16).astype(F32), 0.0)
-                act[:, cols] = (relu_up * relu_up).astype(BF16)
-                du[:, cols] = (tmat[:, cols] * (2.0 * relu_up)).astype(BF16)
+        cols = pl.ds(0, f)
+        piece = mm(h2[:, depth], w1[depth, :])
+        if j == 0:
+            part_c[:, cols] = piece
+        elif j < len(late) - 2:
+            part_c[:, cols] += piece
+        else:
+            relu_up = jnp.maximum((part_c[:, cols] + piece).astype(BF16).astype(F32), 0.0)
+            act[...] = (relu_up * relu_up).astype(BF16)
+            du[...] = (tmat[...] * (2.0 * relu_up)).astype(BF16)
 
     gather_h2.feed(1, up)
     put(h2, h2_out)
     put(act, act_out)
     put(du, du_out)
-    sum_dh2 = Scatter(6, part_b, dr_b, snd_b, lnk_b, rows, 2)
-    sum_dh2.run(lambda cols: mm_bt(du[...], w1[cols, :]))
+    sum_dh2 = Scatter(12, part_b, dr_b, snd_b, lnk_b, rows, 4)
+    sum_dh2.run(lambda cols: mm_bt(du[...], w1[cols, :]), lag=2)
 
     sum_mlp = Scatter(4, part_c, dr_c, snd_c, lnk_c, half)
-    sum_mlp.run(lambda cols: mm(act[...], w2[:, cols]), drain=False)
+    sum_mlp.run(lambda cols: mm(act[...], w2[:, cols]))
 
     gather_dx1 = Gather(dx1, late)
     normed2, scale2 = centre(mid[...].astype(F32))
@@ -409,9 +408,9 @@
         lo = nqd + nkd + k * hd
         dqkv[:, lo:lo + hd] = grad_v
     put(dqkv, dqkv_out)
-    sum_dh1 = Scatter(4, part_a, dr_d, send.at[pl.ds(0, rows)])
+    sum_dh1 = Scatter(2, part_a, dr_d, send.at[pl.ds(0, rows)])
     sum_attn.pair_sent()
-    sum_dh1.run(lambda cols: mm_bt(dqkv[...], wqkv[cols, :]), drain=False)
+    sum_dh1.run(lambda cols: mm_bt(dqkv[...], wqkv[cols, :]))
     sum_dh1.drain()
     put(send, send_out)
     sum_dh1.kept()
@@ -466,7 +465,7 @@
         return pltpu.VMEM(shape, F32)
 
     out_shape = [arr((seq, d), BF16)] * 4 + [arr((seq, f), BF16)] * 2 + [arr((seq, nqd), BF16), arr((seq, n_all), BF16)] + [arr((half, d), BF16)] * 2 + [arr((rows, d), BF16), arr((rows + half, d), F32), arr((rows, d), F32), arr((half, d), F32)] + [arr((1, d), F32)] * 2
-    n_sems = 3 * (4 + 1 + 3 + 3) + 2 * (4 + 6 + 4 + 4) + (5 + 9 + 5) + 2
+    n_sems = 3 * (4 + 1 + 3 + 3) + 2 * (6 + 12 + 4 + 2) + (7 + 17 + 5) + 2
     scratch = [
         pltpu.VMEM((1, seq), jnp.int32), vf(1, hd), vf(1, d), vf(1, d), vf(1, d), vf(1, d),
         vm(d, n_all), vm(nqd, d), vm(d, f), vm(f, d),
@@ -556,7 +555,11 @@
         copy.start()
 
     def ready(*which):
-        return lambda: [loads[i].wait() for i in which] and None
+        def wait():
+            for i in which:
+                loads[i].wait()
+
+        return wait
 
     return ready
 
@@ -672,11 +675,12 @@
     def swap(v, bit):
         return lax.ppermute(v, 'tp', [(i, i ^ bit) for i in range(n_tp)])
 
-    recv = swap(send, 2)
+    recv = swap(send, 3)
     dw2, dwq, dwk, dwv = grads_first(dims, act, dyf, h1, dqkv)
     y, dx, lng, dg2, db2, dw1, dwo = grads_second(dims, dw2, h2, du, ctx, dx1, hkeep, recv, x2, dmid, g1, dg2, db2, ykeep, mid, y)
     others = [swap(lng, bit) for bit in (1, 2, 3)]
-    sums = ((lng + others[0]) + (others[1] + others[2])).reshape(2, d)
+    half = lng.shape[0] // 2
+    sums = [((lng[at] + others[0][at]) + (others[1][at] + others[2][at])).reshape(d) for at in (slice(0, half), slice(half, None))]
     return (y.reshape(x.shape), dx.reshape(x.shape), sums[0], sums[1], dg2.reshape(d), db2.reshape(d), dwq, dwk, dwv, dwo, dw1, dw2)
 
 

time: 94.4 us -> 94.4 us (level)
    reshape x0 -> x1, other arithmetic: none -> 1.34 us  [layer_step(): (lng[at] + others[0][at] + (others[1][at] + others[2][at])).reshape(d)]
where the time goes in v6:
time: 94.4 us; the launch traced here: 94.2 us
  Pallas kernels  86.5 us (92%)
  waiting for transfers between devices  3.05 us (3%)
  starting transfers between devices  2.57 us (3%)
  other arithmetic  1.34 us (1%)
    pallas_call x1, Pallas kernels, chain(): pl.pallas_call(functools.partial(chain_kernel, dims), out_shape=out_shape...  58.2 us
    pallas_call x1, Pallas kernels, grads_first(): pl.pallas_call(functools.partial(grads_first_kernel, dims), out_shape=[ar...  14.9 us
    pallas_call x1, Pallas kernels, grads_second(): pl.pallas_call(functools.partial(grads_second_kernel, dims), out_shape=[a...  13.4 us
    ppermute x4, waiting for transfers between devices, swap(): return lax.ppermute(v, 'tp', [(i, i ^ bit) for i in range(n_tp)])  3.05 us
    ppermute x4, starting transfers between devices, swap(): return lax.ppermute(v, 'tp', [(i, i ^ bit) for i in range(n_tp)])  2.57 us
  transfers between devices with their start and end apart: 4, of which 2 were waited for; matrix products, arithmetic and copies ran while one was open for 0% of the time, Pallas kernels for 16%

profile of v6, /device:TPU:0, one launch (start us, length us, event | category | flops | bytes accessed | tf_op | source)
XLA Modules:
  0.0 94.2 jit_solution(12330687000806400487)
XLA Ops:
  0.6 58.2 %chain.1 = (bf16[128,3072]{1,0:T(8,128)(2,1)}, bf16[128,3072]{1,0:T(8,128)(2,1)}, bf16[128,3072]{1,0:T(8,128)(2,1)}, bf16[128,3072]{1,0:T(8,128)(2,1)}, bf16[128...) custom-call(bf16[32,3072]{1,0:T(8,128)(2,1)} %bitcast.15, ...), custom_call_target="tpu_custom_call" | custom-call | tf_op jit(solution)/shard_map/chain/pallas_call | solution.py:483
  58.9 0.7 collective-permute-start
  59.6 14.9 %grads_first.1 = (f32[2048,3072]{1,0:T(8,128)}, f32[3072,768]{1,0:T(8,128)}, f32[3072,256]{1,0:T(8,128)}, f32[3072,256]{1,0:T(8,128)}) custom-call(bf16[128,2048]{1,0:T(8,128)(2,1)} %get-tuple-element.39.act_hbm, bf16[128,3072]{1,0:T(8,128)(2,1)} %get-tuple-element.40.dy_hbm, bf16[128,3072]{1,0:T(8,128)(2,1)} %get-tuple-element.41.h1_hbm, ...), custom_call_target="tpu_custom_call" | custom-call | flops 2617245696 | bytes 40894464 | tf_op jit(solution)/shard_map/grads_first/pallas_call | solution.py:627
  74.5 0.0 collective-permute-done.recv_hbm
  74.5 13.4 %grads_second.1 = (bf16[32,3072]{1,0:T(8,128)(2,1)}, bf16[32,3072]{1,0:T(8,128)(2,1)}, f32[48,128]{1,0:T(8,128)}, f32[1,3072]{1,0:T(1,128)}, f32[1,3072]{1,0:T(1...) custom-call(f32[2048,3072]{1,0:T(8,128)} %get-tuple-element.38.order, bf16[128,3072]{1,0:T(8,128)(2,1)} %get-tuple-element.44.h2_hbm, ...), custom_call_target="tpu_custom_call" | custom-call | flops 2214592512 | bytes 34603008 | tf_op jit(solution)/shard_map/grads_second/pallas_call | solution.py:649
  87.9 1.1 %collective-permute-start.3 = (f32[48,128]{1,0:T(8,128)}, f32[48,128]{1,0:T(8,128)S(1)}, u32[]{:S(2)}, u32[]{:S(2)}) collective-permute-start(f32[48,128]{1,0:T(8,128)} %get-tuple-element.58), channel_id=1, source_target_pairs={{0,3},{1,2},{2,1},{3,0},{4,7},{5,6},{6,5},{7,4}} | collective-permute-start | bytes 73736 | tf_op jit(solution)/shard_map/ppermute | solution.py:676
  89.0 0.6 collective-permute-start.2
  89.6 0.2 collective-permute-start.1
  89.8 1.4 %collective-permute-done.3 = f32[48,128]{1,0:T(8,128)S(1)} collective-permute-done((f32[48,128]{1,0:T(8,128)}, f32[48,128]{1,0:T(8,128)S(1)}, u32[]{:S(2)}, u32[]{:S(2)}) %collective-permute-start.3) | collective-permute-done | bytes 24608 | tf_op jit(solution)/shard_map/ppermute | solution.py:676
  91.2 1.6 %collective-permute-done.2 = f32[48,128]{1,0:T(8,128)S(1)} collective-permute-done((f32[48,128]{1,0:T(8,128)}, f32[48,128]{1,0:T(8,128)S(1)}, u32[]{:S(2)}, u32[]{:S(2)}) %collective-permute-start.2) | collective-permute-done | bytes 24608 | tf_op jit(solution)/shard_map/ppermute | solution.py:676
  92.8 0.0 collective-permute-done.1
  92.8 1.3 %fusion.1 = (f32[3072]{0:T(1024)}, f32[3072]{0:T(1024)}) fusion(f32[48,128]{1,0:T(8,128)S(1)} %collective-permute-done.3, f32[48,128]{1,0:T(8,128)S(1)} %collective-permute-done.2, f32[48,128]{1,0:T(8,128)S(1)} %collective-permute-done.1, f32[48,128]{1,0:T(8,128)} %get-tuple-element.58), kind=kLoop, calls=%fused_computation.2 | loop fusion | flops 18432 | bytes 122880 | tf_op jit(solution)/shard_map/reshape | solution.py:683
Async XLA Ops:
  58.9 15.6 %collective-permute-start = (f32[48,3072]{1,0:T(8,128)}, f32[48,3072]{1,0:T(8,128)}, u32[]{:S(2)}, u32[]{:S(2)}) collective-permute-start(f32[48,3072]{1,0:T(8,128)} %get-tuple-element.49), channel_id=1, source_target_pairs={{0,3},{1,2},{2,1},{3,0},{4,7},{5,6},{6,5},{7,4}} | collective-permute-start | bytes 1769480 | tf_op jit(solution)/shard_map/ppermute | solution.py:676
  87.9 3.3 %collective-permute-start.3 = (f32[48,128]{1,0:T(8,128)}, f32[48,128]{1,0:T(8,128)S(1)}, u32[]{:S(2)}, u32[]{:S(2)}) collective-permute-start(f32[48,128]{1,0:T(8,128)} %get-tuple-element.58), channel_id=1, source_target_pairs={{0,3},{1,2},{2,1},{3,0},{4,7},{5,6},{6,5},{7,4}} | collective-permute-start | bytes 73736 | tf_op jit(solution)/shard_map/ppermute | solution.py:676
  89.0 3.8 %collective-permute-start.2 = (f32[48,128]{1,0:T(8,128)}, f32[48,128]{1,0:T(8,128)S(1)}, u32[]{:S(2)}, u32[]{:S(2)}) collective-permute-start(f32[48,128]{1,0:T(8,128)} %get-tuple-element.58), channel_id=1, source_target_pairs={{0,2},{1,3},{2,0},{3,1},{4,6},{5,7},{6,4},{7,5}} | collective-permute-start | bytes 73736 | tf_op jit(solution)/shard_map/ppermute | solution.py:676
  89.6 3.2 %collective-permute-start.1 = (f32[48,128]{1,0:T(8,128)}, f32[48,128]{1,0:T(8,128)S(1)}, u32[]{:S(2)}, u32[]{:S(2)}) collective-permute-start(f32[48,128]{1,0:T(8,128)} %get-tuple-element.58), channel_id=1, source_target_pairs={{0,1},{1,0},{2,3},{3,2},{4,5},{5,4},{6,7},{7,6}} | collective-permute-start | bytes 73736 | tf_op jit(solution)/shard_map/ppermute | solution.py:676

commit v7 on v6

--- a/solution.py
+++ b/solution.py
@@ -574,14 +574,14 @@
         stage, sem)
 
 
-def grads_second_kernel(dims, order, h2_hbm, du_hbm, ctx_hbm, dx1_hbm, hkeep_hbm, recv_hbm, x_hbm, dmid_hbm, g1_hbm, dg2_hbm, db2_hbm, ykeep_hbm, mid_hbm, y_hbm,
-                        y_out, dx_out, lng_out, dg2_out, db2_out, dw1, dwo,
-                        h2, du, ctx, dx1, hkeep, recv, x, dmid, g1, ykeep, mid, y, lng, dg2, db2, stage, in_sem, end_sem, sem):
+def grads_second_kernel(dims, order, h2_hbm, du_hbm, hkeep_hbm, recv_hbm, x_hbm, dmid_hbm, g1_hbm, dg2_hbm, db2_hbm, ykeep_hbm, mid_hbm, y_hbm,
+                        y_out, dx_out, lng_out, dg2_out, db2_out, dw1,
+                        h2, du, hkeep, recv, x, dmid, g1, ykeep, mid, y, lng, dg2, db2, stage, in_sem, end_sem, sem):
     seq, d, hd, nq, nk, f, rows = dims
     half = rows // 2
     top, low = pl.ds(0, half), pl.ds(half, half)
     ready = start_loads(((h2_hbm, h2), (du_hbm, du), (hkeep_hbm, hkeep), (recv_hbm, recv), (x_hbm, x), (dmid_hbm, dmid), (g1_hbm, g1),
-                         (dg2_hbm, dg2), (db2_hbm, db2), (ykeep_hbm, ykeep), (mid_hbm, mid), (y_hbm, y.at[top]), (ctx_hbm, ctx), (dx1_hbm, dx1)), in_sem)
+                         (dg2_hbm, dg2), (db2_hbm, db2), (ykeep_hbm, ykeep), (mid_hbm, mid), (y_hbm, y.at[top])), in_sem)
     ends = [pltpu.make_async_copy(src, dst, end_sem.at[i]) for i, (src, dst) in enumerate(((y, y_out), (dmid, dx_out), (lng, lng_out), (dg2, dg2_out), (db2, db2_out)))]
 
     def first_norm_back():
@@ -605,11 +605,15 @@
 
     lead = SLOTS * TILE
     stream_grads(
-        dw1_jobs(ready(0, 1), 0, lead) + dw1_jobs(first_norm_back, lead, d - lead)
-        + outer_jobs(ready(12, 13), ctx, dx1, lambda at: [(dwo.at[at], 0, d)], ctx.shape[1]),
+        dw1_jobs(ready(0, 1), 0, lead) + dw1_jobs(first_norm_back, lead, d - lead),
         stage, sem)
     for copy in ends:
         copy.wait()
+
+
+def grads_third_kernel(order, ctx_hbm, dx1_hbm, dwo, ctx, dx1, stage, in_sem, sem):
+    ready = start_loads(((ctx_hbm, ctx), (dx1_hbm, dx1)), in_sem)
+    stream_grads(outer_jobs(ready(0, 1), ctx, dx1, lambda at: [(dwo.at[at], 0, dx1.shape[1])], ctx.shape[1], TILE), stage, sem)
 
 
 def cost(flops, nbytes):
@@ -636,9 +640,9 @@
     )(act, dyf, h1, dqkv)
 
 
-def grads_second(dims, order, h2, du, ctx, dx1, hkeep, recv, x, dmid, g1, dg2, db2, ykeep, mid, y):
+def grads_second(dims, order, h2, du, hkeep, recv, x, dmid, g1, dg2, db2, ykeep, mid, y):
     seq, d, hd, nq, nk, f, rows = dims
-    nqd, half = nq * hd, rows // 2
+    half = rows // 2
 
     def vb(*shape):
         return pltpu.VMEM(shape, BF16)
@@ -648,15 +652,30 @@
 
     return pl.pallas_call(
         functools.partial(grads_second_kernel, dims),
-        out_shape=[arr((rows, d), BF16), arr((rows, d), BF16), arr((2 * d // 128, 128)), arr((1, d)), arr((1, d)), arr((d, f)), arr((nqd, d))],
-        in_specs=[ANY] * 15, out_specs=[ANY] * 7,
-        scratch_shapes=[vb(seq, d), vb(seq, f), vb(seq, nqd), vb(seq, d), vf(rows, d), vf(rows + half, d), vb(rows, d), vb(rows, d), vf(1, d),
+        out_shape=[arr((rows, d), BF16), arr((rows, d), BF16), arr((2 * d // 128, 128)), arr((1, d)), arr((1, d)), arr((d, f))],
+        in_specs=[ANY] * 13, out_specs=[ANY] * 6,
+        scratch_shapes=[vb(seq, d), vb(seq, f), vf(rows, d), vf(rows + half, d), vb(rows, d), vb(rows, d), vf(1, d),
                         vf(half, d), vb(half, d), vb(rows, d), vf(2 * d // 128, 128), vf(1, d), vf(1, d),
-                        vf(SLOTS, TILE, d), pltpu.SemaphoreType.DMA((14,)), pltpu.SemaphoreType.DMA((5,)), pltpu.SemaphoreType.DMA((SLOTS, 3))],
+                        vf(SLOTS, TILE, f), pltpu.SemaphoreType.DMA((12,)), pltpu.SemaphoreType.DMA((5,)), pltpu.SemaphoreType.DMA((SLOTS, 3))],
         compiler_params=pltpu.CompilerParams(vmem_limit_bytes=VMEM_LIMIT),
-        cost_estimate=cost(2 * seq * d * (f + nqd), 4 * d * (f + nqd)),
+        cost_estimate=cost(2 * seq * d * f, 4 * d * f),
         name="grads_second",
-    )(order, h2, du, ctx, dx1, hkeep, recv, x, dmid, g1, dg2, db2, ykeep, mid, y)
+    )(order, h2, du, hkeep, recv, x, dmid, g1, dg2, db2, ykeep, mid, y)
+
+
+def grads_third(dims, order, ctx, dx1):
+    seq, d, hd, nq, nk, f, rows = dims
+    nqd = nq * hd
+    return pl.pallas_call(
+        grads_third_kernel,
+        out_shape=arr((nqd, d)),
+        in_specs=[ANY] * 3, out_specs=ANY,
+        scratch_shapes=[pltpu.VMEM((seq, nqd), BF16), pltpu.VMEM((seq, d), BF16), pltpu.VMEM((SLOTS, TILE, d), F32),
+                        pltpu.SemaphoreType.DMA((2,)), pltpu.SemaphoreType.DMA((SLOTS, 3))],
+        compiler_params=pltpu.CompilerParams(vmem_limit_bytes=VMEM_LIMIT),
+        cost_estimate=cost(2 * seq * d * nqd, 4 * d * nqd),
+        name="grads_third",
+    )(order, ctx, dx1)
 
 
 def layer_step(x, dy, positions, g1, b1, g2, b2, wq, wk, wv, wo, w1, w2, head_dim, n_tp):
@@ -677,8 +696,9 @@
 
     recv = swap(send, 3)
     dw2, dwq, dwk, dwv = grads_first(dims, act, dyf, h1, dqkv)
-    y, dx, lng, dg2, db2, dw1, dwo = grads_second(dims, dw2, h2, du, ctx, dx1, hkeep, recv, x2, dmid, g1, dg2, db2, ykeep, mid, y)
+    y, dx, lng, dg2, db2, dw1 = grads_second(dims, dw2, h2, du, hkeep, recv, x2, dmid, g1, dg2, db2, ykeep, mid, y)
     others = [swap(lng, bit) for bit in (1, 2, 3)]
+    dwo = grads_third(dims, lng, ctx, dx1)
     half = lng.shape[0] // 2
     sums = [((lng[at] + others[0][at]) + (others[1][at] + others[2][at])).reshape(d) for at in (slice(0, half), slice(half, None))]
     return (y.reshape(x.shape), dx.reshape(x.shape), sums[0], sums[1], dg2.reshape(d), db2.reshape(d), dwq, dwk, dwv, dwo, dw1, dw2)

time: 94.4 us -> 94.1 us (level)
  waiting for transfers between devices: 3.05 us -> 0.01 us
  Pallas kernels: 86.5 us -> 89.1 us
    pallas_call x0 -> x1, Pallas kernels: none -> 5.49 us  [grads_third(): pl.pallas_call(grads_third_kernel, out_shape=arr((nqd, d)), in_specs=[ANY...]
    ppermute x4, waiting for transfers between devices: 3.05 us -> 0.01 us  [swap(): return lax.ppermute(v, 'tp', [(i, i ^ bit) for i in range(n_tp)])]
    pallas_call x1, Pallas kernels: 13.4 us -> 10.5 us  [grads_second(): pl.pallas_call(functools.partial(grads_second_kernel, dims), out_shape=[a...]
  transfers between devices with their start and end apart: 4 -> 4, of which waited for: 2 -> 0; matrix products, arithmetic and copies ran while one was open for 0% -> 0% of each run, Pallas kernels for 16% -> 22%
where the time goes in v7:
time: 94.1 us; the launch traced here: 93.9 us
  Pallas kernels  89.1 us (95%)
  starting transfers between devices  2.56 us (3%)
  other arithmetic  1.44 us (2%)
    pallas_call x1, Pallas kernels, chain(): pl.pallas_call(functools.partial(chain_kernel, dims), out_shape=out_shape...  58.2 us
    pallas_call x1, Pallas kernels, grads_first(): pl.pallas_call(functools.partial(grads_first_kernel, dims), out_shape=[ar...  14.9 us
    pallas_call x1, Pallas kernels, grads_second(): pl.pallas_call(functools.partial(grads_second_kernel, dims), out_shape=[a...  10.5 us
    pallas_call x1, Pallas kernels, grads_third(): pl.pallas_call(grads_third_kernel, out_shape=arr((nqd, d)), in_specs=[ANY...  5.49 us
    ppermute x4, starting transfers between devices, swap(): return lax.ppermute(v, 'tp', [(i, i ^ bit) for i in range(n_tp)])  2.56 us
  transfers between devices with their start and end apart: 4, of which 0 were waited for; matrix products, arithmetic and copies ran while one was open for 0% of the time, Pallas kernels for 22%

profile of v7, /device:TPU:0, one launch (start us, length us, event | category | flops | bytes accessed | tf_op | source)
XLA Modules:
  0.0 93.9 jit_solution(1871004882128382600)
XLA Ops:
  0.6 58.2 %chain.1 = (bf16[128,3072]{1,0:T(8,128)(2,1)}, bf16[128,3072]{1,0:T(8,128)(2,1)}, bf16[128,3072]{1,0:T(8,128)(2,1)}, bf16[128,3072]{1,0:T(8,128)(2,1)}, bf16[128...) custom-call(bf16[32,3072]{1,0:T(8,128)(2,1)} %bitcast.15, ...), custom_call_target="tpu_custom_call" | custom-call | tf_op jit(solution)/shard_map/chain/pallas_call | solution.py:483
  58.9 0.7 collective-permute-start
  59.6 14.9 %grads_first.1 = (f32[2048,3072]{1,0:T(8,128)}, f32[3072,768]{1,0:T(8,128)}, f32[3072,256]{1,0:T(8,128)}, f32[3072,256]{1,0:T(8,128)}) custom-call(bf16[128,2048]{1,0:T(8,128)(2,1)} %get-tuple-element.38.act_hbm, bf16[128,3072]{1,0:T(8,128)(2,1)} %get-tuple-element.39.dy_hbm, bf16[128,3072]{1,0:T(8,128)(2,1)} %get-tuple-element.40.h1_hbm, ...), custom_call_target="tpu_custom_call" | custom-call | flops 2617245696 | bytes 40894464 | tf_op jit(solution)/shard_map/grads_first/pallas_call | solution.py:631
  74.5 0.0 collective-permute-done.recv_hbm
  74.5 10.5 %grads_second.1 = (bf16[32,3072]{1,0:T(8,128)(2,1)}, bf16[32,3072]{1,0:T(8,128)(2,1)}, f32[48,128]{1,0:T(8,128)}, f32[1,3072]{1,0:T(1,128)}, f32[1,3072]{1,0:T(1,128)}, /*index=5*/f32[3072,2048]{1,0:T(8,128)}) custom-call(f32[2048,3072]{1,0:T(8,128)} %get-tuple-element.37.order, bf16[128,3072]{1,0:T(8,128)(2,1)} %get-tuple-element.43.h2_hbm, ...), custom_call_target="tpu_custom_call" | custom-call | flops 1610612736 | bytes 25165824 | tf_op jit(solution)/shard_map/grads_second/pallas_call | solution.py:653
  85.0 0.1 collective-permute-start.1
  85.1 1.4 %collective-permute-start.2 = (f32[48,128]{1,0:T(8,128)}, f32[48,128]{1,0:T(8,128)}, u32[]{:S(2)}, u32[]{:S(2)}) collective-permute-start(f32[48,128]{1,0:T(8,128)} %get-tuple-element.55.order), channel_id=1, source_target_pairs={{0,2},{1,3},{2,0},{3,1},{4,6},{5,7},{6,4},{7,5}} | collective-permute-start | bytes 73736 | tf_op jit(solution)/shard_map/ppermute | solution.py:695
  86.5 0.4 collective-permute-start.3
  86.9 5.5 %grads_third.1 = f32[768,3072]{1,0:T(8,128)} custom-call(f32[48,128]{1,0:T(8,128)} %get-tuple-element.55.order, bf16[128,768]{1,0:T(8,128)(2,1)} %get-tuple-element.61.ctx_hbm, bf16[128,3072]{1,0:T(8,128)(2,1)} %get-tuple-element.62.dx1_hbm), custom_call_target="tpu_custom_call" | custom-call | flops 603979776 | bytes 9437184 | tf_op jit(solution)/shard_map/grads_third/pallas_call | solution.py:669
  92.4 0.0 collective-permute-done.1
  92.4 0.0 collective-permute-done.2
  92.4 0.0 collective-permute-done.3
  92.4 1.4 %fusion.1 = (f32[3072]{0:T(1024)}, f32[3072]{0:T(1024)}) fusion(f32[48,128]{1,0:T(8,128)} %collective-permute-done.3, f32[48,128]{1,0:T(8,128)} %collective-permute-done.2, f32[48,128]{1,0:T(8,128)} %collective-permute-done.1, f32[48,128]{1,0:T(8,128)} %get-tuple-element.55.order), kind=kLoop, calls=%fused_computation.2 | loop fusion | flops 18432 | bytes 122880 | tf_op jit(solution)/shard_map/reshape | solution.py:703
Async XLA Ops:
  58.9 15.6 %collective-permute-start = (f32[48,3072]{1,0:T(8,128)}, f32[48,3072]{1,0:T(8,128)}, u32[]{:S(2)}, u32[]{:S(2)}) collective-permute-start(f32[48,3072]{1,0:T(8,128)} %get-tuple-element.46), channel_id=1, source_target_pairs={{0,3},{1,2},{2,1},{3,0},{4,7},{5,6},{6,5},{7,4}} | collective-permute-start | bytes 1769480 | tf_op jit(solution)/shard_map/ppermute | solution.py:695
  85.0 7.4 %collective-permute-start.1 = (f32[48,128]{1,0:T(8,128)}, f32[48,128]{1,0:T(8,128)}, u32[]{:S(2)}, u32[]{:S(2)}) collective-permute-start(f32[48,128]{1,0:T(8,128)} %get-tuple-element.55.order), channel_id=1, source_target_pairs={{0,1},{1,0},{2,3},{3,2},{4,5},{5,4},{6,7},{7,6}} | collective-permute-start | bytes 73736 | tf_op jit(solution)/shard_map/ppermute | solution.py:695
  85.1 7.3 %collective-permute-start.2 = (f32[48,128]{1,0:T(8,128)}, f32[48,128]{1,0:T(8,128)}, u32[]{:S(2)}, u32[]{:S(2)}) collective-permute-start(f32[48,128]{1,0:T(8,128)} %get-tuple-element.55.order), channel_id=1, source_target_pairs={{0,2},{1,3},{2,0},{3,1},{4,6},{5,7},{6,4},{7,5}} | collective-permute-start | bytes 73736 | tf_op jit(solution)/shard_map/ppermute | solution.py:695
  86.5 5.9 %collective-permute-start.3 = (f32[48,128]{1,0:T(8,128)}, f32[48,128]{1,0:T(8,128)}, u32[]{:S(2)}, u32[]{:S(2)}) collective-permute-start(f32[48,128]{1,0:T(8,128)} %get-tuple-element.55.order), channel_id=1, source_target_pairs={{0,3},{1,2},{2,1},{3,0},{4,7},{5,6},{6,5},{7,4}} | collective-permute-start | bytes 73736 | tf_op jit(solution)/shard_map/ppermute | solution.py:695

commit v8 on v7

--- a/solution.py
+++ b/solution.py
@@ -348,7 +348,7 @@
     put(h2, h2_out)
     put(act, act_out)
     put(du, du_out)
-    sum_dh2 = Scatter(12, part_b, dr_b, snd_b, lnk_b, rows, 4)
+    sum_dh2 = Scatter(8, part_b, dr_b, snd_b, lnk_b, rows, 3)
     sum_dh2.run(lambda cols: mm_bt(du[...], w1[cols, :]), lag=2)
 
     sum_mlp = Scatter(4, part_c, dr_c, snd_c, lnk_c, half)
@@ -465,7 +465,7 @@
         return pltpu.VMEM(shape, F32)
 
     out_shape = [arr((seq, d), BF16)] * 4 + [arr((seq, f), BF16)] * 2 + [arr((seq, nqd), BF16), arr((seq, n_all), BF16)] + [arr((half, d), BF16)] * 2 + [arr((rows, d), BF16), arr((rows + half, d), F32), arr((rows, d), F32), arr((half, d), F32)] + [arr((1, d), F32)] * 2
-    n_sems = 3 * (4 + 1 + 3 + 3) + 2 * (6 + 12 + 4 + 2) + (7 + 17 + 5) + 2
+    n_sems = 3 * (4 + 1 + 3 + 3) + 2 * (6 + 8 + 4 + 2) + (7 + 12 + 5) + 2
     scratch = [
         pltpu.VMEM((1, seq), jnp.int32), vf(1, hd), vf(1, d), vf(1, d), vf(1, d), vf(1, d),
         vm(d, n_all), vm(nqd, d), vm(d, f), vm(f, d),

time: 94.1 us -> 93.8 us (level)
  no operation moved by 1% of the time
where the time goes in v8:
time: 93.8 us; the launch traced here: 93.6 us
  Pallas kernels  88.9 us (95%)
  starting transfers between devices  2.56 us (3%)
  other arithmetic  1.44 us (2%)
    pallas_call x1, Pallas kernels, chain(): pl.pallas_call(functools.partial(chain_kernel, dims), out_shape=out_shape...  58 us
    pallas_call x1, Pallas kernels, grads_first(): pl.pallas_call(functools.partial(grads_first_kernel, dims), out_shape=[ar...  14.9 us
    pallas_call x1, Pallas kernels, grads_second(): pl.pallas_call(functools.partial(grads_second_kernel, dims), out_shape=[a...  10.5 us
    pallas_call x1, Pallas kernels, grads_third(): pl.pallas_call(grads_third_kernel, out_shape=arr((nqd, d)), in_specs=[ANY...  5.49 us
    ppermute x4, starting transfers between devices, swap(): return lax.ppermute(v, 'tp', [(i, i ^ bit) for i in range(n_tp)])  2.56 us
  transfers between devices with their start and end apart: 4, of which 0 were waited for; matrix products, arithmetic and copies ran while one was open for 0% of the time, Pallas kernels for 22%

profile of v8, /device:TPU:0, one launch (start us, length us, event | category | flops | bytes accessed | tf_op | source)
XLA Modules:
  0.0 93.6 jit_solution(16435650539365619360)
XLA Ops:
  0.6 58.0 %chain.1 = (bf16[128,3072]{1,0:T(8,128)(2,1)}, bf16[128,3072]{1,0:T(8,128)(2,1)}, bf16[128,3072]{1,0:T(8,128)(2,1)}, bf16[128,3072]{1,0:T(8,128)(2,1)}, bf16[128...) custom-call(bf16[32,3072]{1,0:T(8,128)(2,1)} %bitcast.15, ...), custom_call_target="tpu_custom_call" | custom-call | tf_op jit(solution)/shard_map/chain/pallas_call | solution.py:483
  58.6 0.7 collective-permute-start
  59.3 14.9 %grads_first.1 = (f32[2048,3072]{1,0:T(8,128)}, f32[3072,768]{1,0:T(8,128)}, f32[3072,256]{1,0:T(8,128)}, f32[3072,256]{1,0:T(8,128)}) custom-call(bf16[128,2048]{1,0:T(8,128)(2,1)} %get-tuple-element.38.act_hbm, bf16[128,3072]{1,0:T(8,128)(2,1)} %get-tuple-element.39.dy_hbm, bf16[128,3072]{1,0:T(8,128)(2,1)} %get-tuple-element.40.h1_hbm, ...), custom_call_target="tpu_custom_call" | custom-call | flops 2617245696 | bytes 40894464 | tf_op jit(solution)/shard_map/grads_first/pallas_call | solution.py:631
  74.2 0.0 collective-permute-done.recv_hbm
  74.2 10.5 %grads_second.1 = (bf16[32,3072]{1,0:T(8,128)(2,1)}, bf16[32,3072]{1,0:T(8,128)(2,1)}, f32[48,128]{1,0:T(8,128)}, f32[1,3072]{1,0:T(1,128)}, f32[1,3072]{1,0:T(1,128)}, /*index=5*/f32[3072,2048]{1,0:T(8,128)}) custom-call(f32[2048,3072]{1,0:T(8,128)} %get-tuple-element.37.order, bf16[128,3072]{1,0:T(8,128)(2,1)} %get-tuple-element.43.h2_hbm, ...), custom_call_target="tpu_custom_call" | custom-call | flops 1610612736 | bytes 25165824 | tf_op jit(solution)/shard_map/grads_second/pallas_call | solution.py:653
  84.7 0.1 collective-permute-start.1
  84.8 1.4 %collective-permute-start.2 = (f32[48,128]{1,0:T(8,128)}, f32[48,128]{1,0:T(8,128)}, u32[]{:S(2)}, u32[]{:S(2)}) collective-permute-start(f32[48,128]{1,0:T(8,128)} %get-tuple-element.55.order), channel_id=1, source_target_pairs={{0,2},{1,3},{2,0},{3,1},{4,6},{5,7},{6,4},{7,5}} | collective-permute-start | bytes 73736 | tf_op jit(solution)/shard_map/ppermute | solution.py:695
  86.2 0.4 collective-permute-start.3
  86.6 5.5 %grads_third.1 = f32[768,3072]{1,0:T(8,128)} custom-call(f32[48,128]{1,0:T(8,128)} %get-tuple-element.55.order, bf16[128,768]{1,0:T(8,128)(2,1)} %get-tuple-element.61.ctx_hbm, bf16[128,3072]{1,0:T(8,128)(2,1)} %get-tuple-element.62.dx1_hbm), custom_call_target="tpu_custom_call" | custom-call | flops 603979776 | bytes 9437184 | tf_op jit(solution)/shard_map/grads_third/pallas_call | solution.py:669
  92.1 0.0 collective-permute-done.1
  92.1 0.0 collective-permute-done.2
  92.1 0.0 collective-permute-done.3
  92.2 1.4 %fusion.1 = (f32[3072]{0:T(1024)}, f32[3072]{0:T(1024)}) fusion(f32[48,128]{1,0:T(8,128)} %collective-permute-done.3, f32[48,128]{1,0:T(8,128)} %collective-permute-done.2, f32[48,128]{1,0:T(8,128)} %collective-permute-done.1, f32[48,128]{1,0:T(8,128)} %get-tuple-element.55.order), kind=kLoop, calls=%fused_computation.2 | loop fusion | flops 18432 | bytes 122880 | tf_op jit(solution)/shard_map/reshape | solution.py:703
Async XLA Ops:
  58.6 15.6 %collective-permute-start = (f32[48,3072]{1,0:T(8,128)}, f32[48,3072]{1,0:T(8,128)}, u32[]{:S(2)}, u32[]{:S(2)}) collective-permute-start(f32[48,3072]{1,0:T(8,128)} %get-tuple-element.46), channel_id=1, source_target_pairs={{0,3},{1,2},{2,1},{3,0},{4,7},{5,6},{6,5},{7,4}} | collective-permute-start | bytes 1769480 | tf_op jit(solution)/shard_map/ppermute | solution.py:695
  84.7 7.4 %collective-permute-start.1 = (f32[48,128]{1,0:T(8,128)}, f32[48,128]{1,0:T(8,128)}, u32[]{:S(2)}, u32[]{:S(2)}) collective-permute-start(f32[48,128]{1,0:T(8,128)} %get-tuple-element.55.order), channel_id=1, source_target_pairs={{0,1},{1,0},{2,3},{3,2},{4,5},{5,4},{6,7},{7,6}} | collective-permute-start | bytes 73736 | tf_op jit(solution)/shard_map/ppermute | solution.py:695
  84.8 7.3 %collective-permute-start.2 = (f32[48,128]{1,0:T(8,128)}, f32[48,128]{1,0:T(8,128)}, u32[]{:S(2)}, u32[]{:S(2)}) collective-permute-start(f32[48,128]{1,0:T(8,128)} %get-tuple-element.55.order), channel_id=1, source_target_pairs={{0,2},{1,3},{2,0},{3,1},{4,6},{5,7},{6,4},{7,5}} | collective-permute-start | bytes 73736 | tf_op jit(solution)/shard_map/ppermute | solution.py:695
  86.2 5.9 %collective-permute-start.3 = (f32[48,128]{1,0:T(8,128)}, f32[48,128]{1,0:T(8,128)}, u32[]{:S(2)}, u32[]{:S(2)}) collective-permute-start(f32[48,128]{1,0:T(8,128)} %get-tuple-element.55.order), channel_id=1, source_target_pairs={{0,3},{1,2},{2,1},{3,0},{4,7},{5,6},{6,5},{7,4}} | collective-permute-start | bytes 73736 | tf_op jit(solution)/shard_map/ppermute | solution.py:695

commit v9 on v8

--- a/solution.py
+++ b/solution.py
@@ -408,7 +408,7 @@
         lo = nqd + nkd + k * hd
         dqkv[:, lo:lo + hd] = grad_v
     put(dqkv, dqkv_out)
-    sum_dh1 = Scatter(2, part_a, dr_d, send.at[pl.ds(0, rows)])
+    sum_dh1 = Scatter(3, part_a, dr_d, send.at[pl.ds(0, rows)])
     sum_attn.pair_sent()
     sum_dh1.run(lambda cols: mm_bt(dqkv[...], wqkv[cols, :]))
     sum_dh1.drain()
@@ -465,7 +465,7 @@
         return pltpu.VMEM(shape, F32)
 
     out_shape = [arr((seq, d), BF16)] * 4 + [arr((seq, f), BF16)] * 2 + [arr((seq, nqd), BF16), arr((seq, n_all), BF16)] + [arr((half, d), BF16)] * 2 + [arr((rows, d), BF16), arr((rows + half, d), F32), arr((rows, d), F32), arr((half, d), F32)] + [arr((1, d), F32)] * 2
-    n_sems = 3 * (4 + 1 + 3 + 3) + 2 * (6 + 8 + 4 + 2) + (7 + 12 + 5) + 2
+    n_sems = 3 * (4 + 1 + 3 + 3) + 2 * (6 + 8 + 4 + 3) + (7 + 12 + 5) + 2
     scratch = [
         pltpu.VMEM((1, seq), jnp.int32), vf(1, hd), vf(1, d), vf(1, d), vf(1, d), vf(1, d),
         vm(d, n_all), vm(nqd, d), vm(d, f), vm(f, d),

time: 93.8 us -> 93.8 us (level)
  no operation moved by 1% of the time
where the time goes in v9:
time: 93.8 us; the launch traced here: 93.6 us
  Pallas kernels  88.9 us (95%)
  starting transfers between devices  2.56 us (3%)
  other arithmetic  1.44 us (2%)
    pallas_call x1, Pallas kernels, chain(): pl.pallas_call(functools.partial(chain_kernel, dims), out_shape=out_shape...  57.9 us
    pallas_call x1, Pallas kernels, grads_first(): pl.pallas_call(functools.partial(grads_first_kernel, dims), out_shape=[ar...  14.9 us
    pallas_call x1, Pallas kernels, grads_second(): pl.pallas_call(functools.partial(grads_second_kernel, dims), out_shape=[a...  10.5 us
    pallas_call x1, Pallas kernels, grads_third(): pl.pallas_call(grads_third_kernel, out_shape=arr((nqd, d)), in_specs=[ANY...  5.5 us
    ppermute x4, starting transfers between devices, swap(): return lax.ppermute(v, 'tp', [(i, i ^ bit) for i in range(n_tp)])  2.56 us
  transfers between devices with their start and end apart: 4, of which 0 were waited for; matrix products, arithmetic and copies ran while one was open for 0% of the time, Pallas kernels for 22%

profile of v9, /device:TPU:0, one launch (start us, length us, event | category | flops | bytes accessed | tf_op | source)
XLA Modules:
  0.0 93.6 jit_solution(6748722349707829864)
XLA Ops:
  0.6 57.9 %chain.1 = (bf16[128,3072]{1,0:T(8,128)(2,1)}, bf16[128,3072]{1,0:T(8,128)(2,1)}, bf16[128,3072]{1,0:T(8,128)(2,1)}, bf16[128,3072]{1,0:T(8,128)(2,1)}, bf16[128...) custom-call(bf16[32,3072]{1,0:T(8,128)(2,1)} %bitcast.15, ...), custom_call_target="tpu_custom_call" | custom-call | tf_op jit(solution)/shard_map/chain/pallas_call | solution.py:483
  58.6 0.7 collective-permute-start
  59.3 14.9 %grads_first.1 = (f32[2048,3072]{1,0:T(8,128)}, f32[3072,768]{1,0:T(8,128)}, f32[3072,256]{1,0:T(8,128)}, f32[3072,256]{1,0:T(8,128)}) custom-call(bf16[128,2048]{1,0:T(8,128)(2,1)} %get-tuple-element.38.act_hbm, bf16[128,3072]{1,0:T(8,128)(2,1)} %get-tuple-element.39.dy_hbm, bf16[128,3072]{1,0:T(8,128)(2,1)} %get-tuple-element.40.h1_hbm, ...), custom_call_target="tpu_custom_call" | custom-call | flops 2617245696 | bytes 40894464 | tf_op jit(solution)/shard_map/grads_first/pallas_call | solution.py:631
  74.2 0.0 collective-permute-done.recv_hbm
  74.2 10.5 %grads_second.1 = (bf16[32,3072]{1,0:T(8,128)(2,1)}, bf16[32,3072]{1,0:T(8,128)(2,1)}, f32[48,128]{1,0:T(8,128)}, f32[1,3072]{1,0:T(1,128)}, f32[1,3072]{1,0:T(1,128)}, /*index=5*/f32[3072,2048]{1,0:T(8,128)}) custom-call(f32[2048,3072]{1,0:T(8,128)} %get-tuple-element.37.order, bf16[128,3072]{1,0:T(8,128)(2,1)} %get-tuple-element.43.h2_hbm, ...), custom_call_target="tpu_custom_call" | custom-call | flops 1610612736 | bytes 25165824 | tf_op jit(solution)/shard_map/grads_second/pallas_call | solution.py:653
  84.7 0.1 collective-permute-start.1
  84.8 1.4 %collective-permute-start.2 = (f32[48,128]{1,0:T(8,128)}, f32[48,128]{1,0:T(8,128)}, u32[]{:S(2)}, u32[]{:S(2)}) collective-permute-start(f32[48,128]{1,0:T(8,128)} %get-tuple-element.55.order), channel_id=1, source_target_pairs={{0,2},{1,3},{2,0},{3,1},{4,6},{5,7},{6,4},{7,5}} | collective-permute-start | bytes 73736 | tf_op jit(solution)/shard_map/ppermute | solution.py:695
  86.2 0.4 collective-permute-start.3
  86.6 5.5 %grads_third.1 = f32[768,3072]{1,0:T(8,128)} custom-call(f32[48,128]{1,0:T(8,128)} %get-tuple-element.55.order, bf16[128,768]{1,0:T(8,128)(2,1)} %get-tuple-element.61.ctx_hbm, bf16[128,3072]{1,0:T(8,128)(2,1)} %get-tuple-element.62.dx1_hbm), custom_call_target="tpu_custom_call" | custom-call | flops 603979776 | bytes 9437184 | tf_op jit(solution)/shard_map/grads_third/pallas_call | solution.py:669
  92.1 0.0 collective-permute-done.1
  92.1 0.0 collective-permute-done.2
  92.1 0.0 collective-permute-done.3
  92.1 1.4 %fusion.1 = (f32[3072]{0:T(1024)}, f32[3072]{0:T(1024)}) fusion(f32[48,128]{1,0:T(8,128)} %collective-permute-done.3, f32[48,128]{1,0:T(8,128)} %collective-permute-done.2, f32[48,128]{1,0:T(8,128)} %collective-permute-done.1, f32[48,128]{1,0:T(8,128)} %get-tuple-element.55.order), kind=kLoop, calls=%fused_computation.2 | loop fusion | flops 18432 | bytes 122880 | tf_op jit(solution)/shard_map/reshape | solution.py:703
Async XLA Ops:
  58.6 15.6 %collective-permute-start = (f32[48,3072]{1,0:T(8,128)}, f32[48,3072]{1,0:T(8,128)}, u32[]{:S(2)}, u32[]{:S(2)}) collective-permute-start(f32[48,3072]{1,0:T(8,128)} %get-tuple-element.46), channel_id=1, source_target_pairs={{0,3},{1,2},{2,1},{3,0},{4,7},{5,6},{6,5},{7,4}} | collective-permute-start | bytes 1769480 | tf_op jit(solution)/shard_map/ppermute | solution.py:695
  84.7 7.4 %collective-permute-start.1 = (f32[48,128]{1,0:T(8,128)}, f32[48,128]{1,0:T(8,128)}, u32[]{:S(2)}, u32[]{:S(2)}) collective-permute-start(f32[48,128]{1,0:T(8,128)} %get-tuple-element.55.order), channel_id=1, source_target_pairs={{0,1},{1,0},{2,3},{3,2},{4,5},{5,4},{6,7},{7,6}} | collective-permute-start | bytes 73736 | tf_op jit(solution)/shard_map/ppermute | solution.py:695
  84.8 7.3 %collective-permute-start.2 = (f32[48,128]{1,0:T(8,128)}, f32[48,128]{1,0:T(8,128)}, u32[]{:S(2)}, u32[]{:S(2)}) collective-permute-start(f32[48,128]{1,0:T(8,128)} %get-tuple-element.55.order), channel_id=1, source_target_pairs={{0,2},{1,3},{2,0},{3,1},{4,6},{5,7},{6,4},{7,5}} | collective-permute-start | bytes 73736 | tf_op jit(solution)/shard_map/ppermute | solution.py:695
  86.2 5.9 %collective-permute-start.3 = (f32[48,128]{1,0:T(8,128)}, f32[48,128]{1,0:T(8,128)}, u32[]{:S(2)}, u32[]{:S(2)}) collective-permute-start(f32[48,128]{1,0:T(8,128)} %get-tuple-element.55.order), channel_id=1, source_target_pairs={{0,3},{1,2},{2,1},{3,0},{4,7},{5,6},{6,5},{7,4}} | collective-permute-start | bytes 73736 | tf_op jit(solution)/shard_map/ppermute | solution.py:695
